TPU v7x, 256 devices: a whole 4x4x8 slice. The times are simulated.
256 devices in a mesh: kf: 64 (over z, y, core), kc: 4 (over x).
Axes of the slice: x: 4, y: 4, z: 8, core: 2. Of those that a mesh axis runs over, the one named last changes fastest.
Arguments:
- kernel_coarse: bfloat16 [2048, 2048], P('kf'), may hold values from -6 to 6
- coefficients: bfloat16 [1024, 256], P(('kf', 'kc')), may hold values from -1.5 to 1.5
- nearest: int32 [1024], replicated, may hold values from 0 to 127
Outputs:
- kernel_fine: bfloat16 [16384, 16384], P('kf', 'kc')
All inputs are finite; a program needn't handle non-finite values.
Results may differ from a plain program's by a relative error of at most 0.0049.
Values may be sent and summed in bfloat16 or wider, within the bound.
No kernel may reach another device: no remote copies, remote signals or barrier semaphores. Data moves between devices by JAX's collectives and lax.ppermute only.
A program may use at most 64 MiB of HBM per device.

v0:
```python
import jax
import jax.numpy as jnp
from jax import lax
from jax.sharding import Mesh
from jax.sharding import PartitionSpec as P

P_SIZE = 16
KF = ("kf_0", "kf_1", "kf_2")
KF_KC = ("kf_0", "kf_1", "kf_2", "kc")


def joined_along(pieces, dim):
    shape = list(pieces.shape[1:])
    shape[dim] *= pieces.shape[0]
    return jnp.moveaxis(pieces, 0, dim).reshape(shape)


def gather_in_order(value, axes, sequence):
    pieces = value
    for k in sequence:
        pieces = lax.all_gather(pieces, axes[k])
    done = sequence[::-1]
    back = [done.index(k) for k in range(len(axes))]
    pieces = pieces.transpose(*back, *range(len(axes), pieces.ndim))
    return pieces.reshape(-1, *value.shape)


def whole_of(value, axes, sequence, dim):
    return joined_along(gather_in_order(value, axes, sequence), dim)


def copy_for_each(value, axis):
    copies = jnp.broadcast_to(value, (lax.axis_size(axis), *value.shape))
    return lax.all_to_all(copies, axis, split_axis=0, concat_axis=0, tiled=True)


def gathered_copies(value, axis, dim):
    pieces = copy_for_each(value, axis)
    return joined_along(pieces, dim)


def rotate(kernel_rows, coef_block):
    point_count = coef_block.shape[0]
    pair_count = coef_block.shape[1]
    shaped = kernel_rows.reshape(kernel_rows.shape[0], point_count, pair_count)
    turned = jnp.einsum("ckn,kan->cka", shaped, coef_block, preferred_element_type=jnp.float32)
    return turned.astype(jnp.bfloat16).reshape(kernel_rows.shape[0], point_count * pair_count)


def shards(kernel_coarse, coefficients, nearest):
    pair_count = P_SIZE
    total_rows = kernel_coarse.shape[1]
    fine_total = nearest.shape[0]
    slab_size = fine_total // lax.axis_size(KF)
    kc_count = lax.axis_size("kc")
    part_index = lax.axis_index("kc")
    offsets = jnp.arange(pair_count, dtype=jnp.int32)
    coef_whole = whole_of(coefficients, KF_KC, (0, 1, 3, 2), 0).reshape(
        fine_total, pair_count, pair_count
    )
    share_size = slab_size // kc_count
    grouped = nearest.reshape(lax.axis_size(KF), kc_count, share_size)
    chosen = lax.dynamic_index_in_dim(grouped, part_index, 1, keepdims=False)
    columns = (chosen.reshape(-1)[:, None] * pair_count + offsets[None, :]).reshape(-1)
    outgoing = jnp.take(kernel_coarse, columns, axis=1)
    received = lax.all_to_all(outgoing, KF, split_axis=1, concat_axis=0, tiled=True)
    own_coef = coefficients.reshape(share_size, pair_count, pair_count)
    turned = rotate(received, own_coef)
    rotated = gathered_copies(turned, "kc", 1)
    col_total = fine_total // kc_count
    col_coarse = lax.dynamic_slice_in_dim(nearest, part_index * col_total, col_total)
    coef_cols = lax.dynamic_slice_in_dim(coef_whole, part_index * col_total, col_total, 0)
    stacked = rotated.reshape(total_rows // pair_count, pair_count, rotated.shape[1])
    picked = jnp.take(stacked, col_coarse, axis=0)
    result = jnp.einsum("jnr,jbn->rjb", picked, coef_cols, preferred_element_type=jnp.float32)
    return result.reshape(result.shape[0], col_total * pair_count).astype(jnp.bfloat16)


def solution(mesh):
    split = Mesh(mesh.devices.reshape(8, 4, 2, mesh.shape["kc"]), ("kf_0", "kf_1", "kf_2", "kc"))
    in_specs = (P(KF, None), P(KF_KC, None), P())
    out_specs = P(KF, "kc")
    return jax.shard_map(
        shards, mesh=split, in_specs=in_specs, out_specs=out_specs, check_vma=False
    )
```

profile of v0, /device:TPU:6, one launch (start us, length us, event | category | flops | bytes accessed | tf_op | source)
XLA Modules:
  0.0 115.7 jit_solution(15562219418831374504)
XLA Ops:
  0.0 0.9 reshape.83
  0.9 0.5 broadcast.58
  1.4 0.8 fusion.10
  2.9 1.2 %copy.37 = bf16[32,2048]{0,1:T(8,128)(2,1)S(1)} copy(bf16[32,2048]{1,0:T(8,128)(2,1)} %param.3) | data formatting | bytes 262144 | tf_op args[0]
  4.1 12.1 %gather_fusion = bf16[4096,32]{1,0:T(8,128)(2,1)S(1)} fusion(bf16[32,2048]{0,1:T(8,128)(2,1)S(1)} %copy.37, s32[4096]{0:T(1024)S(1)} %broadcast_clamp_fusion), kind=kCustom, calls=%fused_computation | custom fusion | bytes 540672 | tf_op jit(solution)/shard_map/jit(_take)/gather | solution.py:65
  16.3 0.4 copy.38
  16.7 1.0 reshape.120
  17.7 12.1 %all-to-all-start = ((bf16[64,2,1024]{2,1,0:T(2,128)(2,1)}), bf16[64,2,1024]{2,1,0:T(2,128)(2,1)S(1)}, u32[]{:S(2)}, u32[]{:S(2)}) async-start(bf16[64,2,1024]{2,1,0:T(2,128)(2,1)} %reshape.120), calls=%async_computation | async-start | bytes 524288 | tf_op jit(solution)/shard_map/all_to_all | solution.py:66
  30.0 12.8 %all-to-all-done = bf16[64,2,1024]{2,1,0:T(2,128)(2,1)S(1)} async-done(((bf16[64,2,1024]{2,1,0:T(2,128)(2,1)}), bf16[64,2,1024]{2,1,0:T(2,128)(2,1)S(1)}, u32[]{:S(2)}, u32[]{:S(2)}) %all-to-all-start) | async-done | bytes 262176 | tf_op jit(solution)/shard_map/all_to_all | solution.py:66
  43.1 1.6 %copy.39 = bf16[64,32,64]{1,0,2:T(8,128)(2,1)S(1)} copy(bf16[64,32,64]{2,1,0:T(8,128)(2,1)S(1)} %bitcast_bitcast_fusion) | data formatting | bytes 524288 | tf_op jit(solution)/shard_map/all_to_all | solution.py:66
  44.7 1.1 reshape.84
  46.1 1.1 broadcast_in_dim.29
  47.1 4.8 %all-to-all-start.1 = ((bf16[4,2048,64]{1,2,0:T(8,128)(2,1)}), bf16[4,2048,64]{1,2,0:T(8,128)(2,1)S(1)}, u32[]{:S(2)}, u32[]{:S(2)}) async-start(bf16[4,2048,64]{1,2,0:T(8,128)(2,1)} %broadcast_in_dim.29), calls=%async_computation.1 | async-start | bytes 2097152 | tf_op jit(solution)/shard_map/all_to_all | solution.py:34
  51.9 21.4 %all-gather.4 = bf16[8,4,256]{2,1,0:T(4,128)(2,1)S(1)} all-gather(bf16[1,4,256]{2,1,0:T(4,128)(2,1)S(1)} %bitcast.45), channel_id=2, replica_groups=mesh['kf_0'=8,'kf_1'=4,'kf_2'=2,'kc'=4] {'kf_0'}, dimensions={0}, use_global_device_ids=true | all-gather | bytes 18432 | tf_op jit(solution)/shard_map/all_gather | solution.py:21
  73.4 11.9 %all-gather.1 = bf16[32,4,256]{2,1,0:T(4,128)(2,1)S(1)} all-gather(bf16[8,4,256]{2,1,0:T(4,128)(2,1)S(1)} %all-gather.4), channel_id=3, replica_groups=mesh['kf_0'=8,'kf_1'=4,'kf_2'=2,'kc'=4] {'kf_1'}, dimensions={0}, use_global_device_ids=true | all-gather | bytes 81920 | tf_op jit(solution)/shard_map/all_gather | solution.py:21
  85.2 12.3 %all-gather.2 = bf16[16,8,4,256]{3,1,2,0:T(8,128)(2,1)S(1)} all-gather(bf16[4,8,4,256]{3,1,2,0:T(8,128)(2,1)S(1)} %copy.32), channel_id=4, replica_groups=mesh['kf_0'=8,'kf_1'=4,'kf_2'=2,'kc'=4] {'kc'}, dimensions={0}, use_global_device_ids=true | all-gather | bytes 327680 | tf_op jit(solution)/shard_map/all_gather | solution.py:21
  97.5 2.2 %all-gather.3 = bf16[8,4,8,4,256]{4,2,3,1,0:T(8,128)(2,1)S(1)} all-gather(bf16[4,4,8,4,256]{4,2,3,1,0:T(8,128)(2,1)S(1)} %bitcast.40), channel_id=5, replica_groups=mesh['kf_0'=8,'kf_1'=4,'kf_2'=2,'kc'=4] {'kf_2'}, dimensions={0}, use_global_device_ids=true | all-gather | bytes 786432 | tf_op jit(solution)/shard_map/all_gather | solution.py:21
  99.9 4.1 %reshape_reshape_reshape.3 = bf16[1024,16,16]{2,1,0:T(8,128)(2,1)} reshape(bf16[8,4,2,4,4,256]{5,4,3,2,1,0:T(4,128)(2,1)S(1)} %bitcast.37) | data formatting | bytes 1048576 | tf_op jit(solution)/shard_map/reshape;reshape;reshape | solution.py:58
  104.0 0.8 compare_and_fusion.1
  104.8 1.4 %copy.40 = bf16[2048,4,64]{2,1,0:T(4,128)(2,1)S(1)} copy(bf16[2048,4,64]{0,2,1:T(8,128)(2,1)S(1)} %bitcast.36) | data formatting | bytes 2097152 | tf_op jit(solution)/shard_map/transpose | solution.py:15
  106.2 1.4 %reshape_reshape.3 = bf16[128,16,256]{2,1,0:T(8,128)(2,1)S(1)} reshape(bf16[2048,4,64]{2,1,0:T(4,128)(2,1)S(1)} %copy.40) | data formatting | bytes 2097152 | tf_op jit(solution)/shard_map/reshape;reshape | solution.py:73
  107.6 0.8 gather_fusion.1
  108.3 3.3 %fusion.3 = bf16[256,16,256]{2,1,0:T(8,128)(2,1)} fusion(bf16[256,16,256]{2,1,0:T(8,128)(2,1)S(1)} %gather_fusion.1, pred[256]{0:T(512)(128)(4,1)S(1)} %get-tuple-element.5, bf16[1024,16,16]{2,1,0:T(8,128)(2,1)} %reshape_reshape_reshape.3, s32[]{:T(128)S(6)} %select_n.39), kind=kOutput, calls=%fused_computation.6 | convolution fusion | flops 35651584 | bytes 5243140 | tf_op jit(solution)/shard_map/jnr,jbn->rjb/dot_general | solution.py:75
  111.7 4.1 %copy.41 = bf16[256,4096]{1,0:T(8,128)(2,1)} copy(bf16[256,4096]{0,1:T(8,128)(2,1)} %bitcast.35) | data formatting | bytes 4194304 | tf_op jit(solution)/shard_map/convert_element_type | solution.py:76
  (22 shorter events, 1.7 us)
Async XLA Ops:
  16.3 13.6 %copy-start = (bf16[4,256]{1,0:T(4,128)(2,1)S(1)}, bf16[4,256]{1,0:T(4,128)(2,1)}, u32[]{:S(2)}) copy-start(bf16[4,256]{1,0:T(4,128)(2,1)} %param.4) | copy-start | bytes 6148
  17.7 25.0 %all-to-all-start = ((bf16[64,2,1024]{2,1,0:T(2,128)(2,1)}), bf16[64,2,1024]{2,1,0:T(2,128)(2,1)S(1)}, u32[]{:S(2)}, u32[]{:S(2)}) async-start(bf16[64,2,1024]{2,1,0:T(2,128)(2,1)} %reshape.120), calls=%async_computation | async-start | bytes 524288 | tf_op jit(solution)/shard_map/all_to_all | solution.py:66
  47.1 57.6 %all-to-all-start.1 = ((bf16[4,2048,64]{1,2,0:T(8,128)(2,1)}), bf16[4,2048,64]{1,2,0:T(8,128)(2,1)S(1)}, u32[]{:S(2)}, u32[]{:S(2)}) async-start(bf16[4,2048,64]{1,2,0:T(8,128)(2,1)} %broadcast_in_dim.29), calls=%async_computation.1 | async-start | bytes 2097152 | tf_op jit(solution)/shard_map/all_to_all | solution.py:34
where the time goes:
time: 118 us; the launch traced here: 116 us
  blocking collectives  47.7 us (40%)
  local copies, waits for them, and re-layouts  32.8 us (28%)
  starting transfers between devices  16.9 us (14%)
  waiting for transfers between devices  12.8 us (11%)
  matrix products  3.53 us (3%)
  other arithmetic  1.75 us (1%)
    all_gather x4, blocking collectives, gather_in_order(): pieces = lax.all_gather(pieces, axes[k])  47.7 us
    all_to_all x1, waiting for transfers between devices, shards(): lax.all_to_all(outgoing, KF, split_axis=1, concat_axis=0, tiled=True)  12.8 us
    gather x2, local copies, waits for them, and re-layouts, shards(): outgoing = jnp.take(kernel_coarse, columns, axis=1)  12.5 us
    all_to_all x1, starting transfers between devices, shards(): lax.all_to_all(outgoing, KF, split_axis=1, concat_axis=0, tiled=True)  12.1 us
    all_to_all x1, starting transfers between devices, copy_for_each(): return lax.all_to_all(copies, axis, split_axis=0, concat_axis=0, tiled=True)  4.77 us
    another operation x1, local copies, waits for them, and re-layouts, shards(): whole_of(coefficients, KF_KC, (0, 1, 3, 2), 0)  4.08 us
    convert_element_type x1, local copies, waits for them, and re-layouts, shards(): result.reshape(result.shape[0], col_total * pair_count).astype(jnp.bfloat16)  4.06 us
    dot_general x1, matrix products, shards(): jnp.einsum('jnr,jbn->rjb', picked, coef_cols, preferred_element_type=jnp....  3.33 us
  transfers between devices with their start and end apart: 2, of which 1 were waited for; matrix products, arithmetic and copies ran while one was open for 5% of the time, Pallas kernels for 0%

commit v1 on v0

v1 whole, which is shorter than its diff:
```python
import jax
import jax.numpy as jnp
from jax import lax
from jax.experimental import pallas as pl
from jax.experimental.pallas import tpu as pltpu
from jax.sharding import Mesh
from jax.sharding import PartitionSpec as P

KF = ("kf_0", "kf_1", "kf_2")
ZY = ("kf_0", "kf_1")
KF_KC = ("kf_0", "kf_1", "kf_2", "kc")
LANES = 128
PAIRS = 16
POINTS = 4
PEERS = 32


def iota(shape, dim):
    return lax.broadcasted_iota(jnp.int32, shape, dim)


def spread_rows(coef):
    group = iota((PAIRS, LANES), 1) // PAIRS
    row = iota((PAIRS, LANES), 0)
    keep = group == row % 8
    low = row < 8
    pieces = []
    for p in range(coef.shape[0]):
        first = jnp.broadcast_to(coef[p : p + 1, :LANES], (PAIRS, LANES))
        second = jnp.broadcast_to(coef[p : p + 1, LANES:], (PAIRS, LANES))
        pieces.append(jnp.where(keep, jnp.where(low, first, second), 0.0))
    return jnp.concatenate(pieces, axis=0).astype(jnp.bfloat16)


def repeated(width):
    same = iota((LANES, width), 0) % PAIRS == iota((LANES, width), 1) % PAIRS
    return jnp.where(same, 1.0, 0.0).astype(jnp.bfloat16)


def pack_kernel(near, own, other, coef_own, coef_other, out, blocks):
    kc = lax.axis_index("kc")
    core = lax.axis_index("kf_2")
    for b in range(16):
        cut = slice(b * LANES, (b + 1) * LANES)
        blocks[core, b] = own[:, cut].astype(jnp.float32)
        blocks[1 - core, b] = other[:, cut].astype(jnp.float32)
    a = coef_own[...].astype(jnp.float32)
    o = coef_other[...].astype(jnp.float32)
    first = jnp.where(core == 0, a, o)
    second = jnp.where(core == 0, o, a)
    coef = jnp.concatenate(
        [first[:, :LANES], first[:, LANES:], second[:, :LANES], second[:, LANES:]], axis=0
    ).astype(jnp.bfloat16)
    group = iota((PAIRS, LANES), 1) // PAIRS
    base = 16 * core + 4 * kc

    def body(d, carry):
        for h in range(2):
            tile = jnp.zeros((PAIRS, LANES), jnp.float32)
            for j in range(POINTS):
                c = near[32 * d + base + j]
                for lo in range(2):
                    at = lo * POINTS + j
                    piece = blocks[h, c // 8, lo * PAIRS : (lo + 1) * PAIRS, :]
                    turned = pltpu.roll(piece, ((at - c % 8) % 8) * PAIRS, 1)
                    tile = jnp.where(group == at, turned, tile)
            out[d, h * PAIRS : (h + 1) * PAIRS, :] = tile.astype(jnp.bfloat16)
        out[d, 2 * PAIRS :, :] = coef
        return carry

    lax.fori_loop(0, PEERS, body, 0)


def final_kernel(near, mine, left, right, far_a, far_b, coef_cols, rows_0, rows_l, rows_r, rows_f, out, turn):
    kc = lax.axis_index("kc")
    t = pl.program_id(0)

    @pl.when(t == 0)
    def _():
        keep = iota((POINTS * PAIRS, LANES), 1) // PAIRS % POINTS == iota((POINTS * PAIRS, LANES), 0) // PAIRS
        for i, ref in enumerate((rows_0, rows_l, rows_r, rows_f)):
            wide = jnp.dot(
                spread_rows(ref[...].astype(jnp.float32)), repeated(LANES), preferred_element_type=jnp.float32
            )
            turn[i] = jnp.where(keep, wide, 0.0).astype(jnp.bfloat16)

    z_low, y, core = t // 8, t // 2 % 4, t % 2
    spread = []
    for x in range(4):
        chunk = coef_cols[(z_low * 4 + x) * 4 + y, pl.ds(core * 8, 8), :].astype(jnp.float32)
        spread.append(spread_rows(jnp.concatenate([chunk[:POINTS], chunk[POINTS:]], axis=1)))
    wide = jnp.dot(jnp.concatenate(spread, axis=0), repeated(256), preferred_element_type=jnp.float32)
    diag = iota((256, 256), 0) // PAIRS == iota((256, 256), 1) // PAIRS
    cols = jnp.where(diag, wide, 0.0).astype(jnp.bfloat16)

    half = iota((PAIRS, LANES), 1) // 64
    picks = [[], [], [], []]
    for i in range(16):
        c = near[256 * kc + 16 * t + i]
        zy = c // 4
        at = pl.multiple_of((c // 2 % 2) * PAIRS, PAIRS)
        keep = half == c % 2
        far = jnp.where(
            zy < PEERS // 2,
            far_a[jnp.minimum(zy, PEERS // 2 - 1), pl.ds(at, PAIRS), :],
            far_b[jnp.maximum(zy - PEERS // 2, 0), pl.ds(at, PAIRS), :],
        )
        for n, block in enumerate((mine[zy, pl.ds(at, PAIRS), :], left[zy, pl.ds(at, PAIRS), :], right[zy, pl.ds(at, PAIRS), :], far)):
            picks[n].append(jnp.where(keep, block, jnp.zeros_like(block)))
    for n, step in enumerate((0, 3, 1, 2)):
        block = jnp.concatenate(picks[n], axis=0)
        turned = lax.dot_general(turn[n], block, (((1,), (1,)), ((), ())), preferred_element_type=jnp.float32)
        result = lax.dot_general(
            turned.astype(jnp.bfloat16), cols, (((1,), (1,)), ((), ())), preferred_element_type=jnp.float32
        )
        at = pl.multiple_of((kc + step) % 4 * 64, 64)
        out[pl.ds(at, 64), :] = result.astype(jnp.bfloat16)


def shift(value, by):
    return lax.ppermute(value, "kc", [(i, (i + by) % 4) for i in range(4)])


def spread_coefficients(swap_core):
    pairs = []
    for z in range(8):
        for y in range(4):
            for c in range(2):
                for x in range(4):
                    new_c = 1 - c if swap_core else c
                    source = ((z * 4 + y) * 2 + c) * 4 + x
                    target = ((((z % 2) * 4 + x) * 4 + y) * 2 + new_c) * 4 + z // 2
                    pairs.append((source, target))
    return pairs


def shards(kernel_coarse, coefficients, nearest):
    vmem = pl.BlockSpec(memory_space=pltpu.VMEM)
    smem = pl.BlockSpec(memory_space=pltpu.SMEM)
    other = lax.ppermute(kernel_coarse, "kf_2", [(0, 1), (1, 0)])
    coef_own = lax.ppermute(coefficients, KF_KC, spread_coefficients(False))
    coef_other = lax.ppermute(coefficients, KF_KC, spread_coefficients(True))
    outgoing = pl.pallas_call(
        pack_kernel,
        out_shape=jax.ShapeDtypeStruct((PEERS, 48, LANES), jnp.bfloat16),
        in_specs=[smem, vmem, vmem, vmem, vmem],
        out_specs=vmem,
        scratch_shapes=[pltpu.VMEM((2, 16, 32, LANES), jnp.float32)],
        compiler_params=pltpu.CompilerParams(vmem_limit_bytes=8 << 20),
        cost_estimate=pl.CostEstimate(flops=4000000, bytes_accessed=650000, transcendentals=0),
    )(nearest, kernel_coarse, other, coef_own, coef_other)
    received = lax.all_to_all(outgoing, ZY, split_axis=0, concat_axis=0, tiled=True)
    mine = received[:, :32]
    coef_cols = received[:, 32:]
    left = shift(mine, 1)
    right = shift(mine, -1)
    far_a = shift(left[: PEERS // 2], 1)
    far_b = shift(right[PEERS // 2 :], -1)
    rows_l, rows_r, rows_f = shift(coefficients, 1), shift(coefficients, -1), shift(coefficients, 2)
    return pl.pallas_call(
        final_kernel,
        grid=(16,),
        out_shape=jax.ShapeDtypeStruct((256, 4096), jnp.bfloat16),
        in_specs=[smem] + [vmem] * 10,
        out_specs=pl.BlockSpec((256, 256), lambda t: (0, t)),
        scratch_shapes=[pltpu.VMEM((4, 64, LANES), jnp.bfloat16)],
        compiler_params=pltpu.CompilerParams(vmem_limit_bytes=8 << 20),
        cost_estimate=pl.CostEstimate(flops=20000000, bytes_accessed=3400000, transcendentals=0),
    )(nearest, mine, left, right, far_a, far_b, coef_cols, coefficients, rows_l, rows_r, rows_f)


def solution(mesh):
    split = Mesh(mesh.devices.reshape(8, 4, 2, mesh.shape["kc"]), KF_KC)
    return jax.shard_map(
        shards,
        mesh=split,
        in_specs=(P(KF, None), P(KF_KC, None), P()),
        out_specs=P(KF, "kc"),
        check_vma=False,
    )
```

time: 118 us -> 78.6 us (0.67); the launches traced: 116 us -> 78.4 us
  local copies, waits for them, and re-layouts: 32.8 us -> 1.65 us
  blocking collectives: 47.7 us -> 22.6 us
  Pallas kernels: 0 us -> 20 us
  starting transfers between devices: 16.9 us -> 21.7 us
  matrix products: 3.53 us -> 0 us
  other arithmetic: 1.75 us -> 0 us
    all_gather x4 -> x0, blocking collectives: 47.7 us -> none  [gather_in_order(): pieces = lax.all_gather(pieces, axes[k])]
    all_to_all x0 -> x1, blocking collectives: none -> 22.6 us  [shards(): lax.all_to_all(outgoing, ZY, split_axis=0, concat_axis=0, tiled=True)]
    ppermute x0 -> x10, starting transfers between devices: none -> 21.7 us  [the longest x7 11.1 us: shift(): return lax.ppermute(value, 'kc', [(i, (i + by) % 4) for i in range(4)])]
    pallas_call x0 -> x2, Pallas kernels: none -> 20 us  [the longest x1 14.4 us: shards(): pl.pallas_call(final_kernel, grid=(16,), out_shape=jax.ShapeDtypeStruct((...]
    all_to_all x2 -> x0, starting transfers between devices: 16.9 us -> none  [the longest x1 12.1 us: shards(): lax.all_to_all(outgoing, KF, split_axis=1, concat_axis=0, tiled=True)]
    gather x3 -> x0, local copies, waits for them, and re-layouts: 13.3 us -> none  [the longest x2 12.5 us: shards(): outgoing = jnp.take(kernel_coarse, columns, axis=1)]
    all_to_all x2 -> x0, waiting for transfers between devices: 12.8 us -> none  [the longest x1 12.8 us: shards(): lax.all_to_all(outgoing, KF, split_axis=1, concat_axis=0, tiled=True)]
    ppermute x0 -> x10, waiting for transfers between devices: none -> 12.4 us  [the longest x7 8.46 us: shift(): return lax.ppermute(value, 'kc', [(i, (i + by) % 4) for i in range(4)])]
  transfers between devices with their start and end apart: 2 -> 10, of which waited for: 1 -> 5; matrix products, arithmetic and copies ran while one was open for 5% -> 0% of each run, Pallas kernels for 0% -> 0%
where the time goes in v1:
time: 78.6 us; the launch traced here: 78.4 us
  blocking collectives  22.6 us (29%)
  starting transfers between devices  21.7 us (28%)
  Pallas kernels  20 us (25%)
  waiting for transfers between devices  12.4 us (16%)
  local copies, waits for them, and re-layouts  1.65 us (2%)
    all_to_all x1, blocking collectives, shards(): lax.all_to_all(outgoing, ZY, split_axis=0, concat_axis=0, tiled=True)  22.6 us
    pallas_call x1, Pallas kernels, shards(): pl.pallas_call(final_kernel, grid=(16,), out_shape=jax.ShapeDtypeStruct((...  14.4 us
    ppermute x7, starting transfers between devices, shift(): return lax.ppermute(value, 'kc', [(i, (i + by) % 4) for i in range(4)])  11.1 us
    ppermute x7, waiting for transfers between devices, shift(): return lax.ppermute(value, 'kc', [(i, (i + by) % 4) for i in range(4)])  8.46 us
    ppermute x1, starting transfers between devices, shards(): coef_own = lax.ppermute(coefficients, KF_KC, spread_coefficients(False))  5.95 us
    pallas_call x1, Pallas kernels, shards(): pl.pallas_call(pack_kernel, out_shape=jax.ShapeDtypeStruct((PEERS, 48, LA...  5.65 us
    ppermute x1, starting transfers between devices, shards(): coef_other = lax.ppermute(coefficients, KF_KC, spread_coefficients(True))  4.65 us
    ppermute x1, waiting for transfers between devices, shards(): coef_own = lax.ppermute(coefficients, KF_KC, spread_coefficients(False))  3.93 us
  transfers between devices with their start and end apart: 10, of which 5 were waited for; matrix products, arithmetic and copies ran while one was open for 0% of the time, Pallas kernels for 0%

profile of v1, /device:TPU:6, one launch (start us, length us, event | category | flops | bytes accessed | tf_op | source)
XLA Modules:
  0.0 78.4 jit_solution(145056742485483234)
XLA Ops:
  0.0 0.0 collective-permute-start
  0.0 4.7 %collective-permute-start.2 = (bf16[4,256]{1,0:T(4,128)(2,1)}, bf16[4,256]{1,0:T(4,128)(2,1)S(1)}, u32[]{:S(2)}, u32[]{:S(2)}) collective-permute-start(bf16[4,256]{1,0:T(4,128)(2,1)} %rows_0.1), channel_id=1, source_target_pairs={{0,4},{1,36},{2,68},{3,100},{4,0},{5,32},{6,64},{7,96},{8,12},{9,4... | collective-permute-start | bytes 6152 | tf_op jit(solution)/shard_map/ppermute | solution.py:142
  4.7 6.0 %collective-permute-start.1 = (bf16[4,256]{1,0:T(4,128)(2,1)}, bf16[4,256]{1,0:T(4,128)(2,1)S(1)}, u32[]{:S(2)}, u32[]{:S(2)}) collective-permute-start(bf16[4,256]{1,0:T(4,128)(2,1)} %rows_0.1), channel_id=1, source_target_pairs={{0,0},{1,32},{2,64},{3,96},{4,4},{5,36},{6,68},{7,100},{8,8},{9,40... | collective-permute-start | bytes 6152 | tf_op jit(solution)/shard_map/ppermute | solution.py:141
  10.6 0.0 collective-permute-done.2.coef_other
  10.6 3.9 %collective-permute-done.1.coef_own = bf16[4,256]{1,0:T(4,128)(2,1)S(1)} collective-permute-done((bf16[4,256]{1,0:T(4,128)(2,1)}, bf16[4,256]{1,0:T(4,128)(2,1)S(1)}, u32[]{:S(2)}, u32[]{:S(2)}) %collective-permute-start.1) | collective-permute-done | bytes 2080 | tf_op jit(solution)/shard_map/ppermute | solution.py:141
  14.6 0.0 collective-permute-done.other
  14.6 0.9 %copy-done = bf16[32,2048]{1,0:T(8,128)(2,1)S(1)} copy-done((bf16[32,2048]{1,0:T(8,128)(2,1)S(1)}, bf16[32,2048]{1,0:T(8,128)(2,1)}, u32[]{:S(2)}) %copy-start) | copy-done | bytes 131096
  15.5 0.7 copy-done.1
  16.2 5.7 %shard_map.37 = bf16[32,48,128]{2,1,0:T(8,128)(2,1)S(1)} custom-call(s32[1024]{0:T(1024)S(1)} %copy-done.1, bf16[32,2048]{1,0:T(8,128)(2,1)S(1)} %copy-done, bf16[32,2048]{1,0:T(8,128)(2,1)S(1)} %collective-permute-done.other, bf16[4,256]{1,0:T(4,128)(2,1)S(1)} %collective-permute-done.1.coef_own, bf16[4,256]{1,0:T(4,128)(2,1)S(1)} %collective-permute-done.2.coef_other), custom_call_target="tpu_custom_call" | custom-call | flops 4000000 | bytes 650000 | tf_op jit(solution)/shard_map/pallas_call | solution.py:143
  21.8 22.6 %all_to_all.5 = bf16[32,48,128]{2,1,0:T(8,128)(2,1)S(1)} all-to-all(bf16[32,48,128]{2,1,0:T(8,128)(2,1)S(1)} %shard_map.37), channel_id=1, replica_groups=mesh['kf_0'=8,'kf_1'=4,'kf_2'=2,'kc'=4] {'kf_0','kf_1'}, dimensions={0} | all-to-all | bytes 786432 | tf_op jit(solution)/shard_map/all_to_all | solution.py:152
  44.4 0.1 collective-permute-start.4
  44.5 3.2 %collective-permute-start.3 = (bf16[32,32,128]{2,1,0:T(8,128)(2,1)S(1)}, bf16[32,32,128]{2,1,0:T(8,128)(2,1)S(1)}, u32[]{:S(2)}, u32[]{:S(2)}) collective-permute-start(bf16[32,32,128]{2,1,0:T(8,128)(2,1)S(1)} %slice.16.mine), channel_id=1, source_target_pairs={{0,1},{1,2},{2,3},{3,0},{4,5},{5,6},{6,7},{7,4},{8,9},{9,10},{10,1... | collective-permute-start | bytes 786440 | tf_op jit(solution)/shard_map/ppermute | solution.py:121
  47.7 4.4 %collective-permute-done.4.right = bf16[32,32,128]{2,1,0:T(8,128)(2,1)S(1)} collective-permute-done((bf16[32,32,128]{2,1,0:T(8,128)(2,1)S(1)}, bf16[32,32,128]{2,1,0:T(8,128)(2,1)S(1)}, u32[]{:S(2)}, u32[]{:S(2)}) %collective-permute-start.4) | collective-permute-done | bytes 262176 | tf_op jit(solution)/shard_map/ppermute | solution.py:121
  52.2 1.2 %collective-permute-start.6 = (bf16[16,32,128]{2,1,0:T(8,128)(2,1)S(1)}, bf16[16,32,128]{2,1,0:T(8,128)(2,1)S(1)}, u32[]{:S(2)}, u32[]{:S(2)}) collective-permute-start(bf16[16,32,128]{2,1,0:T(8,128)(2,1)S(1)} %slice.18), channel_id=1, source_target_pairs={{0,3},{1,0},{2,1},{3,2},{4,7},{5,4},{6,5},{7,6},{8,11},{9,8},{10,9... | collective-permute-start | bytes 393224 | tf_op jit(solution)/shard_map/ppermute | solution.py:121
  53.3 0.1 collective-permute-done.3.left
  53.4 2.2 %collective-permute-start.5 = (bf16[16,32,128]{2,1,0:T(8,128)(2,1)S(1)}, bf16[16,32,128]{2,1,0:T(8,128)(2,1)S(1)}, u32[]{:S(2)}, u32[]{:S(2)}) collective-permute-start(bf16[16,32,128]{2,1,0:T(8,128)(2,1)S(1)} %slice.17), channel_id=1, source_target_pairs={{0,1},{1,2},{2,3},{3,0},{4,5},{5,6},{6,7},{7,4},{8,9},{9,10},{10,1... | collective-permute-start | bytes 393224 | tf_op jit(solution)/shard_map/ppermute | solution.py:121
  55.7 0.3 collective-permute-start.8
  56.0 2.9 %collective-permute-start.7 = (bf16[4,256]{1,0:T(4,128)(2,1)S(1)}, bf16[4,256]{1,0:T(4,128)(2,1)S(1)}, u32[]{:S(2)}, u32[]{:S(2)}) collective-permute-start(bf16[4,256]{1,0:T(4,128)(2,1)S(1)} %copy-done.3), channel_id=1, source_target_pairs={{0,1},{1,2},{2,3},{3,0},{4,5},{5,6},{6,7},{7,4},{8,9},{9,10},{10,1... | collective-permute-start | bytes 6152 | tf_op jit(solution)/shard_map/ppermute | solution.py:121
  58.9 1.1 %collective-permute-start.9 = (bf16[4,256]{1,0:T(4,128)(2,1)S(1)}, bf16[4,256]{1,0:T(4,128)(2,1)S(1)}, u32[]{:S(2)}, u32[]{:S(2)}) collective-permute-start(bf16[4,256]{1,0:T(4,128)(2,1)S(1)} %copy-done.3), channel_id=1, source_target_pairs={{0,2},{1,3},{2,0},{3,1},{4,6},{5,7},{6,4},{7,5},{8,10},{9,11},{10,... | collective-permute-start | bytes 6152 | tf_op jit(solution)/shard_map/ppermute | solution.py:121
  60.0 0.4 collective-permute-done.8.rows_r
  60.5 0.0 collective-permute-done.7.rows_l
  60.5 3.5 %collective-permute-done.9.rows_f = bf16[4,256]{1,0:T(4,128)(2,1)S(1)} collective-permute-done((bf16[4,256]{1,0:T(4,128)(2,1)S(1)}, bf16[4,256]{1,0:T(4,128)(2,1)S(1)}, u32[]{:S(2)}, u32[]{:S(2)}) %collective-permute-start.9) | collective-permute-done | bytes 2080 | tf_op jit(solution)/shard_map/ppermute | solution.py:121
  64.0 0.0 collective-permute-done.5.far_a
  64.0 14.4 %shard_map.38 = bf16[256,4096]{1,0:T(8,128)(2,1)} custom-call(s32[1024]{0:T(1024)S(1)} %copy-done.2, bf16[32,32,128]{2,1,0:T(8,128)(2,1)S(1)} %slice.16.mine, bf16[32,32,128]{2,1,0:T(8,128)(2,1)S(1)} %collective-permute-done.3.left, bf16[32,32,128]{2,1,0:T(8,128)(2,1)S(1)} %collective-permute-done.4.right, ...), custom_call_target="tpu_custom_call" | custom-call | flops 20000000 | bytes 3400000 | tf_op jit(solution)/shard_map/pallas_call | solution.py:160
  (11 shorter events, 0.1 us)
Async XLA Ops:
  0.0 14.6 %collective-permute-start = (bf16[32,2048]{1,0:T(8,128)(2,1)}, bf16[32,2048]{1,0:T(8,128)(2,1)S(1)}, u32[]{:S(2)}, u32[]{:S(2)}) collective-permute-start(bf16[32,2048]{1,0:T(8,128)(2,1)} %own.1), channel_id=1, source_target_pairs={{0,4},{4,0},{1,5},{5,1},{2,6},{6,2},{3,7},{7,3},{8,12},{12,8},{9,1... | collective-permute-start | bytes 393224 | tf_op jit(solution)/shard_map/ppermute | solution.py:140
  0.0 10.6 %collective-permute-start.2 = (bf16[4,256]{1,0:T(4,128)(2,1)}, bf16[4,256]{1,0:T(4,128)(2,1)S(1)}, u32[]{:S(2)}, u32[]{:S(2)}) collective-permute-start(bf16[4,256]{1,0:T(4,128)(2,1)} %rows_0.1), channel_id=1, source_target_pairs={{0,4},{1,36},{2,68},{3,100},{4,0},{5,32},{6,64},{7,96},{8,12},{9,4... | collective-permute-start | bytes 6152 | tf_op jit(solution)/shard_map/ppermute | solution.py:142
  4.7 9.9 %collective-permute-start.1 = (bf16[4,256]{1,0:T(4,128)(2,1)}, bf16[4,256]{1,0:T(4,128)(2,1)S(1)}, u32[]{:S(2)}, u32[]{:S(2)}) collective-permute-start(bf16[4,256]{1,0:T(4,128)(2,1)} %rows_0.1), channel_id=1, source_target_pairs={{0,0},{1,32},{2,64},{3,96},{4,4},{5,36},{6,68},{7,100},{8,8},{9,40... | collective-permute-start | bytes 6152 | tf_op jit(solution)/shard_map/ppermute | solution.py:141
  14.6 0.9 %copy-start = (bf16[32,2048]{1,0:T(8,128)(2,1)S(1)}, bf16[32,2048]{1,0:T(8,128)(2,1)}, u32[]{:S(2)}) copy-start(bf16[32,2048]{1,0:T(8,128)(2,1)} %own.1) | copy-start | bytes 393220
  15.5 0.7 copy-start.1
  16.1 39.5 %copy-start.3 = (bf16[4,256]{1,0:T(4,128)(2,1)S(1)}, bf16[4,256]{1,0:T(4,128)(2,1)}, u32[]{:S(2)}) copy-start(bf16[4,256]{1,0:T(4,128)(2,1)} %rows_0.1) | copy-start | bytes 6148
  16.2 47.8 %copy-start.2 = (s32[1024]{0:T(1024)S(1)}, s32[1024]{0:T(1024)}, u32[]{:S(2)}) copy-start(s32[1024]{0:T(1024)} %near.3) | copy-start | bytes 12292
  44.4 7.7 %collective-permute-start.4 = (bf16[32,32,128]{2,1,0:T(8,128)(2,1)S(1)}, bf16[32,32,128]{2,1,0:T(8,128)(2,1)S(1)}, u32[]{:S(2)}, u32[]{:S(2)}) collective-permute-start(bf16[32,32,128]{2,1,0:T(8,128)(2,1)S(1)} %slice.16.mine), channel_id=1, source_target_pairs={{0,3},{1,0},{2,1},{3,2},{4,7},{5,4},{6,5},{7,6},{8,11},{9,8},{10,9... | collective-permute-start | bytes 786440 | tf_op jit(solution)/shard_map/ppermute | solution.py:121
  44.5 8.9 %collective-permute-start.3 = (bf16[32,32,128]{2,1,0:T(8,128)(2,1)S(1)}, bf16[32,32,128]{2,1,0:T(8,128)(2,1)S(1)}, u32[]{:S(2)}, u32[]{:S(2)}) collective-permute-start(bf16[32,32,128]{2,1,0:T(8,128)(2,1)S(1)} %slice.16.mine), channel_id=1, source_target_pairs={{0,1},{1,2},{2,3},{3,0},{4,5},{5,6},{6,7},{7,4},{8,9},{9,10},{10,1... | collective-permute-start | bytes 786440 | tf_op jit(solution)/shard_map/ppermute | solution.py:121
  52.2 11.8 %collective-permute-start.6 = (bf16[16,32,128]{2,1,0:T(8,128)(2,1)S(1)}, bf16[16,32,128]{2,1,0:T(8,128)(2,1)S(1)}, u32[]{:S(2)}, u32[]{:S(2)}) collective-permute-start(bf16[16,32,128]{2,1,0:T(8,128)(2,1)S(1)} %slice.18), channel_id=1, source_target_pairs={{0,3},{1,0},{2,1},{3,2},{4,7},{5,4},{6,5},{7,6},{8,11},{9,8},{10,9... | collective-permute-start | bytes 393224 | tf_op jit(solution)/shard_map/ppermute | solution.py:121
  53.4 10.6 %collective-permute-start.5 = (bf16[16,32,128]{2,1,0:T(8,128)(2,1)S(1)}, bf16[16,32,128]{2,1,0:T(8,128)(2,1)S(1)}, u32[]{:S(2)}, u32[]{:S(2)}) collective-permute-start(bf16[16,32,128]{2,1,0:T(8,128)(2,1)S(1)} %slice.17), channel_id=1, source_target_pairs={{0,1},{1,2},{2,3},{3,0},{4,5},{5,6},{6,7},{7,4},{8,9},{9,10},{10,1... | collective-permute-start | bytes 393224 | tf_op jit(solution)/shard_map/ppermute | solution.py:121
  55.7 4.8 %collective-permute-start.8 = (bf16[4,256]{1,0:T(4,128)(2,1)S(1)}, bf16[4,256]{1,0:T(4,128)(2,1)S(1)}, u32[]{:S(2)}, u32[]{:S(2)}) collective-permute-start(bf16[4,256]{1,0:T(4,128)(2,1)S(1)} %copy-done.3), channel_id=1, source_target_pairs={{0,3},{1,0},{2,1},{3,2},{4,7},{5,4},{6,5},{7,6},{8,11},{9,8},{10,9... | collective-permute-start | bytes 6152 | tf_op jit(solution)/shard_map/ppermute | solution.py:121
  56.0 4.5 %collective-permute-start.7 = (bf16[4,256]{1,0:T(4,128)(2,1)S(1)}, bf16[4,256]{1,0:T(4,128)(2,1)S(1)}, u32[]{:S(2)}, u32[]{:S(2)}) collective-permute-start(bf16[4,256]{1,0:T(4,128)(2,1)S(1)} %copy-done.3), channel_id=1, source_target_pairs={{0,1},{1,2},{2,3},{3,0},{4,5},{5,6},{6,7},{7,4},{8,9},{9,10},{10,1... | collective-permute-start | bytes 6152 | tf_op jit(solution)/shard_map/ppermute | solution.py:121
  58.9 5.1 %collective-permute-start.9 = (bf16[4,256]{1,0:T(4,128)(2,1)S(1)}, bf16[4,256]{1,0:T(4,128)(2,1)S(1)}, u32[]{:S(2)}, u32[]{:S(2)}) collective-permute-start(bf16[4,256]{1,0:T(4,128)(2,1)S(1)} %copy-done.3), channel_id=1, source_target_pairs={{0,2},{1,3},{2,0},{3,1},{4,6},{5,7},{6,4},{7,5},{8,10},{9,11},{10,... | collective-permute-start | bytes 6152 | tf_op jit(solution)/shard_map/ppermute | solution.py:121

commit v2 on v0

v2 whole, which is shorter than its diff:
```python
import jax
import jax.numpy as jnp
from jax import lax
from jax.experimental import pallas as pl
from jax.experimental.pallas import tpu as pltpu
from jax.sharding import Mesh
from jax.sharding import PartitionSpec as P

KF = ("kf_0", "kf_1", "kf_2")
ZY = ("kf_0", "kf_1")
KF_KC = ("kf_0", "kf_1", "kf_2", "kc")
LANES = 128
PAIRS = 16
POINTS = 4
PEERS = 32
BF16 = jnp.bfloat16
F32 = jnp.float32
VMEM = pl.BlockSpec(memory_space=pltpu.VMEM)
SMEM = pl.BlockSpec(memory_space=pltpu.SMEM)
ANY = pl.BlockSpec(memory_space=pl.ANY)


def iota(shape, dim):
    return lax.broadcasted_iota(jnp.int32, shape, dim)


def dot_t(a, b):
    return lax.dot_general(a, b, (((1,), (1,)), ((), ())), preferred_element_type=F32)


def pack_rows(near, rows, out, copies, at_row):
    kc = lax.axis_index("kc")
    core = lax.axis_index("kf_2")
    for b in range(16):
        block = rows[:, b * LANES : (b + 1) * LANES].astype(F32)
        for s in range(8):
            turned = pltpu.roll(block, s * PAIRS, 1) if s else block
            copies[s, b] = turned.astype(BF16)
    group = iota((PAIRS, LANES), 1) // PAIRS
    base = 16 * core + 4 * kc

    def body(d, carry):
        tile = None
        for j in range(POINTS):
            c = near[32 * d + base + j]
            for lo in range(2):
                at = lo * POINTS + j
                piece = copies[(at - c) & 7, c >> 3, lo * PAIRS : (lo + 1) * PAIRS, :]
                tile = piece if tile is None else jnp.where(group == at, piece, tile)
        out[d, pl.ds(at_row, PAIRS), :] = tile
        return carry

    lax.fori_loop(0, PEERS, body, 0, unroll=4)


def pack_own_kernel(near, own, out, copies):
    pack_rows(near, own, out, copies, pl.multiple_of(lax.axis_index("kf_2") * PAIRS, PAIRS))


def pack_other_kernel(near, other, coef_own, coef_other, half_packed, out, copies):
    core = lax.axis_index("kf_2")
    pack_rows(near, other, out, copies, pl.multiple_of((1 - core) * PAIRS, PAIRS))
    a = coef_own[...].astype(F32)
    o = coef_other[...].astype(F32)
    first = jnp.where(core == 0, a, o)
    second = jnp.where(core == 0, o, a)
    coef = jnp.concatenate(
        [first[:, :LANES], first[:, LANES:], second[:, :LANES], second[:, LANES:]], axis=0
    ).astype(BF16)
    for d in range(PEERS):
        out[d, 2 * PAIRS :, :] = coef


def split_kernel(received, coef_own, up, down, across):
    kc = lax.axis_index("kc")
    mine = coef_own[...].astype(F32)
    mine = jnp.concatenate([mine[:, :LANES], mine[:, LANES:]], axis=0)
    mine = jnp.concatenate([mine, jnp.zeros_like(mine)], axis=0).astype(BF16)
    for zy in range(PEERS):
        for h in range(2):
            block = received[zy, h * PAIRS : (h + 1) * PAIRS, :]
            up[2 * zy + h] = block
            down[2 * zy + h] = block
    for step, target, at in ((1, up, 64), (3, down, 64), (2, across, 0)):
        first = (kc + step) % 4 * 8
        for p in range(8):
            target[at + p] = received[first + p, 2 * PAIRS :, :]
        target[at + 8] = mine


def spread(row_of, count):
    keep = iota((8, LANES), 1) // PAIRS == iota((8, LANES), 0)
    pieces = []
    for p in range(count):
        for half in range(2):
            pieces.append(jnp.where(keep, jnp.broadcast_to(row_of(p, half), (8, LANES)), 0.0))
    return jnp.concatenate(pieces, axis=0).astype(BF16)


def repeat_matrix():
    same = iota((LANES, LANES), 0) % PAIRS == iota((LANES, LANES), 1) % PAIRS
    return jnp.where(same, 1.0, 0.0).astype(BF16)


def set_halves(halves):
    low = iota((PAIRS, LANES), 1) < 64
    halves[0] = jnp.where(low, 1.0, 0.0).astype(BF16)
    halves[1] = jnp.where(low, 0.0, 1.0).astype(BF16)


def rotate_points(near, halves, first, sources):
    picks = [[] for _ in sources]
    for i in range(8):
        c = near[first + i]
        keep = halves[c & 1]
        for n, (blocks, _) in enumerate(sources):
            picks[n].append(blocks[c >> 1] * keep)
    return [dot_t(turn, jnp.concatenate(p, axis=0)).astype(BF16) for p, (_, turn) in zip(picks, sources)]


def middle_kernel(near, received, mine, left, right, far_coef, out, cols, turn_far, pieces, turns, halves, result, sem):
    kc = lax.axis_index("kc")
    set_halves(halves)
    repeat = repeat_matrix()
    for p in range(8):
        pieces[kc, p] = received[kc * 8 + p, 2 * PAIRS :, :].astype(F32)
        pieces[(kc + 3) % 4, p] = left[64 + p].astype(F32)
        pieces[(kc + 1) % 4, p] = right[64 + p].astype(F32)
        pieces[(kc + 2) % 4, p] = far_coef[p].astype(F32)
    own_group = iota((64, LANES), 1) // PAIRS % POINTS == iota((64, LANES), 0) // PAIRS
    for n, row in enumerate((mine[72], left[72], right[72], far_coef[8])):
        row = row.astype(F32)
        wide = jnp.dot(
            spread(lambda p, half: row[half * POINTS + p : half * POINTS + p + 1], POINTS),
            repeat,
            preferred_element_type=F32,
        )
        value = jnp.where(own_group, wide, 0.0).astype(BF16)
        if n < 3:
            turns[n] = value
        else:
            turn_far[...] = value
    diag = iota((LANES, LANES), 0) // PAIRS == iota((LANES, LANES), 1) // PAIRS

    def copy(n, v):
        row = pl.multiple_of((kc + (0, 3, 1)[n]) % 4 * 64, 64)
        at = pl.ds(pl.multiple_of(v * 512, 512), 512)
        return pltpu.make_async_copy(result.at[n, :, at], out.at[pl.ds(row, 64), at], sem.at[n, v])

    def body(v, carry):
        for h in range(2):
            for par in range(2):
                u = v * 4 + h * 2 + par

                def row_of(p, half):
                    r = h * 8 + half * POINTS + p % POINTS
                    return pieces[par * 2 + p // POINTS, v, r : r + 1, :]

                wide = jnp.dot(spread(row_of, 8), repeat, preferred_element_type=F32)
                block = jnp.where(diag, wide, 0.0).astype(BF16)
                cols[u] = block
                turned = rotate_points(
                    near, halves, 256 * kc + 8 * u, ((mine, turns[0]), (left, turns[1]), (right, turns[2]))
                )
                at = pl.ds(pl.multiple_of(u * LANES, LANES), LANES)
                for n in range(3):
                    result[n, :, at] = dot_t(turned[n], block).astype(BF16)
        for n in range(3):
            copy(n, v).start()
        return carry

    lax.fori_loop(0, 8, body, 0)

    def finish(v, carry):
        for n in range(3):
            copy(n, v).wait()
        return carry

    lax.fori_loop(0, 8, finish, 0)


def far_kernel(near, far, cols, turn_far, partial, out, halves, result, sem):
    kc = lax.axis_index("kc")
    set_halves(halves)

    def copy(v):
        row = pl.multiple_of((kc + 2) % 4 * 64, 64)
        at = pl.ds(pl.multiple_of(v * 512, 512), 512)
        return pltpu.make_async_copy(result.at[:, at], out.at[pl.ds(row, 64), at], sem.at[v])

    def body(v, carry):
        for s in range(4):
            u = v * 4 + s
            (turned,) = rotate_points(near, halves, 256 * kc + 8 * u, ((far, turn_far[...]),))
            at = pl.ds(pl.multiple_of(u * LANES, LANES), LANES)
            result[:, at] = dot_t(turned, cols[u]).astype(BF16)
        copy(v).start()
        return carry

    lax.fori_loop(0, 8, body, 0)

    def finish(v, carry):
        copy(v).wait()
        return carry

    lax.fori_loop(0, 8, finish, 0)


def call(kernel, outs, in_specs, out_specs, scratch, flops, aliases=None):
    return pl.pallas_call(
        kernel,
        out_shape=outs,
        in_specs=in_specs,
        out_specs=out_specs,
        scratch_shapes=scratch,
        input_output_aliases=aliases or {},
        compiler_params=pltpu.CompilerParams(vmem_limit_bytes=8 << 20),
        cost_estimate=pl.CostEstimate(flops=flops, bytes_accessed=flops // 10, transcendentals=0),
    )


def shape(*dims):
    return jax.ShapeDtypeStruct(dims, BF16)


def shift(value, by):
    return lax.ppermute(value, "kc", [(i, (i + by) % 4) for i in range(4)])


def partner(value):
    return lax.ppermute(value, "kf_2", [(0, 1), (1, 0)])


def shards(kernel_coarse, coefficients, nearest):
    other = partner(kernel_coarse)
    coef_other = partner(coefficients)
    copies = [pltpu.VMEM((8, 16, 32, LANES), BF16)]
    packed = call(pack_own_kernel, shape(PEERS, 48, LANES), [SMEM, VMEM], VMEM, copies, 1000000)(
        nearest, kernel_coarse
    )
    packed = call(
        pack_other_kernel, shape(PEERS, 48, LANES), [SMEM] + [VMEM] * 4, VMEM, copies, 1000000, {4: 0}
    )(nearest, other, coefficients, coef_other, packed)
    received = lax.all_to_all(packed, ZY, split_axis=0, concat_axis=0, tiled=True)
    block = (PAIRS, LANES)
    up, down, across = call(
        split_kernel, (shape(73, *block), shape(73, *block), shape(9, *block)), [VMEM, VMEM], (VMEM,) * 3, [], 100000
    )(received, coefficients)
    left = shift(up, 1)
    right = shift(down, -1)
    far_coef = shift(across, 2)
    far = jnp.concatenate([shift(left[:PEERS], 1), shift(right[PEERS:64], -1)], axis=0)
    half_masks = pltpu.VMEM((2, *block), BF16)
    partial, cols, turn_far = call(
        middle_kernel,
        (shape(256, 4096), shape(32, LANES, LANES), shape(64, LANES)),
        [SMEM] + [VMEM] * 5,
        (ANY, VMEM, VMEM),
        [
            pltpu.VMEM((4, 8, *block), F32),
            pltpu.VMEM((3, 64, LANES), BF16),
            half_masks,
            pltpu.VMEM((3, 64, 4096), BF16),
            pltpu.SemaphoreType.DMA((3, 8)),
        ],
        8000000,
    )(nearest, received, up, left, right, far_coef)
    return call(
        far_kernel,
        shape(256, 4096),
        [SMEM] + [VMEM] * 3 + [ANY],
        ANY,
        [half_masks, pltpu.VMEM((64, 4096), BF16), pltpu.SemaphoreType.DMA((8,))],
        3000000,
        {4: 0},
    )(nearest, far, cols, turn_far, partial)


def solution(mesh):
    split = Mesh(mesh.devices.reshape(8, 4, 2, mesh.shape["kc"]), KF_KC)
    return jax.shard_map(
        shards,
        mesh=split,
        in_specs=(P(KF, None), P(KF_KC, None), P()),
        out_specs=P(KF, "kc"),
        check_vma=False,
    )
```

time: 118 us -> 63.3 us (0.54); the launches traced: 116 us -> 63.2 us
  local copies, waits for them, and re-layouts: 32.8 us -> 2.29 us
  blocking collectives: 47.7 us -> 26.7 us
  Pallas kernels: 0 us -> 16.3 us
  starting transfers between devices: 16.9 us -> 7.2 us
  matrix products: 3.53 us -> 0 us
  waiting for transfers between devices: 12.8 us -> 10.5 us
  other arithmetic: 1.75 us -> 0.03 us
    all_gather x4 -> x0, blocking collectives: 47.7 us -> none  [gather_in_order(): pieces = lax.all_gather(pieces, axes[k])]
    all_to_all x0 -> x1, blocking collectives: none -> 26.7 us  [shards(): lax.all_to_all(packed, ZY, split_axis=0, concat_axis=0, tiled=True)]
    all_to_all x2 -> x0, starting transfers between devices: 16.9 us -> none  [the longest x1 12.1 us: shards(): lax.all_to_all(outgoing, KF, split_axis=1, concat_axis=0, tiled=True)]
    pallas_call x0 -> x5, Pallas kernels: none -> 16.3 us  [the longest x1 8.86 us: shards(): call(middle_kernel, (shape(256, 4096), shape(32, LANES, LANES), shape(64,...]
    gather x3 -> x0, local copies, waits for them, and re-layouts: 13.3 us -> none  [the longest x2 12.5 us: shards(): outgoing = jnp.take(kernel_coarse, columns, axis=1)]
    all_to_all x2 -> x0, waiting for transfers between devices: 12.8 us -> none  [the longest x1 12.8 us: shards(): lax.all_to_all(outgoing, KF, split_axis=1, concat_axis=0, tiled=True)]
    ppermute x0 -> x7, waiting for transfers between devices: none -> 10.5 us  [the longest x5 10.5 us: shift(): return lax.ppermute(value, 'kc', [(i, (i + by) % 4) for i in range(4)])]
    ppermute x0 -> x7, starting transfers between devices: none -> 7.2 us  [the longest x5 6.69 us: shift(): return lax.ppermute(value, 'kc', [(i, (i + by) % 4) for i in range(4)])]
  transfers between devices with their start and end apart: 2 -> 7, of which waited for: 1 -> 2; matrix products, arithmetic and copies ran while one was open for 5% -> 0% of each run, Pallas kernels for 0% -> 16%
where the time goes in v2:
time: 63.3 us; the launch traced here: 63.2 us
  blocking collectives  26.7 us (42%)
  Pallas kernels  16.3 us (26%)
  waiting for transfers between devices  10.5 us (17%)
  starting transfers between devices  7.2 us (11%)
  local copies, waits for them, and re-layouts  2.29 us (4%)
    all_to_all x1, blocking collectives, shards(): lax.all_to_all(packed, ZY, split_axis=0, concat_axis=0, tiled=True)  26.7 us
    ppermute x5, waiting for transfers between devices, shift(): return lax.ppermute(value, 'kc', [(i, (i + by) % 4) for i in range(4)])  10.5 us
    pallas_call x1, Pallas kernels, shards(): call(middle_kernel, (shape(256, 4096), shape(32, LANES, LANES), shape(64,...  8.86 us
    ppermute x5, starting transfers between devices, shift(): return lax.ppermute(value, 'kc', [(i, (i + by) % 4) for i in range(4)])  6.69 us
    pallas_call x1, Pallas kernels, shards(): call(far_kernel, shape(256, 4096), [SMEM] + [VMEM] * 3 + [ANY], ANY, [hal...  4.33 us
    unnamed x8, local copies, waits for them, and re-layouts  2.27 us
    pallas_call x1, Pallas kernels, shards(): call(pack_other_kernel, shape(PEERS, 48, LANES), [SMEM] + [VMEM] * 4, VME...  1.52 us
    pallas_call x1, Pallas kernels, shards(): call(pack_own_kernel, shape(PEERS, 48, LANES), [SMEM, VMEM], VMEM, copies...  1.5 us
  transfers between devices with their start and end apart: 7, of which 2 were waited for; matrix products, arithmetic and copies ran while one was open for 0% of the time, Pallas kernels for 16%

profile of v2, /device:TPU:6, one launch (start us, length us, event | category | flops | bytes accessed | tf_op | source)
XLA Modules:
  0.0 63.2 jit_solution(562361566764721194)
XLA Ops:
  0.0 0.0 collective-permute-start
  0.0 0.5 collective-permute-start.1
  0.5 0.9 %copy-done = bf16[32,2048]{1,0:T(8,128)(2,1)S(1)} copy-done((bf16[32,2048]{1,0:T(8,128)(2,1)S(1)}, bf16[32,2048]{1,0:T(8,128)(2,1)}, u32[]{:S(2)}) %copy-start) | copy-done | bytes 131096
  1.4 0.7 %copy-done.1 = s32[1024]{0:T(1024)S(1)} copy-done((s32[1024]{0:T(1024)S(1)}, s32[1024]{0:T(1024)}, u32[]{:S(2)}) %copy-start.1) | copy-done | bytes 4120
  2.1 1.5 %shard_map.37.half_packed = bf16[32,48,128]{2,1,0:T(8,128)(2,1)S(1)} custom-call(s32[1024]{0:T(1024)S(1)} %copy-done.1, bf16[32,2048]{1,0:T(8,128)(2,1)S(1)} %copy-done), custom_call_target="tpu_custom_call" | custom-call | flops 1000000 | bytes 100000 | tf_op jit(solution)/shard_map/pallas_call | solution.py:238
  3.6 0.0 collective-permute-done.1.coef_other
  3.6 0.0 collective-permute-done.other
  3.6 0.0 copy-start.3
  3.6 0.7 %copy-done.3 = bf16[4,256]{1,0:T(4,128)(2,1)S(1)} copy-done((bf16[4,256]{1,0:T(4,128)(2,1)S(1)}, bf16[4,256]{1,0:T(4,128)(2,1)}, u32[]{:S(2)}) %copy-start.3) | copy-done | bytes 2072
  4.3 1.5 %shard_map.38 = bf16[32,48,128]{2,1,0:T(8,128)(2,1)S(1)} custom-call(s32[1024]{0:T(1024)S(1)} %copy-done.1, bf16[32,2048]{1,0:T(8,128)(2,1)S(1)} %collective-permute-done.other, bf16[4,256]{1,0:T(4,128)(2,1)S(1)} %copy-done.3, bf16[4,256]{1,0:T(4,128)(2,1)S(1)} %collective-permute-done.1.coef_other, ...), custom_call_target="tpu_custom_call", output_to_operand_aliasing={{}: (4, {})} | custom-call | flops 1000000 | bytes 100000 | tf_op jit(solution)/shard_map/pallas_call | solution.py:241
  5.8 26.7 %all_to_all.5.received = bf16[32,48,128]{2,1,0:T(8,128)(2,1)S(1)} all-to-all(bf16[32,48,128]{2,1,0:T(8,128)(2,1)S(1)} %shard_map.38), channel_id=1, replica_groups=mesh['kf_0'=8,'kf_1'=4,'kf_2'=2,'kc'=4] {'kf_0','kf_1'}, dimensions={0} | all-to-all | bytes 786432 | tf_op jit(solution)/shard_map/all_to_all | solution.py:244
  32.6 0.1 shard_map.39
  32.7 0.9 %collective-permute-start.4 = (bf16[73,16,128]{2,1,0:T(8,128)(2,1)S(1)}, bf16[73,16,128]{2,1,0:T(8,128)(2,1)S(1)}, u32[]{:S(2)}, u32[]{:S(2)}) collective-permute-start(bf16[73,16,128]{2,1,0:T(8,128)(2,1)S(1)} %get-tuple-element.12), channel_id=1, source_target_pairs={{0,3},{1,0},{2,1},{3,2},{4,7},{5,4},{6,5},{7,6},{8,11},{9,8},{10,9... | collective-permute-start | bytes 897032 | tf_op jit(solution)/shard_map/ppermute | solution.py:227
  33.6 2.4 %collective-permute-start.2 = (bf16[73,16,128]{2,1,0:T(8,128)(2,1)S(1)}, bf16[73,16,128]{2,1,0:T(8,128)(2,1)S(1)}, u32[]{:S(2)}, u32[]{:S(2)}) collective-permute-start(bf16[73,16,128]{2,1,0:T(8,128)(2,1)S(1)} %get-tuple-element.11.mine), channel_id=1, source_target_pairs={{0,1},{1,2},{2,3},{3,0},{4,5},{5,6},{6,7},{7,4},{8,9},{9,10},{10,1... | collective-permute-start | bytes 897032 | tf_op jit(solution)/shard_map/ppermute | solution.py:227
  36.0 5.0 %collective-permute-done.4.right = bf16[73,16,128]{2,1,0:T(8,128)(2,1)S(1)} collective-permute-done((bf16[73,16,128]{2,1,0:T(8,128)(2,1)S(1)}, bf16[73,16,128]{2,1,0:T(8,128)(2,1)S(1)}, u32[]{:S(2)}, u32[]{:S(2)}) %collective-permute-start.4) | collective-permute-done | bytes 299040 | tf_op jit(solution)/shard_map/ppermute | solution.py:227
  41.0 0.1 collective-permute-start.5
  41.1 0.0 collective-permute-done.2.left
  41.1 3.3 %collective-permute-start.3 = (bf16[32,16,128]{2,1,0:T(8,128)(2,1)S(1)}, bf16[32,16,128]{2,1,0:T(8,128)(2,1)S(1)}, u32[]{:S(2)}, u32[]{:S(2)}) collective-permute-start(bf16[32,16,128]{2,1,0:T(8,128)(2,1)S(1)} %slice.8), channel_id=1, source_target_pairs={{0,1},{1,2},{2,3},{3,0},{4,5},{5,6},{6,7},{7,4},{8,9},{9,10},{10,1... | collective-permute-start | bytes 393224 | tf_op jit(solution)/shard_map/ppermute | solution.py:227
  44.4 0.0 collective-permute-start.6
  44.4 5.5 %collective-permute-done.6.far_coef = bf16[9,16,128]{2,1,0:T(8,128)(2,1)S(1)} collective-permute-done((bf16[9,16,128]{2,1,0:T(8,128)(2,1)S(1)}, bf16[9,16,128]{2,1,0:T(8,128)(2,1)S(1)}, u32[]{:S(2)}, u32[]{:S(2)}) %collective-permute-start.6) | collective-permute-done | bytes 36896 | tf_op jit(solution)/shard_map/ppermute | solution.py:227
  49.9 8.9 %shard_map.40 = (bf16[256,4096]{1,0:T(8,128)(2,1)}, bf16[32,128,128]{2,1,0:T(8,128)(2,1)S(1)}, bf16[64,128]{1,0:T(8,128)(2,1)S(1)}) custom-call(s32[1024]{0:T(1024)S(1)} %copy-done.2, bf16[32,48,128]{2,1,0:T(8,128)(2,1)S(1)} %all_to_all.5.received, bf16[73,16,128]{2,1,0:T(8,128)(2,1)S(1)} %get-tuple-element.11.mine, ...), custom_call_target="tpu_custom_call" | custom-call | flops 8000000 | bytes 800000 | tf_op jit(solution)/shard_map/pallas_call | solution.py:254
  58.8 0.0 collective-permute-done.5
  58.8 0.0 collective-permute-done.3
  58.8 4.3 %shard_map.41 = bf16[256,4096]{1,0:T(8,128)(2,1)} custom-call(s32[1024]{0:T(1024)S(1)} %copy-done.2, bf16[64,16,128]{2,1,0:T(8,128)(2,1)S(1)} %pad_maximum_fusion.far, bf16[32,128,128]{2,1,0:T(8,128)(2,1)S(1)} %get-tuple-element.14.cols, bf16[64,128]{1,0:T(8,128)(2,1)S(1)} %get-tuple-element.15.turn_far, ...), custom_call_target="tpu_custom_call", output_to_operand_aliasing={{}: (4, {})} | custom-call | flops 3000000 | bytes 300000 | tf_op jit(solution)/shard_map/pallas_call | solution.py:268
  (7 shorter events, 0.1 us)
Async XLA Ops:
  0.0 3.6 %collective-permute-start = (bf16[32,2048]{1,0:T(8,128)(2,1)}, bf16[32,2048]{1,0:T(8,128)(2,1)S(1)}, u32[]{:S(2)}, u32[]{:S(2)}) collective-permute-start(bf16[32,2048]{1,0:T(8,128)(2,1)} %own.1), channel_id=1, source_target_pairs={{0,4},{4,0},{1,5},{5,1},{2,6},{6,2},{3,7},{7,3},{8,12},{12,8},{9,1... | collective-permute-start | bytes 393224 | tf_op jit(solution)/shard_map/ppermute | solution.py:231
  0.0 3.6 %collective-permute-start.1 = (bf16[4,256]{1,0:T(4,128)(2,1)}, bf16[4,256]{1,0:T(4,128)(2,1)S(1)}, u32[]{:S(2)}, u32[]{:S(2)}) collective-permute-start(bf16[4,256]{1,0:T(4,128)(2,1)} %coef_own.3), channel_id=1, source_target_pairs={{0,4},{4,0},{1,5},{5,1},{2,6},{6,2},{3,7},{7,3},{8,12},{12,8},{9,1... | collective-permute-start | bytes 6152 | tf_op jit(solution)/shard_map/ppermute | solution.py:231
  0.5 0.9 %copy-start = (bf16[32,2048]{1,0:T(8,128)(2,1)S(1)}, bf16[32,2048]{1,0:T(8,128)(2,1)}, u32[]{:S(2)}) copy-start(bf16[32,2048]{1,0:T(8,128)(2,1)} %own.1) | copy-start | bytes 393220
  1.4 0.7 %copy-start.1 = (s32[1024]{0:T(1024)S(1)}, s32[1024]{0:T(1024)}, u32[]{:S(2)}) copy-start(s32[1024]{0:T(1024)} %near.7) | copy-start | bytes 12292
  2.1 47.8 %copy-start.2 = (s32[1024]{0:T(1024)S(1)}, s32[1024]{0:T(1024)}, u32[]{:S(2)}) copy-start(s32[1024]{0:T(1024)} %near.7) | copy-start | bytes 12292
  3.6 0.7 %copy-start.3 = (bf16[4,256]{1,0:T(4,128)(2,1)S(1)}, bf16[4,256]{1,0:T(4,128)(2,1)}, u32[]{:S(2)}) copy-start(bf16[4,256]{1,0:T(4,128)(2,1)} %coef_own.3) | copy-start | bytes 6148
  32.7 8.3 %collective-permute-start.4 = (bf16[73,16,128]{2,1,0:T(8,128)(2,1)S(1)}, bf16[73,16,128]{2,1,0:T(8,128)(2,1)S(1)}, u32[]{:S(2)}, u32[]{:S(2)}) collective-permute-start(bf16[73,16,128]{2,1,0:T(8,128)(2,1)S(1)} %get-tuple-element.12), channel_id=1, source_target_pairs={{0,3},{1,0},{2,1},{3,2},{4,7},{5,4},{6,5},{7,6},{8,11},{9,8},{10,9... | collective-permute-start | bytes 897032 | tf_op jit(solution)/shard_map/ppermute | solution.py:227
  33.6 7.5 %collective-permute-start.2 = (bf16[73,16,128]{2,1,0:T(8,128)(2,1)S(1)}, bf16[73,16,128]{2,1,0:T(8,128)(2,1)S(1)}, u32[]{:S(2)}, u32[]{:S(2)}) collective-permute-start(bf16[73,16,128]{2,1,0:T(8,128)(2,1)S(1)} %get-tuple-element.11.mine), channel_id=1, source_target_pairs={{0,1},{1,2},{2,3},{3,0},{4,5},{5,6},{6,7},{7,4},{8,9},{9,10},{10,1... | collective-permute-start | bytes 897032 | tf_op jit(solution)/shard_map/ppermute | solution.py:227
  41.0 17.7 %collective-permute-start.5 = (bf16[32,16,128]{2,1,0:T(8,128)(2,1)S(1)}, bf16[32,16,128]{2,1,0:T(8,128)(2,1)S(1)}, u32[]{:S(2)}, u32[]{:S(2)}) collective-permute-start(bf16[32,16,128]{2,1,0:T(8,128)(2,1)S(1)} %slice.9), channel_id=1, source_target_pairs={{0,3},{1,0},{2,1},{3,2},{4,7},{5,4},{6,5},{7,6},{8,11},{9,8},{10,9... | collective-permute-start | bytes 393224 | tf_op jit(solution)/shard_map/ppermute | solution.py:227
  41.1 17.6 %collective-permute-start.3 = (bf16[32,16,128]{2,1,0:T(8,128)(2,1)S(1)}, bf16[32,16,128]{2,1,0:T(8,128)(2,1)S(1)}, u32[]{:S(2)}, u32[]{:S(2)}) collective-permute-start(bf16[32,16,128]{2,1,0:T(8,128)(2,1)S(1)} %slice.8), channel_id=1, source_target_pairs={{0,1},{1,2},{2,3},{3,0},{4,5},{5,6},{6,7},{7,4},{8,9},{9,10},{10,1... | collective-permute-start | bytes 393224 | tf_op jit(solution)/shard_map/ppermute | solution.py:227
  44.4 5.5 %collective-permute-start.6 = (bf16[9,16,128]{2,1,0:T(8,128)(2,1)S(1)}, bf16[9,16,128]{2,1,0:T(8,128)(2,1)S(1)}, u32[]{:S(2)}, u32[]{:S(2)}) collective-permute-start(bf16[9,16,128]{2,1,0:T(8,128)(2,1)S(1)} %get-tuple-element.13), channel_id=1, source_target_pairs={{0,2},{1,3},{2,0},{3,1},{4,6},{5,7},{6,4},{7,5},{8,10},{9,11},{10,... | collective-permute-start | bytes 110600 | tf_op jit(solution)/shard_map/ppermute | solution.py:227

commit v3 on v2

--- a/solution.py
+++ b/solution.py
@@ -5,6 +5,7 @@
 from jax.experimental.pallas import tpu as pltpu
 from jax.sharding import Mesh
 from jax.sharding import PartitionSpec as P
+
 
 KF = ("kf_0", "kf_1", "kf_2")
 ZY = ("kf_0", "kf_1")
@@ -108,20 +109,22 @@
     halves[1] = jnp.where(low, 0.0, 1.0).astype(BF16)
 
 
-def rotate_points(near, halves, first, sources):
-    picks = [[] for _ in sources]
-    for i in range(8):
+def pick_points(near, halves, first, sources, picked):
+    for i in range(32):
         c = near[first + i]
         keep = halves[c & 1]
-        for n, (blocks, _) in enumerate(sources):
-            picks[n].append(blocks[c >> 1] * keep)
-    return [dot_t(turn, jnp.concatenate(p, axis=0)).astype(BF16) for p, (_, turn) in zip(picks, sources)]
-
-
-def middle_kernel(near, received, mine, left, right, far_coef, out, cols, turn_far, pieces, turns, halves, result, sem):
+        for n, blocks in enumerate(sources):
+            picked[n, i * PAIRS : (i + 1) * PAIRS, :] = blocks[c >> 1] * keep
+
+
+def middle_kernel(
+    near, received, mine, left, right, far_coef, out, cols, turn_far, pieces, turns, halves, diag, picked, turned, result, sem
+):
     kc = lax.axis_index("kc")
     set_halves(halves)
     repeat = repeat_matrix()
+    same = iota((LANES, LANES), 0) // PAIRS == iota((LANES, LANES), 1) // PAIRS
+    diag[...] = jnp.where(same, 1.0, 0.0).astype(BF16)
     for p in range(8):
         pieces[kc, p] = received[kc * 8 + p, 2 * PAIRS :, :].astype(F32)
         pieces[(kc + 3) % 4, p] = left[64 + p].astype(F32)
@@ -140,70 +143,70 @@
             turns[n] = value
         else:
             turn_far[...] = value
-    diag = iota((LANES, LANES), 0) // PAIRS == iota((LANES, LANES), 1) // PAIRS
 
     def copy(n, v):
         row = pl.multiple_of((kc + (0, 3, 1)[n]) % 4 * 64, 64)
-        at = pl.ds(pl.multiple_of(v * 512, 512), 512)
+        at = pl.ds(v * 1024, 1024)
         return pltpu.make_async_copy(result.at[n, :, at], out.at[pl.ds(row, 64), at], sem.at[n, v])
 
-    def body(v, carry):
-        for h in range(2):
-            for par in range(2):
-                u = v * 4 + h * 2 + par
-
-                def row_of(p, half):
-                    r = h * 8 + half * POINTS + p % POINTS
-                    return pieces[par * 2 + p // POINTS, v, r : r + 1, :]
-
-                wide = jnp.dot(spread(row_of, 8), repeat, preferred_element_type=F32)
-                block = jnp.where(diag, wide, 0.0).astype(BF16)
-                cols[u] = block
-                turned = rotate_points(
-                    near, halves, 256 * kc + 8 * u, ((mine, turns[0]), (left, turns[1]), (right, turns[2]))
-                )
-                at = pl.ds(pl.multiple_of(u * LANES, LANES), LANES)
+    def build(v):
+        for s in range(4):
+            h, par = s // 2, s % 2
+
+            def row_of(p, half):
+                r = h * 8 + half * POINTS + p % POINTS
+                return pieces[par * 2 + p // POINTS, v, r : r + 1, :]
+
+            wide = jnp.dot(spread(row_of, 8), repeat, preferred_element_type=F32)
+            cols[4 * v + s] = wide.astype(BF16) * diag[...]
+
+    def turn(v):
+        pick_points(near, halves, 256 * kc + 32 * v, (mine, left, right), picked)
+        for n in range(3):
+            turned[n * 64 : (n + 1) * 64, v * 512 : (v + 1) * 512] = dot_t(turns[n], picked[n]).astype(BF16)
+
+    def expand(v):
+        for u in range(4 * v, 4 * v + 4):
+            at = slice(u * LANES, (u + 1) * LANES)
+            block = dot_t(turned[:, at], cols[u]).astype(BF16)
+            for n in range(3):
+                result[n, :, at] = block[n * 64 : (n + 1) * 64]
+
+    for v in range(9):
+        if v < 8:
+            build(v)
+            turn(v)
+        if v > 0:
+            expand(v - 1)
+            if v % 2 == 0:
                 for n in range(3):
-                    result[n, :, at] = dot_t(turned[n], block).astype(BF16)
-        for n in range(3):
-            copy(n, v).start()
-        return carry
-
-    lax.fori_loop(0, 8, body, 0)
-
-    def finish(v, carry):
+                    copy(n, v // 2 - 1).start()
+    for v in range(4):
         for n in range(3):
             copy(n, v).wait()
-        return carry
-
-    lax.fori_loop(0, 8, finish, 0)
-
-
-def far_kernel(near, far, cols, turn_far, partial, out, halves, result, sem):
+
+
+def far_kernel(near, far, cols, turn_far, partial, out, halves, picked, turned, result, sem):
     kc = lax.axis_index("kc")
     set_halves(halves)
 
     def copy(v):
         row = pl.multiple_of((kc + 2) % 4 * 64, 64)
-        at = pl.ds(pl.multiple_of(v * 512, 512), 512)
+        at = pl.ds(v * 1024, 1024)
         return pltpu.make_async_copy(result.at[:, at], out.at[pl.ds(row, 64), at], sem.at[v])
 
-    def body(v, carry):
-        for s in range(4):
-            u = v * 4 + s
-            (turned,) = rotate_points(near, halves, 256 * kc + 8 * u, ((far, turn_far[...]),))
-            at = pl.ds(pl.multiple_of(u * LANES, LANES), LANES)
-            result[:, at] = dot_t(turned, cols[u]).astype(BF16)
-        copy(v).start()
-        return carry
-
-    lax.fori_loop(0, 8, body, 0)
-
-    def finish(v, carry):
+    for v in range(9):
+        if v < 8:
+            pick_points(near, halves, 256 * kc + 32 * v, (far,), picked.at[v % 2])
+            turned[:, v * 512 : (v + 1) * 512] = dot_t(turn_far[...], picked[v % 2, 0]).astype(BF16)
+        if v > 0:
+            for u in range(4 * v - 4, 4 * v):
+                at = slice(u * LANES, (u + 1) * LANES)
+                result[:, at] = dot_t(turned[:, at], cols[u]).astype(BF16)
+            if v % 2 == 0:
+                copy(v // 2 - 1).start()
+    for v in range(4):
         copy(v).wait()
-        return carry
-
-    lax.fori_loop(0, 8, finish, 0)
 
 
 def call(kernel, outs, in_specs, out_specs, scratch, flops, aliases=None):
@@ -246,9 +249,9 @@
     up, down, across = call(
         split_kernel, (shape(73, *block), shape(73, *block), shape(9, *block)), [VMEM, VMEM], (VMEM,) * 3, [], 100000
     )(received, coefficients)
+    far_coef = shift(across, 2)
     left = shift(up, 1)
     right = shift(down, -1)
-    far_coef = shift(across, 2)
     far = jnp.concatenate([shift(left[:PEERS], 1), shift(right[PEERS:64], -1)], axis=0)
     half_masks = pltpu.VMEM((2, *block), BF16)
     partial, cols, turn_far = call(
@@ -260,8 +263,11 @@
             pltpu.VMEM((4, 8, *block), F32),
             pltpu.VMEM((3, 64, LANES), BF16),
             half_masks,
+            pltpu.VMEM((LANES, LANES), BF16),
+            pltpu.VMEM((3, 512, LANES), BF16),
+            pltpu.VMEM((192, 4096), BF16),
             pltpu.VMEM((3, 64, 4096), BF16),
-            pltpu.SemaphoreType.DMA((3, 8)),
+            pltpu.SemaphoreType.DMA((3, 4)),
         ],
         8000000,
     )(nearest, received, up, left, right, far_coef)
@@ -270,7 +276,13 @@
         shape(256, 4096),
         [SMEM] + [VMEM] * 3 + [ANY],
         ANY,
-        [half_masks, pltpu.VMEM((64, 4096), BF16), pltpu.SemaphoreType.DMA((8,))],
+        [
+            half_masks,
+            pltpu.VMEM((2, 1, 512, LANES), BF16),
+            pltpu.VMEM((64, 4096), BF16),
+            pltpu.VMEM((64, 4096), BF16),
+            pltpu.SemaphoreType.DMA((4,)),
+        ],
         3000000,
         {4: 0},
     )(nearest, far, cols, turn_far, partial)

time: 63.3 us -> 57.2 us (0.904)
  Pallas kernels: 16.3 us -> 10.1 us
    pallas_call x1, Pallas kernels: 8.86 us -> 4.28 us  [shards(): call(middle_kernel, (shape(256, 4096), shape(32, LANES, LANES), shape(64,...]
    pallas_call x1, Pallas kernels: 4.33 us -> 2.73 us  [shards(): call(far_kernel, shape(256, 4096), [SMEM] + [VMEM] * 3 + [ANY], ANY, [hal...]
  transfers between devices with their start and end apart: 7 -> 7, of which waited for: 2 -> 2; matrix products, arithmetic and copies ran while one was open for 0% -> 0% of each run, Pallas kernels for 16% -> 10%
where the time goes in v3:
time: 57.2 us; the launch traced here: 57 us
  blocking collectives  26.7 us (47%)
  waiting for transfers between devices  10.5 us (18%)
  Pallas kernels  10.1 us (18%)
  starting transfers between devices  7.2 us (13%)
  local copies, waits for them, and re-layouts  2.29 us (4%)
    all_to_all x1, blocking collectives, shards(): lax.all_to_all(packed, ZY, split_axis=0, concat_axis=0, tiled=True)  26.7 us
    ppermute x5, waiting for transfers between devices, shift(): return lax.ppermute(value, 'kc', [(i, (i + by) % 4) for i in range(4)])  10.5 us
    ppermute x5, starting transfers between devices, shift(): return lax.ppermute(value, 'kc', [(i, (i + by) % 4) for i in range(4)])  6.69 us
    pallas_call x1, Pallas kernels, shards(): call(middle_kernel, (shape(256, 4096), shape(32, LANES, LANES), shape(64,...  4.28 us
    pallas_call x1, Pallas kernels, shards(): call(far_kernel, shape(256, 4096), [SMEM] + [VMEM] * 3 + [ANY], ANY, [hal...  2.73 us
    unnamed x8, local copies, waits for them, and re-layouts  2.27 us
    pallas_call x1, Pallas kernels, shards(): call(pack_other_kernel, shape(PEERS, 48, LANES), [SMEM] + [VMEM] * 4, VME...  1.52 us
    pallas_call x1, Pallas kernels, shards(): call(pack_own_kernel, shape(PEERS, 48, LANES), [SMEM, VMEM], VMEM, copies...  1.5 us
  transfers between devices with their start and end apart: 7, of which 2 were waited for; matrix products, arithmetic and copies ran while one was open for 0% of the time, Pallas kernels for 10%

profile of v3, /device:TPU:6, one launch (start us, length us, event | category | flops | bytes accessed | tf_op | source)
XLA Modules:
  0.0 57.0 jit_solution(7887858164133886236)
XLA Ops:
  0.0 0.0 collective-permute-start
  0.0 0.5 collective-permute-start.1
  0.5 0.9 %copy-done = bf16[32,2048]{1,0:T(8,128)(2,1)S(1)} copy-done((bf16[32,2048]{1,0:T(8,128)(2,1)S(1)}, bf16[32,2048]{1,0:T(8,128)(2,1)}, u32[]{:S(2)}) %copy-start) | copy-done | bytes 131096
  1.4 0.7 %copy-done.1 = s32[1024]{0:T(1024)S(1)} copy-done((s32[1024]{0:T(1024)S(1)}, s32[1024]{0:T(1024)}, u32[]{:S(2)}) %copy-start.1) | copy-done | bytes 4120
  2.1 1.5 %shard_map.37.half_packed = bf16[32,48,128]{2,1,0:T(8,128)(2,1)S(1)} custom-call(s32[1024]{0:T(1024)S(1)} %copy-done.1, bf16[32,2048]{1,0:T(8,128)(2,1)S(1)} %copy-done), custom_call_target="tpu_custom_call" | custom-call | flops 1000000 | bytes 100000 | tf_op jit(solution)/shard_map/pallas_call | solution.py:241
  3.6 0.0 collective-permute-done.1.coef_other
  3.6 0.0 collective-permute-done.other
  3.6 0.0 copy-start.3
  3.6 0.7 %copy-done.3 = bf16[4,256]{1,0:T(4,128)(2,1)S(1)} copy-done((bf16[4,256]{1,0:T(4,128)(2,1)S(1)}, bf16[4,256]{1,0:T(4,128)(2,1)}, u32[]{:S(2)}) %copy-start.3) | copy-done | bytes 2072
  4.3 1.5 %shard_map.38 = bf16[32,48,128]{2,1,0:T(8,128)(2,1)S(1)} custom-call(s32[1024]{0:T(1024)S(1)} %copy-done.1, bf16[32,2048]{1,0:T(8,128)(2,1)S(1)} %collective-permute-done.other, bf16[4,256]{1,0:T(4,128)(2,1)S(1)} %copy-done.3, bf16[4,256]{1,0:T(4,128)(2,1)S(1)} %collective-permute-done.1.coef_other, ...), custom_call_target="tpu_custom_call", output_to_operand_aliasing={{}: (4, {})} | custom-call | flops 1000000 | bytes 100000 | tf_op jit(solution)/shard_map/pallas_call | solution.py:244
  5.8 26.7 %all_to_all.5.received = bf16[32,48,128]{2,1,0:T(8,128)(2,1)S(1)} all-to-all(bf16[32,48,128]{2,1,0:T(8,128)(2,1)S(1)} %shard_map.38), channel_id=1, replica_groups=mesh['kf_0'=8,'kf_1'=4,'kf_2'=2,'kc'=4] {'kf_0','kf_1'}, dimensions={0} | all-to-all | bytes 786432 | tf_op jit(solution)/shard_map/all_to_all | solution.py:247
  32.6 0.1 shard_map.39
  32.7 0.9 %collective-permute-start.4 = (bf16[73,16,128]{2,1,0:T(8,128)(2,1)S(1)}, bf16[73,16,128]{2,1,0:T(8,128)(2,1)S(1)}, u32[]{:S(2)}, u32[]{:S(2)}) collective-permute-start(bf16[73,16,128]{2,1,0:T(8,128)(2,1)S(1)} %get-tuple-element.12), channel_id=1, source_target_pairs={{0,3},{1,0},{2,1},{3,2},{4,7},{5,4},{6,5},{7,6},{8,11},{9,8},{10,9... | collective-permute-start | bytes 897032 | tf_op jit(solution)/shard_map/ppermute | solution.py:230
  33.6 2.4 %collective-permute-start.2 = (bf16[73,16,128]{2,1,0:T(8,128)(2,1)S(1)}, bf16[73,16,128]{2,1,0:T(8,128)(2,1)S(1)}, u32[]{:S(2)}, u32[]{:S(2)}) collective-permute-start(bf16[73,16,128]{2,1,0:T(8,128)(2,1)S(1)} %get-tuple-element.11.mine), channel_id=1, source_target_pairs={{0,1},{1,2},{2,3},{3,0},{4,5},{5,6},{6,7},{7,4},{8,9},{9,10},{10,1... | collective-permute-start | bytes 897032 | tf_op jit(solution)/shard_map/ppermute | solution.py:230
  36.0 5.0 %collective-permute-done.4.right = bf16[73,16,128]{2,1,0:T(8,128)(2,1)S(1)} collective-permute-done((bf16[73,16,128]{2,1,0:T(8,128)(2,1)S(1)}, bf16[73,16,128]{2,1,0:T(8,128)(2,1)S(1)}, u32[]{:S(2)}, u32[]{:S(2)}) %collective-permute-start.4) | collective-permute-done | bytes 299040 | tf_op jit(solution)/shard_map/ppermute | solution.py:230
  41.0 0.1 collective-permute-start.5
  41.1 0.0 collective-permute-done.2.left
  41.1 3.3 %collective-permute-start.3 = (bf16[32,16,128]{2,1,0:T(8,128)(2,1)S(1)}, bf16[32,16,128]{2,1,0:T(8,128)(2,1)S(1)}, u32[]{:S(2)}, u32[]{:S(2)}) collective-permute-start(bf16[32,16,128]{2,1,0:T(8,128)(2,1)S(1)} %slice.8), channel_id=1, source_target_pairs={{0,1},{1,2},{2,3},{3,0},{4,5},{5,6},{6,7},{7,4},{8,9},{9,10},{10,1... | collective-permute-start | bytes 393224 | tf_op jit(solution)/shard_map/ppermute | solution.py:230
  44.4 0.0 collective-permute-start.6
  44.4 5.5 %collective-permute-done.6.far_coef = bf16[9,16,128]{2,1,0:T(8,128)(2,1)S(1)} collective-permute-done((bf16[9,16,128]{2,1,0:T(8,128)(2,1)S(1)}, bf16[9,16,128]{2,1,0:T(8,128)(2,1)S(1)}, u32[]{:S(2)}, u32[]{:S(2)}) %collective-permute-start.6) | collective-permute-done | bytes 36896 | tf_op jit(solution)/shard_map/ppermute | solution.py:230
  49.9 4.3 %shard_map.40 = (bf16[256,4096]{1,0:T(8,128)(2,1)}, bf16[32,128,128]{2,1,0:T(8,128)(2,1)S(1)}, bf16[64,128]{1,0:T(8,128)(2,1)S(1)}) custom-call(s32[1024]{0:T(1024)S(1)} %copy-done.2, bf16[32,48,128]{2,1,0:T(8,128)(2,1)S(1)} %all_to_all.5.received, bf16[73,16,128]{2,1,0:T(8,128)(2,1)S(1)} %get-tuple-element.11.mine, ...), custom_call_target="tpu_custom_call" | custom-call | flops 8000000 | bytes 800000 | tf_op jit(solution)/shard_map/pallas_call | solution.py:257
  54.2 0.0 collective-permute-done.5
  54.2 0.0 collective-permute-done.3
  54.2 2.7 %shard_map.41 = bf16[256,4096]{1,0:T(8,128)(2,1)} custom-call(s32[1024]{0:T(1024)S(1)} %copy-done.2, bf16[64,16,128]{2,1,0:T(8,128)(2,1)S(1)} %pad_maximum_fusion.far, bf16[32,128,128]{2,1,0:T(8,128)(2,1)S(1)} %get-tuple-element.14.cols, bf16[64,128]{1,0:T(8,128)(2,1)S(1)} %get-tuple-element.15.turn_far, ...), custom_call_target="tpu_custom_call", output_to_operand_aliasing={{}: (4, {})} | custom-call | flops 3000000 | bytes 300000 | tf_op jit(solution)/shard_map/pallas_call | solution.py:274
  (7 shorter events, 0.1 us)
Async XLA Ops:
  0.0 3.6 %collective-permute-start = (bf16[32,2048]{1,0:T(8,128)(2,1)}, bf16[32,2048]{1,0:T(8,128)(2,1)S(1)}, u32[]{:S(2)}, u32[]{:S(2)}) collective-permute-start(bf16[32,2048]{1,0:T(8,128)(2,1)} %own.1), channel_id=1, source_target_pairs={{0,4},{4,0},{1,5},{5,1},{2,6},{6,2},{3,7},{7,3},{8,12},{12,8},{9,1... | collective-permute-start | bytes 393224 | tf_op jit(solution)/shard_map/ppermute | solution.py:234
  0.0 3.6 %collective-permute-start.1 = (bf16[4,256]{1,0:T(4,128)(2,1)}, bf16[4,256]{1,0:T(4,128)(2,1)S(1)}, u32[]{:S(2)}, u32[]{:S(2)}) collective-permute-start(bf16[4,256]{1,0:T(4,128)(2,1)} %coef_own.3), channel_id=1, source_target_pairs={{0,4},{4,0},{1,5},{5,1},{2,6},{6,2},{3,7},{7,3},{8,12},{12,8},{9,1... | collective-permute-start | bytes 6152 | tf_op jit(solution)/shard_map/ppermute | solution.py:234
  0.5 0.9 %copy-start = (bf16[32,2048]{1,0:T(8,128)(2,1)S(1)}, bf16[32,2048]{1,0:T(8,128)(2,1)}, u32[]{:S(2)}) copy-start(bf16[32,2048]{1,0:T(8,128)(2,1)} %own.1) | copy-start | bytes 393220
  1.4 0.7 %copy-start.1 = (s32[1024]{0:T(1024)S(1)}, s32[1024]{0:T(1024)}, u32[]{:S(2)}) copy-start(s32[1024]{0:T(1024)} %near.7) | copy-start | bytes 12292
  2.1 47.8 %copy-start.2 = (s32[1024]{0:T(1024)S(1)}, s32[1024]{0:T(1024)}, u32[]{:S(2)}) copy-start(s32[1024]{0:T(1024)} %near.7) | copy-start | bytes 12292
  3.6 0.7 %copy-start.3 = (bf16[4,256]{1,0:T(4,128)(2,1)S(1)}, bf16[4,256]{1,0:T(4,128)(2,1)}, u32[]{:S(2)}) copy-start(bf16[4,256]{1,0:T(4,128)(2,1)} %coef_own.3) | copy-start | bytes 6148
  32.7 8.3 %collective-permute-start.4 = (bf16[73,16,128]{2,1,0:T(8,128)(2,1)S(1)}, bf16[73,16,128]{2,1,0:T(8,128)(2,1)S(1)}, u32[]{:S(2)}, u32[]{:S(2)}) collective-permute-start(bf16[73,16,128]{2,1,0:T(8,128)(2,1)S(1)} %get-tuple-element.12), channel_id=1, source_target_pairs={{0,3},{1,0},{2,1},{3,2},{4,7},{5,4},{6,5},{7,6},{8,11},{9,8},{10,9... | collective-permute-start | bytes 897032 | tf_op jit(solution)/shard_map/ppermute | solution.py:230
  33.6 7.5 %collective-permute-start.2 = (bf16[73,16,128]{2,1,0:T(8,128)(2,1)S(1)}, bf16[73,16,128]{2,1,0:T(8,128)(2,1)S(1)}, u32[]{:S(2)}, u32[]{:S(2)}) collective-permute-start(bf16[73,16,128]{2,1,0:T(8,128)(2,1)S(1)} %get-tuple-element.11.mine), channel_id=1, source_target_pairs={{0,1},{1,2},{2,3},{3,0},{4,5},{5,6},{6,7},{7,4},{8,9},{9,10},{10,1... | collective-permute-start | bytes 897032 | tf_op jit(solution)/shard_map/ppermute | solution.py:230
  41.0 13.2 %collective-permute-start.5 = (bf16[32,16,128]{2,1,0:T(8,128)(2,1)S(1)}, bf16[32,16,128]{2,1,0:T(8,128)(2,1)S(1)}, u32[]{:S(2)}, u32[]{:S(2)}) collective-permute-start(bf16[32,16,128]{2,1,0:T(8,128)(2,1)S(1)} %slice.9), channel_id=1, source_target_pairs={{0,3},{1,0},{2,1},{3,2},{4,7},{5,4},{6,5},{7,6},{8,11},{9,8},{10,9... | collective-permute-start | bytes 393224 | tf_op jit(solution)/shard_map/ppermute | solution.py:230
  41.1 13.1 %collective-permute-start.3 = (bf16[32,16,128]{2,1,0:T(8,128)(2,1)S(1)}, bf16[32,16,128]{2,1,0:T(8,128)(2,1)S(1)}, u32[]{:S(2)}, u32[]{:S(2)}) collective-permute-start(bf16[32,16,128]{2,1,0:T(8,128)(2,1)S(1)} %slice.8), channel_id=1, source_target_pairs={{0,1},{1,2},{2,3},{3,0},{4,5},{5,6},{6,7},{7,4},{8,9},{9,10},{10,1... | collective-permute-start | bytes 393224 | tf_op jit(solution)/shard_map/ppermute | solution.py:230
  44.4 5.5 %collective-permute-start.6 = (bf16[9,16,128]{2,1,0:T(8,128)(2,1)S(1)}, bf16[9,16,128]{2,1,0:T(8,128)(2,1)S(1)}, u32[]{:S(2)}, u32[]{:S(2)}) collective-permute-start(bf16[9,16,128]{2,1,0:T(8,128)(2,1)S(1)} %get-tuple-element.13), channel_id=1, source_target_pairs={{0,2},{1,3},{2,0},{3,1},{4,6},{5,7},{6,4},{7,5},{8,10},{9,11},{10,... | collective-permute-start | bytes 110600 | tf_op jit(solution)/shard_map/ppermute | solution.py:230

commit v4 on v3

--- a/solution.py
+++ b/solution.py
@@ -29,38 +29,23 @@
     return lax.dot_general(a, b, (((1,), (1,)), ((), ())), preferred_element_type=F32)
 
 
-def pack_rows(near, rows, out, copies, at_row):
-    kc = lax.axis_index("kc")
-    core = lax.axis_index("kf_2")
+def turn_rows(rows, copies):
     for b in range(16):
         block = rows[:, b * LANES : (b + 1) * LANES].astype(F32)
         for s in range(8):
             turned = pltpu.roll(block, s * PAIRS, 1) if s else block
             copies[s, b] = turned.astype(BF16)
-    group = iota((PAIRS, LANES), 1) // PAIRS
-    base = 16 * core + 4 * kc
-
-    def body(d, carry):
-        tile = None
-        for j in range(POINTS):
-            c = near[32 * d + base + j]
-            for lo in range(2):
-                at = lo * POINTS + j
-                piece = copies[(at - c) & 7, c >> 3, lo * PAIRS : (lo + 1) * PAIRS, :]
-                tile = piece if tile is None else jnp.where(group == at, piece, tile)
-        out[d, pl.ds(at_row, PAIRS), :] = tile
-        return carry
-
-    lax.fori_loop(0, PEERS, body, 0, unroll=4)
-
-
-def pack_own_kernel(near, own, out, copies):
-    pack_rows(near, own, out, copies, pl.multiple_of(lax.axis_index("kf_2") * PAIRS, PAIRS))
-
-
-def pack_other_kernel(near, other, coef_own, coef_other, half_packed, out, copies):
+
+
+def own_kernel(own, near, coef_own, copies):
+    turn_rows(own, copies)
+
+
+def pack_kernel(near, own_copies, other, coef_own, coef_other, out, other_copies):
+    kc = lax.axis_index("kc")
     core = lax.axis_index("kf_2")
-    pack_rows(near, other, out, copies, pl.multiple_of((1 - core) * PAIRS, PAIRS))
+    turn_rows(other, other_copies)
+    copies = (own_copies, other_copies)
     a = coef_own[...].astype(F32)
     o = coef_other[...].astype(F32)
     first = jnp.where(core == 0, a, o)
@@ -68,21 +53,40 @@
     coef = jnp.concatenate(
         [first[:, :LANES], first[:, LANES:], second[:, :LANES], second[:, LANES:]], axis=0
     ).astype(BF16)
-    for d in range(PEERS):
+    group = iota((PAIRS, LANES), 1) // PAIRS
+    base = 16 * core + 4 * kc
+
+    def body(d, carry):
+        tiles = [None, None]
+        for j in range(POINTS):
+            c = near[32 * d + base + j]
+            for lo in range(2):
+                at = lo * POINTS + j
+                for n in range(2):
+                    piece = copies[n][(at - c) & 7, c >> 3, lo * PAIRS : (lo + 1) * PAIRS, :]
+                    tiles[n] = piece if tiles[n] is None else jnp.where(group == at, piece, tiles[n])
+        out[d, pl.ds(pl.multiple_of(core * PAIRS, PAIRS), PAIRS), :] = tiles[0]
+        out[d, pl.ds(pl.multiple_of((1 - core) * PAIRS, PAIRS), PAIRS), :] = tiles[1]
         out[d, 2 * PAIRS :, :] = coef
-
-
-def split_kernel(received, coef_own, up, down, across):
+        return carry
+
+    lax.fori_loop(0, PEERS, body, 0, unroll=4)
+
+
+def split_kernel(received, coef_own, up_1, up_2, down_1, down_2, across):
     kc = lax.axis_index("kc")
     mine = coef_own[...].astype(F32)
     mine = jnp.concatenate([mine[:, :LANES], mine[:, LANES:]], axis=0)
     mine = jnp.concatenate([mine, jnp.zeros_like(mine)], axis=0).astype(BF16)
-    for zy in range(PEERS):
-        for h in range(2):
-            block = received[zy, h * PAIRS : (h + 1) * PAIRS, :]
-            up[2 * zy + h] = block
-            down[2 * zy + h] = block
-    for step, target, at in ((1, up, 64), (3, down, 64), (2, across, 0)):
+    for n in range(64):
+        block = received[n // 2, n % 2 * PAIRS : (n % 2 + 1) * PAIRS, :]
+        if n < 32:
+            up_1[n] = block
+            down_2[n] = block
+        else:
+            up_2[n - 32] = block
+            down_1[n - 32] = block
+    for step, target, at in ((1, up_2, 32), (3, down_2, 32), (2, across, 0)):
         first = (kc + step) % 4 * 8
         for p in range(8):
             target[at + p] = received[first + p, 2 * PAIRS :, :]
@@ -114,11 +118,16 @@
         c = near[first + i]
         keep = halves[c & 1]
         for n, blocks in enumerate(sources):
-            picked[n, i * PAIRS : (i + 1) * PAIRS, :] = blocks[c >> 1] * keep
+            if blocks.shape[0] == PEERS:
+                block = blocks[c >> 2, pl.ds(pl.multiple_of((c >> 1 & 1) * PAIRS, PAIRS), PAIRS), :]
+            else:
+                block = blocks[c >> 1]
+            picked[n, i * PAIRS : (i + 1) * PAIRS, :] = block * keep
 
 
 def middle_kernel(
-    near, received, mine, left, right, far_coef, out, cols, turn_far, pieces, turns, halves, diag, picked, turned, result, sem
+    near, received, coef_own, left, left_coef, right, right_coef, far_coef, out, cols, turn_far,
+    pieces, turns, halves, diag, picked, turned, result, sem
 ):
     kc = lax.axis_index("kc")
     set_halves(halves)
@@ -127,12 +136,14 @@
     diag[...] = jnp.where(same, 1.0, 0.0).astype(BF16)
     for p in range(8):
         pieces[kc, p] = received[kc * 8 + p, 2 * PAIRS :, :].astype(F32)
-        pieces[(kc + 3) % 4, p] = left[64 + p].astype(F32)
-        pieces[(kc + 1) % 4, p] = right[64 + p].astype(F32)
+        pieces[(kc + 3) % 4, p] = left_coef[32 + p].astype(F32)
+        pieces[(kc + 1) % 4, p] = right_coef[32 + p].astype(F32)
         pieces[(kc + 2) % 4, p] = far_coef[p].astype(F32)
     own_group = iota((64, LANES), 1) // PAIRS % POINTS == iota((64, LANES), 0) // PAIRS
-    for n, row in enumerate((mine[72], left[72], right[72], far_coef[8])):
-        row = row.astype(F32)
+    own_rows = coef_own[...].astype(F32)
+    rows = [jnp.concatenate([own_rows[:, :LANES], own_rows[:, LANES:]], axis=0)]
+    rows += [ref[at].astype(F32) for ref, at in ((left_coef, 40), (right_coef, 40), (far_coef, 8))]
+    for n, row in enumerate(rows):
         wide = jnp.dot(
             spread(lambda p, half: row[half * POINTS + p : half * POINTS + p + 1], POINTS),
             repeat,
@@ -161,7 +172,7 @@
             cols[4 * v + s] = wide.astype(BF16) * diag[...]
 
     def turn(v):
-        pick_points(near, halves, 256 * kc + 32 * v, (mine, left, right), picked)
+        pick_points(near, halves, 256 * kc + 32 * v, (received, left, right), picked)
         for n in range(3):
             turned[n * 64 : (n + 1) * 64, v * 512 : (v + 1) * 512] = dot_t(turns[n], picked[n]).astype(BF16)
 
@@ -237,27 +248,32 @@
 def shards(kernel_coarse, coefficients, nearest):
     other = partner(kernel_coarse)
     coef_other = partner(coefficients)
-    copies = [pltpu.VMEM((8, 16, 32, LANES), BF16)]
-    packed = call(pack_own_kernel, shape(PEERS, 48, LANES), [SMEM, VMEM], VMEM, copies, 1000000)(
-        nearest, kernel_coarse
-    )
+    rotations = (8, 16, 32, LANES)
+    own_copies = call(own_kernel, shape(*rotations), [VMEM] * 3, VMEM, [], 1000000)(kernel_coarse, nearest, coefficients)
     packed = call(
-        pack_other_kernel, shape(PEERS, 48, LANES), [SMEM] + [VMEM] * 4, VMEM, copies, 1000000, {4: 0}
-    )(nearest, other, coefficients, coef_other, packed)
+        pack_kernel, shape(PEERS, 48, LANES), [SMEM] + [VMEM] * 4, VMEM, [pltpu.VMEM(rotations, BF16)], 1000000
+    )(nearest, own_copies, other, coefficients, coef_other)
     received = lax.all_to_all(packed, ZY, split_axis=0, concat_axis=0, tiled=True)
     block = (PAIRS, LANES)
-    up, down, across = call(
-        split_kernel, (shape(73, *block), shape(73, *block), shape(9, *block)), [VMEM, VMEM], (VMEM,) * 3, [], 100000
+    sizes = (32, 41, 32, 41, 9)
+    up_1, up_2, down_1, down_2, across = call(
+        split_kernel, tuple(shape(n, *block) for n in sizes), [VMEM, VMEM], (VMEM,) * 5, [], 100000
     )(received, coefficients)
+    left_1 = shift(up_1, 1)
+    right_1 = shift(down_1, -1)
     far_coef = shift(across, 2)
-    left = shift(up, 1)
-    right = shift(down, -1)
-    far = jnp.concatenate([shift(left[:PEERS], 1), shift(right[PEERS:64], -1)], axis=0)
+    left_2 = shift(up_2, 1)
+    right_2 = shift(down_2, -1)
+    far_1 = shift(left_1, 1)
+    far_2 = shift(right_1, -1)
+    left = jnp.concatenate([left_1, left_2[:32]], axis=0)
+    right = jnp.concatenate([right_2[:32], right_1], axis=0)
+    far = jnp.concatenate([far_1, far_2], axis=0)
     half_masks = pltpu.VMEM((2, *block), BF16)
     partial, cols, turn_far = call(
         middle_kernel,
         (shape(256, 4096), shape(32, LANES, LANES), shape(64, LANES)),
-        [SMEM] + [VMEM] * 5,
+        [SMEM] + [VMEM] * 7,
         (ANY, VMEM, VMEM),
         [
             pltpu.VMEM((4, 8, *block), F32),
@@ -270,7 +286,7 @@
             pltpu.SemaphoreType.DMA((3, 4)),
         ],
         8000000,
-    )(nearest, received, up, left, right, far_coef)
+    )(nearest, received, coefficients, left, left_2, right, right_2, far_coef)
     return call(
         far_kernel,
         shape(256, 4096),

time: 57.2 us -> 50.9 us (0.89)
  waiting for transfers between devices: 10.5 us -> 2.96 us
  starting transfers between devices: 7.2 us -> 9.28 us
  Pallas kernels: 10.1 us -> 9.25 us
    ppermute x5 -> x7, waiting for transfers between devices: 10.5 us -> 2.96 us  [shift(): return lax.ppermute(value, 'kc', [(i, (i + by) % 4) for i in range(4)])]
    ppermute x5 -> x7, starting transfers between devices: 6.69 us -> 8.77 us  [shift(): return lax.ppermute(value, 'kc', [(i, (i + by) % 4) for i in range(4)])]
    pallas_call x3, Pallas kernels: 3.09 us -> 2.06 us  [the longest x1 1.67 us: shards(): call(pack_kernel, shape(PEERS, 48, LANES), [SMEM] + [VMEM] * 4, VMEM, [pl...]
    unnamed x8 -> x10, local copies, waits for them, and re-layouts: 2.27 us -> 2.28 us
  transfers between devices with their start and end apart: 7 -> 9, of which waited for: 2 -> 3; matrix products, arithmetic and copies ran while one was open for 0% -> 0% of each run, Pallas kernels for 10% -> 9%
where the time goes in v4:
time: 50.9 us; the launch traced here: 50.7 us
  blocking collectives  26.7 us (52%)
  starting transfers between devices  9.28 us (18%)
  Pallas kernels  9.25 us (18%)
  waiting for transfers between devices  2.96 us (6%)
  local copies, waits for them, and re-layouts  2.3 us (5%)
    all_to_all x1, blocking collectives, shards(): lax.all_to_all(packed, ZY, split_axis=0, concat_axis=0, tiled=True)  26.7 us
    ppermute x7, starting transfers between devices, shift(): return lax.ppermute(value, 'kc', [(i, (i + by) % 4) for i in range(4)])  8.77 us
    pallas_call x1, Pallas kernels, shards(): call(middle_kernel, (shape(256, 4096), shape(32, LANES, LANES), shape(64,...  4.46 us
    ppermute x7, waiting for transfers between devices, shift(): return lax.ppermute(value, 'kc', [(i, (i + by) % 4) for i in range(4)])  2.96 us
    pallas_call x1, Pallas kernels, shards(): call(far_kernel, shape(256, 4096), [SMEM] + [VMEM] * 3 + [ANY], ANY, [hal...  2.73 us
    unnamed x10, local copies, waits for them, and re-layouts  2.28 us
    pallas_call x1, Pallas kernels, shards(): call(pack_kernel, shape(PEERS, 48, LANES), [SMEM] + [VMEM] * 4, VMEM, [pl...  1.67 us
  transfers between devices with their start and end apart: 9, of which 3 were waited for; matrix products, arithmetic and copies ran while one was open for 0% of the time, Pallas kernels for 9%

profile of v4, /device:TPU:6, one launch (start us, length us, event | category | flops | bytes accessed | tf_op | source)
XLA Modules:
  0.0 50.7 jit_solution(1324637177536214882)
XLA Ops:
  0.0 0.5 collective-permute-start.1
  0.5 0.9 %copy-done = bf16[32,2048]{1,0:T(8,128)(2,1)S(1)} copy-done((bf16[32,2048]{1,0:T(8,128)(2,1)S(1)}, bf16[32,2048]{1,0:T(8,128)(2,1)}, u32[]{:S(2)}) %copy-start) | copy-done | bytes 131096
  1.4 0.7 %copy-done.1 = s32[1024]{0:T(1024)S(1)} copy-done((s32[1024]{0:T(1024)S(1)}, s32[1024]{0:T(1024)}, u32[]{:S(2)}) %copy-start.1) | copy-done | bytes 4120
  2.1 0.7 %copy-done.3 = bf16[4,256]{1,0:T(4,128)(2,1)S(1)} copy-done((bf16[4,256]{1,0:T(4,128)(2,1)S(1)}, bf16[4,256]{1,0:T(4,128)(2,1)}, u32[]{:S(2)}) %copy-start.3) | copy-done | bytes 2072
  2.8 0.3 shard_map.37.own_copies
  3.1 0.0 copy-start.2
  3.1 0.0 copy-start.4
  3.1 1.7 %shard_map.38 = bf16[32,48,128]{2,1,0:T(8,128)(2,1)S(1)} custom-call(s32[1024]{0:T(1024)S(1)} %copy-done.1, bf16[8,16,32,128]{3,2,1,0:T(8,128)(2,1)S(1)} %shard_map.37.own_copies, bf16[32,2048]{1,0:T(8,128)(2,1)S(1)} %collective-permute-done.other, bf16[4,256]{1,0:T(4,128)(2,1)S(1)} %copy-done.3, bf16[4,256]{1,0:T(4,128)(2,1)S(1)} %collective-permute-done.1.coef_other), custom_call_target="tpu_custom_call" | custom-call | flops 1000000 | bytes 100000 | tf_op jit(solution)/shard_map/pallas_call | solution.py:253
  4.8 26.7 %all_to_all.5.received = bf16[32,48,128]{2,1,0:T(8,128)(2,1)S(1)} all-to-all(bf16[32,48,128]{2,1,0:T(8,128)(2,1)S(1)} %shard_map.38), channel_id=1, replica_groups=mesh['kf_0'=8,'kf_1'=4,'kf_2'=2,'kc'=4] {'kf_0','kf_1'}, dimensions={0} | all-to-all | bytes 786432 | tf_op jit(solution)/shard_map/all_to_all | solution.py:256
  31.6 0.1 shard_map.39
  31.7 0.6 %collective-permute-start.6 = (bf16[41,16,128]{2,1,0:T(8,128)(2,1)S(1)}, bf16[41,16,128]{2,1,0:T(8,128)(2,1)S(1)}, u32[]{:S(2)}, u32[]{:S(2)}) collective-permute-start(bf16[41,16,128]{2,1,0:T(8,128)(2,1)S(1)} %get-tuple-element.15), channel_id=1, source_target_pairs={{0,1},{1,2},{2,3},{3,0},{4,5},{5,6},{6,7},{7,4},{8,9},{9,10},{10,1... | collective-permute-start | bytes 503816 | tf_op jit(solution)/shard_map/ppermute | solution.py:241
  32.2 1.5 %collective-permute-start.2 = (bf16[32,16,128]{2,1,0:T(8,128)(2,1)S(1)}, bf16[32,16,128]{2,1,0:T(8,128)(2,1)S(1)}, u32[]{:S(2)}, u32[]{:S(2)}) collective-permute-start(bf16[32,16,128]{2,1,0:T(8,128)(2,1)S(1)} %get-tuple-element.13), channel_id=1, source_target_pairs={{0,1},{1,2},{2,3},{3,0},{4,5},{5,6},{6,7},{7,4},{8,9},{9,10},{10,1... | collective-permute-start | bytes 393224 | tf_op jit(solution)/shard_map/ppermute | solution.py:241
  33.7 0.5 %collective-permute-start.4 = (bf16[32,16,128]{2,1,0:T(8,128)(2,1)S(1)}, bf16[32,16,128]{2,1,0:T(8,128)(2,1)S(1)}, u32[]{:S(2)}, u32[]{:S(2)}) collective-permute-start(bf16[32,16,128]{2,1,0:T(8,128)(2,1)S(1)} %get-tuple-element.14), channel_id=1, source_target_pairs={{0,3},{1,0},{2,1},{3,2},{4,7},{5,4},{6,5},{7,6},{8,11},{9,8},{10,9... | collective-permute-start | bytes 393224 | tf_op jit(solution)/shard_map/ppermute | solution.py:241
  34.2 1.5 %collective-permute-start.7 = (bf16[41,16,128]{2,1,0:T(8,128)(2,1)S(1)}, bf16[41,16,128]{2,1,0:T(8,128)(2,1)S(1)}, u32[]{:S(2)}, u32[]{:S(2)}) collective-permute-start(bf16[41,16,128]{2,1,0:T(8,128)(2,1)S(1)} %get-tuple-element.16), channel_id=1, source_target_pairs={{0,3},{1,0},{2,1},{3,2},{4,7},{5,4},{6,5},{7,6},{8,11},{9,8},{10,9... | collective-permute-start | bytes 503816 | tf_op jit(solution)/shard_map/ppermute | solution.py:241
  35.8 2.6 %collective-permute-start.8 = (bf16[9,16,128]{2,1,0:T(8,128)(2,1)S(1)}, bf16[9,16,128]{2,1,0:T(8,128)(2,1)S(1)}, u32[]{:S(2)}, u32[]{:S(2)}) collective-permute-start(bf16[9,16,128]{2,1,0:T(8,128)(2,1)S(1)} %get-tuple-element.17), channel_id=1, source_target_pairs={{0,2},{1,3},{2,0},{3,1},{4,6},{5,7},{6,4},{7,5},{8,10},{9,11},{10,... | collective-permute-start | bytes 110600 | tf_op jit(solution)/shard_map/ppermute | solution.py:241
  38.4 1.4 %collective-permute-done.2 = bf16[32,16,128]{2,1,0:T(8,128)(2,1)S(1)} collective-permute-done((bf16[32,16,128]{2,1,0:T(8,128)(2,1)S(1)}, bf16[32,16,128]{2,1,0:T(8,128)(2,1)S(1)}, u32[]{:S(2)}, u32[]{:S(2)}) %collective-permute-start.2) | collective-permute-done | bytes 131104 | tf_op jit(solution)/shard_map/ppermute | solution.py:241
  39.8 1.1 %collective-permute-start.3 = (bf16[32,16,128]{2,1,0:T(8,128)(2,1)S(1)}, bf16[32,16,128]{2,1,0:T(8,128)(2,1)S(1)}, u32[]{:S(2)}, u32[]{:S(2)}) collective-permute-start(bf16[32,16,128]{2,1,0:T(8,128)(2,1)S(1)} %collective-permute-done.2), channel_id=1, source_target_pairs={{0,1},{1,2},{2,3},{3,0},{4,5},{5,6},{6,7},{7,4},{8,9},{9,10},{10,1... | collective-permute-start | bytes 393224 | tf_op jit(solution)/shard_map/ppermute | solution.py:241
  40.9 0.0 collective-permute-done.4
  40.9 0.9 %collective-permute-start.5 = (bf16[32,16,128]{2,1,0:T(8,128)(2,1)S(1)}, bf16[32,16,128]{2,1,0:T(8,128)(2,1)S(1)}, u32[]{:S(2)}, u32[]{:S(2)}) collective-permute-start(bf16[32,16,128]{2,1,0:T(8,128)(2,1)S(1)} %collective-permute-done.4), channel_id=1, source_target_pairs={{0,3},{1,0},{2,1},{3,2},{4,7},{5,4},{6,5},{7,6},{8,11},{9,8},{10,9... | collective-permute-start | bytes 393224 | tf_op jit(solution)/shard_map/ppermute | solution.py:241
  41.8 0.0 collective-permute-done.6.left_coef
  41.9 0.5 %collective-permute-done.7.right_coef = bf16[41,16,128]{2,1,0:T(8,128)(2,1)S(1)} collective-permute-done((bf16[41,16,128]{2,1,0:T(8,128)(2,1)S(1)}, bf16[41,16,128]{2,1,0:T(8,128)(2,1)S(1)}, u32[]{:S(2)}, u32[]{:S(2)}) %collective-permute-start.7) | collective-permute-done | bytes 167968 | tf_op jit(solution)/shard_map/ppermute | solution.py:241
  42.4 1.0 %collective-permute-done.8.far_coef = bf16[9,16,128]{2,1,0:T(8,128)(2,1)S(1)} collective-permute-done((bf16[9,16,128]{2,1,0:T(8,128)(2,1)S(1)}, bf16[9,16,128]{2,1,0:T(8,128)(2,1)S(1)}, u32[]{:S(2)}, u32[]{:S(2)}) %collective-permute-start.8) | collective-permute-done | bytes 36896 | tf_op jit(solution)/shard_map/ppermute | solution.py:241
  43.5 4.5 %shard_map.40 = (bf16[256,4096]{1,0:T(8,128)(2,1)}, bf16[32,128,128]{2,1,0:T(8,128)(2,1)S(1)}, bf16[64,128]{1,0:T(8,128)(2,1)S(1)}) custom-call(s32[1024]{0:T(1024)S(1)} %copy-done.2, bf16[32,48,128]{2,1,0:T(8,128)(2,1)S(1)} %all_to_all.5.received, bf16[4,256]{1,0:T(4,128)(2,1)S(1)} %copy-done.4, bf16[64,16,128]{2,1,0:T(8,128)(2,1)S(1)} %pad_maximum_fusion.1.left, ...), custom_call_target="tpu_custom_call" | custom-call | flops 8000000 | bytes 800000 | tf_op jit(solution)/shard_map/pallas_call | solution.py:273
  48.0 2.7 %shard_map.41 = bf16[256,4096]{1,0:T(8,128)(2,1)} custom-call(s32[1024]{0:T(1024)S(1)} %copy-done.2, bf16[64,16,128]{2,1,0:T(8,128)(2,1)S(1)} %pad_maximum_fusion.far, bf16[32,128,128]{2,1,0:T(8,128)(2,1)S(1)} %get-tuple-element.18.cols, bf16[64,128]{1,0:T(8,128)(2,1)S(1)} %get-tuple-element.19.turn_far, ...), custom_call_target="tpu_custom_call", output_to_operand_aliasing={{}: (4, {})} | custom-call | flops 3000000 | bytes 300000 | tf_op jit(solution)/shard_map/pallas_call | solution.py:290
  (15 shorter events, 0.1 us)
Async XLA Ops:
  0.0 3.1 %collective-permute-start = (bf16[32,2048]{1,0:T(8,128)(2,1)}, bf16[32,2048]{1,0:T(8,128)(2,1)S(1)}, u32[]{:S(2)}, u32[]{:S(2)}) collective-permute-start(bf16[32,2048]{1,0:T(8,128)(2,1)} %own.1), channel_id=1, source_target_pairs={{0,4},{4,0},{1,5},{5,1},{2,6},{6,2},{3,7},{7,3},{8,12},{12,8},{9,1... | collective-permute-start | bytes 393224 | tf_op jit(solution)/shard_map/ppermute | solution.py:245
  0.0 3.1 %collective-permute-start.1 = (bf16[4,256]{1,0:T(4,128)(2,1)}, bf16[4,256]{1,0:T(4,128)(2,1)S(1)}, u32[]{:S(2)}, u32[]{:S(2)}) collective-permute-start(bf16[4,256]{1,0:T(4,128)(2,1)} %coef_own.7), channel_id=1, source_target_pairs={{0,4},{4,0},{1,5},{5,1},{2,6},{6,2},{3,7},{7,3},{8,12},{12,8},{9,1... | collective-permute-start | bytes 6152 | tf_op jit(solution)/shard_map/ppermute | solution.py:245
  0.5 0.9 %copy-start = (bf16[32,2048]{1,0:T(8,128)(2,1)S(1)}, bf16[32,2048]{1,0:T(8,128)(2,1)}, u32[]{:S(2)}) copy-start(bf16[32,2048]{1,0:T(8,128)(2,1)} %own.1) | copy-start | bytes 393220
  1.4 0.7 %copy-start.1 = (s32[1024]{0:T(1024)S(1)}, s32[1024]{0:T(1024)}, u32[]{:S(2)}) copy-start(s32[1024]{0:T(1024)} %near.7) | copy-start | bytes 12292
  2.1 0.7 %copy-start.3 = (bf16[4,256]{1,0:T(4,128)(2,1)S(1)}, bf16[4,256]{1,0:T(4,128)(2,1)}, u32[]{:S(2)}) copy-start(bf16[4,256]{1,0:T(4,128)(2,1)} %coef_own.7) | copy-start | bytes 6148
  3.1 40.4 %copy-start.2 = (s32[1024]{0:T(1024)S(1)}, s32[1024]{0:T(1024)}, u32[]{:S(2)}) copy-start(s32[1024]{0:T(1024)} %near.7) | copy-start | bytes 12292
  3.1 40.4 %copy-start.4 = (bf16[4,256]{1,0:T(4,128)(2,1)S(1)}, bf16[4,256]{1,0:T(4,128)(2,1)}, u32[]{:S(2)}) copy-start(bf16[4,256]{1,0:T(4,128)(2,1)} %coef_own.7) | copy-start | bytes 6148
  31.7 10.2 %collective-permute-start.6 = (bf16[41,16,128]{2,1,0:T(8,128)(2,1)S(1)}, bf16[41,16,128]{2,1,0:T(8,128)(2,1)S(1)}, u32[]{:S(2)}, u32[]{:S(2)}) collective-permute-start(bf16[41,16,128]{2,1,0:T(8,128)(2,1)S(1)} %get-tuple-element.15), channel_id=1, source_target_pairs={{0,1},{1,2},{2,3},{3,0},{4,5},{5,6},{6,7},{7,4},{8,9},{9,10},{10,1... | collective-permute-start | bytes 503816 | tf_op jit(solution)/shard_map/ppermute | solution.py:241
  32.2 7.6 %collective-permute-start.2 = (bf16[32,16,128]{2,1,0:T(8,128)(2,1)S(1)}, bf16[32,16,128]{2,1,0:T(8,128)(2,1)S(1)}, u32[]{:S(2)}, u32[]{:S(2)}) collective-permute-start(bf16[32,16,128]{2,1,0:T(8,128)(2,1)S(1)} %get-tuple-element.13), channel_id=1, source_target_pairs={{0,1},{1,2},{2,3},{3,0},{4,5},{5,6},{6,7},{7,4},{8,9},{9,10},{10,1... | collective-permute-start | bytes 393224 | tf_op jit(solution)/shard_map/ppermute | solution.py:241
  33.7 7.2 %collective-permute-start.4 = (bf16[32,16,128]{2,1,0:T(8,128)(2,1)S(1)}, bf16[32,16,128]{2,1,0:T(8,128)(2,1)S(1)}, u32[]{:S(2)}, u32[]{:S(2)}) collective-permute-start(bf16[32,16,128]{2,1,0:T(8,128)(2,1)S(1)} %get-tuple-element.14), channel_id=1, source_target_pairs={{0,3},{1,0},{2,1},{3,2},{4,7},{5,4},{6,5},{7,6},{8,11},{9,8},{10,9... | collective-permute-start | bytes 393224 | tf_op jit(solution)/shard_map/ppermute | solution.py:241
  34.2 8.2 %collective-permute-start.7 = (bf16[41,16,128]{2,1,0:T(8,128)(2,1)S(1)}, bf16[41,16,128]{2,1,0:T(8,128)(2,1)S(1)}, u32[]{:S(2)}, u32[]{:S(2)}) collective-permute-start(bf16[41,16,128]{2,1,0:T(8,128)(2,1)S(1)} %get-tuple-element.16), channel_id=1, source_target_pairs={{0,3},{1,0},{2,1},{3,2},{4,7},{5,4},{6,5},{7,6},{8,11},{9,8},{10,9... | collective-permute-start | bytes 503816 | tf_op jit(solution)/shard_map/ppermute | solution.py:241
  35.8 7.7 %collective-permute-start.8 = (bf16[9,16,128]{2,1,0:T(8,128)(2,1)S(1)}, bf16[9,16,128]{2,1,0:T(8,128)(2,1)S(1)}, u32[]{:S(2)}, u32[]{:S(2)}) collective-permute-start(bf16[9,16,128]{2,1,0:T(8,128)(2,1)S(1)} %get-tuple-element.17), channel_id=1, source_target_pairs={{0,2},{1,3},{2,0},{3,1},{4,6},{5,7},{6,4},{7,5},{8,10},{9,11},{10,... | collective-permute-start | bytes 110600 | tf_op jit(solution)/shard_map/ppermute | solution.py:241
  39.8 8.2 %collective-permute-start.3 = (bf16[32,16,128]{2,1,0:T(8,128)(2,1)S(1)}, bf16[32,16,128]{2,1,0:T(8,128)(2,1)S(1)}, u32[]{:S(2)}, u32[]{:S(2)}) collective-permute-start(bf16[32,16,128]{2,1,0:T(8,128)(2,1)S(1)} %collective-permute-done.2), channel_id=1, source_target_pairs={{0,1},{1,2},{2,3},{3,0},{4,5},{5,6},{6,7},{7,4},{8,9},{9,10},{10,1... | collective-permute-start | bytes 393224 | tf_op jit(solution)/shard_map/ppermute | solution.py:241
  40.9 7.1 %collective-permute-start.5 = (bf16[32,16,128]{2,1,0:T(8,128)(2,1)S(1)}, bf16[32,16,128]{2,1,0:T(8,128)(2,1)S(1)}, u32[]{:S(2)}, u32[]{:S(2)}) collective-permute-start(bf16[32,16,128]{2,1,0:T(8,128)(2,1)S(1)} %collective-permute-done.4), channel_id=1, source_target_pairs={{0,3},{1,0},{2,1},{3,2},{4,7},{5,4},{6,5},{7,6},{8,11},{9,8},{10,9... | collective-permute-start | bytes 393224 | tf_op jit(solution)/shard_map/ppermute | solution.py:241

commit v5 on v4

v5 whole, which is shorter than its diff:
```python
import jax
import jax.numpy as jnp
from jax import lax
from jax.experimental import pallas as pl
from jax.experimental.pallas import tpu as pltpu
from jax.sharding import Mesh
from jax.sharding import PartitionSpec as P


KF = ("kf_0", "kf_1", "kf_2")
ZY = ("kf_0", "kf_1")
KF_KC = ("kf_0", "kf_1", "kf_2", "kc")
LANES = 128
PAIRS = 16
POINTS = 4
PEERS = 32
BF16 = jnp.bfloat16
F32 = jnp.float32
VMEM = pl.BlockSpec(memory_space=pltpu.VMEM)
SMEM = pl.BlockSpec(memory_space=pltpu.SMEM)
ANY = pl.BlockSpec(memory_space=pl.ANY)


def iota(shape, dim):
    return lax.broadcasted_iota(jnp.int32, shape, dim)


def dot_t(a, b):
    return lax.dot_general(a, b, (((1,), (1,)), ((), ())), preferred_element_type=F32)


def turn_rows(rows, copies):
    for b in range(16):
        block = rows[:, b * LANES : (b + 1) * LANES].astype(F32)
        for s in range(8):
            turned = pltpu.roll(block, s * PAIRS, 1) if s else block
            copies[s, b] = turned.astype(BF16)


def own_kernel(own, near, coef_own, copies):
    turn_rows(own, copies)


def pack_kernel(near, own_copies, other, coef_own, coef_other, out, other_copies):
    kc = lax.axis_index("kc")
    core = lax.axis_index("kf_2")
    turn_rows(other, other_copies)
    copies = (own_copies, other_copies)
    a = coef_own[...].astype(F32)
    o = coef_other[...].astype(F32)
    first = jnp.where(core == 0, a, o)
    second = jnp.where(core == 0, o, a)
    coef = jnp.concatenate(
        [first[:, :LANES], first[:, LANES:], second[:, :LANES], second[:, LANES:]], axis=0
    ).astype(BF16)
    group = iota((PAIRS, LANES), 1) // PAIRS
    base = 16 * core + 4 * kc

    def body(d, carry):
        tiles = [None, None]
        for j in range(POINTS):
            c = near[32 * d + base + j]
            for lo in range(2):
                at = lo * POINTS + j
                for n in range(2):
                    piece = copies[n][(at - c) & 7, c >> 3, lo * PAIRS : (lo + 1) * PAIRS, :]
                    tiles[n] = piece if tiles[n] is None else jnp.where(group == at, piece, tiles[n])
        out[d, pl.ds(pl.multiple_of(core * PAIRS, PAIRS), PAIRS), :] = tiles[0]
        out[d, pl.ds(pl.multiple_of((1 - core) * PAIRS, PAIRS), PAIRS), :] = tiles[1]
        out[d, 2 * PAIRS :, :] = coef
        return carry

    lax.fori_loop(0, PEERS, body, 0, unroll=4)


def split_kernel(received, coef_own, up_1, up_2, down_1, down_2, across):
    kc = lax.axis_index("kc")
    mine = halves_stacked(coef_own[...].astype(F32))
    mine = jnp.concatenate([mine, jnp.zeros_like(mine)], axis=0).astype(BF16)
    for n in range(64):
        block = received[n // 2, n % 2 * PAIRS : (n % 2 + 1) * PAIRS, :]
        if n < 32:
            up_1[n] = block
            down_2[n] = block
        else:
            up_2[n - 32] = block
            down_1[n - 32] = block
    for step, target, at in ((1, up_1, 32), (3, down_1, 32), (2, across, 0)):
        first = (kc + step) % 4 * 8
        for p in range(8):
            target[at + p] = received[first + p, 2 * PAIRS :, :]
        target[at + 8] = mine


def halves_stacked(coef):
    return jnp.concatenate([coef[:, :LANES], coef[:, LANES:]], axis=0)


def spread(row_of, count):
    keep = iota((8, LANES), 1) // PAIRS == iota((8, LANES), 0)
    pieces = []
    for p in range(count):
        for half in range(2):
            pieces.append(jnp.where(keep, jnp.broadcast_to(row_of(p, half), (8, LANES)), 0.0))
    return jnp.concatenate(pieces, axis=0).astype(BF16)


def repeat_matrix():
    same = iota((LANES, LANES), 0) % PAIRS == iota((LANES, LANES), 1) % PAIRS
    return jnp.where(same, 1.0, 0.0).astype(BF16)


def pair_blocks(low_of, high_of, pairs):
    low = iota((PAIRS, LANES), 1) < 64
    for n in range(64):
        first, second = low_of(n), high_of(n)
        pairs[2 * n] = jnp.where(low, first, pltpu.roll(second.astype(F32), 64, 1).astype(BF16))
        pairs[2 * n + 1] = jnp.where(low, pltpu.roll(first.astype(F32), 64, 1).astype(BF16), second)


def turn_points(near, first, pairs, turn, picked, turned, v):
    for i in range(32):
        picked[v % 2, i * PAIRS : (i + 1) * PAIRS, :] = pairs[near[first + 32 * v + i]]
    turned[:, v * 512 : (v + 1) * 512] = dot_t(turn, picked[v % 2]).astype(BF16)


def expand_points(turned, cols, result, v):
    for u in range(4 * v, 4 * v + 4):
        at = slice(u * LANES, (u + 1) * LANES)
        result[:, at] = jnp.dot(turned[:, at], cols[u], preferred_element_type=F32).astype(BF16)


def middle_kernel(
    near, received, coef_own, left_1, left_2, right_1, far_coef, result, cols, turn_far, pieces, pairs, diag, picked, turned
):
    kc = lax.axis_index("kc")
    repeat = repeat_matrix()
    same = iota((LANES, LANES), 0) // PAIRS == iota((LANES, LANES), 1) // PAIRS
    diag[...] = jnp.where(same, 1.0, 0.0).astype(BF16)

    def turn_of(first, second):
        rows = (first, second)

        def row_of(p, half):
            at = half * POINTS + p % POINTS
            return rows[p // POINTS][at : at + 1]

        return jnp.dot(spread(row_of, 8), repeat, preferred_element_type=F32).astype(BF16) * diag[...]

    turn = turn_of(halves_stacked(coef_own[...].astype(F32)), left_1[40].astype(F32))
    turn_far[...] = turn_of(right_1[40].astype(F32), far_coef[8].astype(F32))
    for p in range(8):
        pieces[kc, p] = received[kc * 8 + p, 2 * PAIRS :, :].astype(F32)
        pieces[(kc + 3) % 4, p] = left_1[32 + p].astype(F32)
        pieces[(kc + 1) % 4, p] = right_1[32 + p].astype(F32)
        pieces[(kc + 2) % 4, p] = far_coef[p].astype(F32)
    pair_blocks(
        lambda n: received[n // 2, n % 2 * PAIRS : (n % 2 + 1) * PAIRS, :],
        lambda n: left_1[n] if n < 32 else left_2[n - 32],
        pairs,
    )

    def build(v):
        for s in range(4):
            h, par = s // 2, s % 2

            def row_of(p, half):
                r = h * 8 + half * POINTS + p % POINTS
                return pieces[par * 2 + p // POINTS, v, r : r + 1, :]

            cols[4 * v + s] = dot_t(repeat, spread(row_of, 8)).astype(BF16) * diag[...]

    for v in range(9):
        if v < 8:
            build(v)
            turn_points(near, 256 * kc, pairs, turn, picked, turned, v)
        if v > 0:
            expand_points(turned, cols, result, v - 1)


def last_kernel(near, right_1, right_2, far_1, far_2, cols, turn_far, first, out, pairs, picked, turned, result, sem):
    kc = lax.axis_index("kc")

    def copy(n, v):
        source = first if n < 2 else result
        row = pl.multiple_of((kc + (0, 3, 1, 2)[n]) % 4 * 64, 64)
        at = pl.ds(v * 1024, 1024)
        return pltpu.make_async_copy(source.at[pl.ds(n % 2 * 64, 64), at], out.at[pl.ds(row, 64), at], sem.at[n, v])

    for v in range(4):
        for n in range(2):
            copy(n, v).start()
    pair_blocks(
        lambda n: right_2[n] if n < 32 else right_1[n - 32], lambda n: far_1[n] if n < 32 else far_2[n - 32], pairs
    )
    turn = turn_far[...]
    for v in range(9):
        if v < 8:
            turn_points(near, 256 * kc, pairs, turn, picked, turned, v)
        if v > 0:
            expand_points(turned, cols, result, v - 1)
            if v % 2 == 0:
                for n in (2, 3):
                    copy(n, v // 2 - 1).start()
    for v in range(4):
        for n in range(4):
            copy(n, v).wait()


def call(kernel, outs, in_specs, out_specs, scratch, flops, aliases=None):
    return pl.pallas_call(
        kernel,
        out_shape=outs,
        in_specs=in_specs,
        out_specs=out_specs,
        scratch_shapes=scratch,
        input_output_aliases=aliases or {},
        compiler_params=pltpu.CompilerParams(vmem_limit_bytes=8 << 20),
        cost_estimate=pl.CostEstimate(flops=flops, bytes_accessed=flops // 10, transcendentals=0),
    )


def shape(*dims):
    return jax.ShapeDtypeStruct(dims, BF16)


def shift(value, by):
    return lax.ppermute(value, "kc", [(i, (i + by) % 4) for i in range(4)])


def partner(value):
    return lax.ppermute(value, "kf_2", [(0, 1), (1, 0)])


def shards(kernel_coarse, coefficients, nearest):
    other = partner(kernel_coarse)
    coef_other = partner(coefficients)
    rotations = (8, 16, 32, LANES)
    own_copies = call(own_kernel, shape(*rotations), [VMEM] * 3, VMEM, [], 1000000)(kernel_coarse.astype(F32), nearest, coefficients)
    packed = call(
        pack_kernel, shape(PEERS, 48, LANES), [SMEM] + [VMEM] * 4, VMEM, [pltpu.VMEM(rotations, BF16)], 1000000
    )(nearest, own_copies, other, coefficients, coef_other)
    received = lax.all_to_all(packed, ZY, split_axis=0, concat_axis=0, tiled=True)
    block = (PAIRS, LANES)
    sizes = (41, 32, 41, 32, 9)
    up_1, up_2, down_1, down_2, across = call(
        split_kernel, tuple(shape(n, *block) for n in sizes), [VMEM, VMEM], (VMEM,) * 5, [], 100000
    )(received, coefficients)
    left_1 = shift(up_1, 1)
    right_1 = shift(down_1, -1)
    far_coef = shift(across, 2)
    left_2 = shift(up_2, 1)
    right_2 = shift(down_2, -1)
    far_1 = shift(left_1[:PEERS], 1)
    far_2 = shift(right_1[:PEERS], -1)
    pairs = pltpu.VMEM((128, *block), BF16)
    picked = pltpu.VMEM((2, 512, LANES), BF16)
    turned = pltpu.VMEM((LANES, 4096), BF16)
    first, cols, turn_far = call(
        middle_kernel,
        (shape(LANES, 4096), shape(32, LANES, LANES), shape(LANES, LANES)),
        [SMEM] + [VMEM] * 6,
        (VMEM,) * 3,
        [pltpu.VMEM((4, 8, *block), F32), pairs, pltpu.VMEM((LANES, LANES), BF16), picked, turned],
        8000000,
    )(nearest, received, coefficients, left_1, left_2, right_1, far_coef)
    return call(
        last_kernel,
        shape(256, 4096),
        [SMEM] + [VMEM] * 7,
        ANY,
        [pairs, picked, turned, turned, pltpu.SemaphoreType.DMA((4, 4))],
        3000000,
    )(nearest, right_1, right_2, far_1, far_2, cols, turn_far, first)


def solution(mesh):
    split = Mesh(mesh.devices.reshape(8, 4, 2, mesh.shape["kc"]), KF_KC)
    return jax.shard_map(
        shards,
        mesh=split,
        in_specs=(P(KF, None), P(KF_KC, None), P()),
        out_specs=P(KF, "kc"),
        check_vma=False,
    )
```

time: 50.9 us -> 54.5 us (1.071)
  waiting for transfers between devices: 2.96 us -> 8.36 us
  Pallas kernels: 9.25 us -> 7.61 us
  local copies, waits for them, and re-layouts: 2.3 us -> 1.39 us
  other arithmetic: 0.08 us -> 0.92 us
    ppermute x7, waiting for transfers between devices: 2.96 us -> 8.35 us  [shift(): return lax.ppermute(value, 'kc', [(i, (i + by) % 4) for i in range(4)])]
    pallas_call x2, Pallas kernels: 7.19 us -> 5.56 us  [the longest x1 2.96 us: shards(): call(last_kernel, shape(256, 4096), [SMEM] + [VMEM] * 7, ANY, [pairs, pic...]
    convert_element_type x0 -> x1, other arithmetic: none -> 0.92 us  [shards(): kernel_coarse.astype(F32)]
    unnamed x10 -> x8, local copies, waits for them, and re-layouts: 2.28 us -> 1.37 us
  transfers between devices with their start and end apart: 9 -> 9, of which waited for: 3 -> 2; matrix products, arithmetic and copies ran while one was open for 0% -> 2% of each run, Pallas kernels for 9% -> 5%
where the time goes in v5:
time: 54.5 us; the launch traced here: 54.4 us
  blocking collectives  26.7 us (49%)
  starting transfers between devices  9.22 us (17%)
  waiting for transfers between devices  8.36 us (15%)
  Pallas kernels  7.61 us (14%)
  local copies, waits for them, and re-layouts  1.39 us (3%)
  other arithmetic  0.92 us (2%)
    all_to_all x1, blocking collectives, shards(): lax.all_to_all(packed, ZY, split_axis=0, concat_axis=0, tiled=True)  26.7 us
    ppermute x7, starting transfers between devices, shift(): return lax.ppermute(value, 'kc', [(i, (i + by) % 4) for i in range(4)])  8.71 us
    ppermute x7, waiting for transfers between devices, shift(): return lax.ppermute(value, 'kc', [(i, (i + by) % 4) for i in range(4)])  8.35 us
    pallas_call x1, Pallas kernels, shards(): call(last_kernel, shape(256, 4096), [SMEM] + [VMEM] * 7, ANY, [pairs, pic...  2.96 us
    pallas_call x1, Pallas kernels, shards(): call(middle_kernel, (shape(LANES, 4096), shape(32, LANES, LANES), shape(L...  2.6 us
    pallas_call x1, Pallas kernels, shards(): call(pack_kernel, shape(PEERS, 48, LANES), [SMEM] + [VMEM] * 4, VMEM, [pl...  1.67 us
    unnamed x8, local copies, waits for them, and re-layouts  1.37 us
  transfers between devices with their start and end apart: 9, of which 2 were waited for; matrix products, arithmetic and copies ran while one was open for 2% of the time, Pallas kernels for 5%

profile of v5, /device:TPU:6, one launch (start us, length us, event | category | flops | bytes accessed | tf_op | source)
XLA Modules:
  0.0 54.4 jit_solution(2514904391347768971)
XLA Ops:
  0.0 0.5 collective-permute-start.1
  0.5 0.9 %convert_element_type.3.own = f32[32,2048]{1,0:T(8,128)S(1)} convert(bf16[32,2048]{1,0:T(8,128)(2,1)} %param.3) | non-fusion elementwise | flops 65536 | bytes 393216 | tf_op jit(solution)/shard_map/convert_element_type | solution.py:239
  1.4 0.0 copy-start
  1.4 0.7 %copy-done = s32[1024]{0:T(1024)S(1)} copy-done((s32[1024]{0:T(1024)S(1)}, s32[1024]{0:T(1024)}, u32[]{:S(2)}) %copy-start) | copy-done | bytes 4120
  2.1 0.7 %copy-done.2 = bf16[4,256]{1,0:T(4,128)(2,1)S(1)} copy-done((bf16[4,256]{1,0:T(4,128)(2,1)S(1)}, bf16[4,256]{1,0:T(4,128)(2,1)}, u32[]{:S(2)}) %copy-start.2) | copy-done | bytes 2072
  2.8 0.3 shard_map.37.own_copies
  3.1 0.0 collective-permute-done.1.coef_other
  3.1 0.0 collective-permute-done.other
  3.1 1.7 %shard_map.38 = bf16[32,48,128]{2,1,0:T(8,128)(2,1)S(1)} custom-call(s32[1024]{0:T(1024)S(1)} %copy-done, bf16[8,16,32,128]{3,2,1,0:T(8,128)(2,1)S(1)} %shard_map.37.own_copies, bf16[32,2048]{1,0:T(8,128)(2,1)S(1)} %collective-permute-done.other, bf16[4,256]{1,0:T(4,128)(2,1)S(1)} %copy-done.2, bf16[4,256]{1,0:T(4,128)(2,1)S(1)} %collective-permute-done.1.coef_other), custom_call_target="tpu_custom_call" | custom-call | flops 1000000 | bytes 100000 | tf_op jit(solution)/shard_map/pallas_call | solution.py:240
  4.8 26.7 %all_to_all.5.received = bf16[32,48,128]{2,1,0:T(8,128)(2,1)S(1)} all-to-all(bf16[32,48,128]{2,1,0:T(8,128)(2,1)S(1)} %shard_map.38), channel_id=1, replica_groups=mesh['kf_0'=8,'kf_1'=4,'kf_2'=2,'kc'=4] {'kf_0','kf_1'}, dimensions={0} | all-to-all | bytes 786432 | tf_op jit(solution)/shard_map/all_to_all | solution.py:243
  31.6 0.1 shard_map.39
  31.7 0.9 %collective-permute-start.2 = (bf16[41,16,128]{2,1,0:T(8,128)(2,1)S(1)}, bf16[41,16,128]{2,1,0:T(8,128)(2,1)S(1)}, u32[]{:S(2)}, u32[]{:S(2)}) collective-permute-start(bf16[41,16,128]{2,1,0:T(8,128)(2,1)S(1)} %get-tuple-element.13), channel_id=1, source_target_pairs={{0,3},{1,0},{2,1},{3,2},{4,7},{5,4},{6,5},{7,6},{8,11},{9,8},{10,9... | collective-permute-start | bytes 503816 | tf_op jit(solution)/shard_map/ppermute | solution.py:228
  32.6 2.4 %collective-permute-start.4 = (bf16[41,16,128]{2,1,0:T(8,128)(2,1)S(1)}, bf16[41,16,128]{2,1,0:T(8,128)(2,1)S(1)}, u32[]{:S(2)}, u32[]{:S(2)}) collective-permute-start(bf16[41,16,128]{2,1,0:T(8,128)(2,1)S(1)} %get-tuple-element.15), channel_id=1, source_target_pairs={{0,1},{1,2},{2,3},{3,0},{4,5},{5,6},{6,7},{7,4},{8,9},{9,10},{10,1... | collective-permute-start | bytes 503816 | tf_op jit(solution)/shard_map/ppermute | solution.py:228
  35.0 0.0 collective-permute-start.7
  35.0 2.0 %collective-permute-start.3 = (bf16[32,16,128]{2,1,0:T(8,128)(2,1)S(1)}, bf16[32,16,128]{2,1,0:T(8,128)(2,1)S(1)}, u32[]{:S(2)}, u32[]{:S(2)}) collective-permute-start(bf16[32,16,128]{2,1,0:T(8,128)(2,1)S(1)} %get-tuple-element.14), channel_id=1, source_target_pairs={{0,3},{1,0},{2,1},{3,2},{4,7},{5,4},{6,5},{7,6},{8,11},{9,8},{10,9... | collective-permute-start | bytes 393224 | tf_op jit(solution)/shard_map/ppermute | solution.py:228
  37.0 2.9 %collective-permute-done.2.right_1 = bf16[41,16,128]{2,1,0:T(8,128)(2,1)S(1)} collective-permute-done((bf16[41,16,128]{2,1,0:T(8,128)(2,1)S(1)}, bf16[41,16,128]{2,1,0:T(8,128)(2,1)S(1)}, u32[]{:S(2)}, u32[]{:S(2)}) %collective-permute-start.2) | collective-permute-done | bytes 167968 | tf_op jit(solution)/shard_map/ppermute | solution.py:228
  39.9 0.1 collective-permute-start.6
  40.0 3.3 %collective-permute-start.5 = (bf16[32,16,128]{2,1,0:T(8,128)(2,1)S(1)}, bf16[32,16,128]{2,1,0:T(8,128)(2,1)S(1)}, u32[]{:S(2)}, u32[]{:S(2)}) collective-permute-start(bf16[32,16,128]{2,1,0:T(8,128)(2,1)S(1)} %slice.8), channel_id=1, source_target_pairs={{0,1},{1,2},{2,3},{3,0},{4,5},{5,6},{6,7},{7,4},{8,9},{9,10},{10,1... | collective-permute-start | bytes 393224 | tf_op jit(solution)/shard_map/ppermute | solution.py:228
  43.3 0.0 collective-permute-start.8
  43.3 5.5 %collective-permute-done.8.far_coef = bf16[9,16,128]{2,1,0:T(8,128)(2,1)S(1)} collective-permute-done((bf16[9,16,128]{2,1,0:T(8,128)(2,1)S(1)}, bf16[9,16,128]{2,1,0:T(8,128)(2,1)S(1)}, u32[]{:S(2)}, u32[]{:S(2)}) %collective-permute-start.8) | collective-permute-done | bytes 36896 | tf_op jit(solution)/shard_map/ppermute | solution.py:228
  48.8 0.0 collective-permute-done.7.left_2
  48.8 2.6 %shard_map.40 = (bf16[128,4096]{1,0:T(8,128)(2,1)S(1)}, bf16[32,128,128]{2,1,0:T(8,128)(2,1)S(1)}, bf16[128,128]{1,0:T(8,128)(2,1)S(1)}) custom-call(s32[1024]{0:T(1024)S(1)} %copy-done.1, bf16[32,48,128]{2,1,0:T(8,128)(2,1)S(1)} %all_to_all.5.received, bf16[4,256]{1,0:T(4,128)(2,1)S(1)} %copy-done.3, ...), custom_call_target="tpu_custom_call" | custom-call | flops 8000000 | bytes 800000 | tf_op jit(solution)/shard_map/pallas_call | solution.py:259
  51.4 0.0 collective-permute-done.3.right_2
  51.4 3.0 %shard_map.41 = bf16[256,4096]{1,0:T(8,128)(2,1)} custom-call(s32[1024]{0:T(1024)S(1)} %copy-done.1, bf16[41,16,128]{2,1,0:T(8,128)(2,1)S(1)} %collective-permute-done.2.right_1, bf16[32,16,128]{2,1,0:T(8,128)(2,1)S(1)} %collective-permute-done.3.right_2, bf16[32,16,128]{2,1,0:T(8,128)(2,1)S(1)} %collective-permute-done.5.far_1, ...), custom_call_target="tpu_custom_call" | custom-call | flops 3000000 | bytes 300000 | tf_op jit(solution)/shard_map/pallas_call | solution.py:267
  (11 shorter events, 0.0 us)
Async XLA Ops:
  0.0 3.1 %collective-permute-start = (bf16[32,2048]{1,0:T(8,128)(2,1)}, bf16[32,2048]{1,0:T(8,128)(2,1)S(1)}, u32[]{:S(2)}, u32[]{:S(2)}) collective-permute-start(bf16[32,2048]{1,0:T(8,128)(2,1)} %param.3), channel_id=1, source_target_pairs={{0,4},{4,0},{1,5},{5,1},{2,6},{6,2},{3,7},{7,3},{8,12},{12,8},{9,1... | collective-permute-start | bytes 393224 | tf_op jit(solution)/shard_map/ppermute | solution.py:232
  0.0 3.1 %collective-permute-start.1 = (bf16[4,256]{1,0:T(4,128)(2,1)}, bf16[4,256]{1,0:T(4,128)(2,1)S(1)}, u32[]{:S(2)}, u32[]{:S(2)}) collective-permute-start(bf16[4,256]{1,0:T(4,128)(2,1)} %coef_own.7), channel_id=1, source_target_pairs={{0,4},{4,0},{1,5},{5,1},{2,6},{6,2},{3,7},{7,3},{8,12},{12,8},{9,1... | collective-permute-start | bytes 6152 | tf_op jit(solution)/shard_map/ppermute | solution.py:232
  1.4 0.7 %copy-start = (s32[1024]{0:T(1024)S(1)}, s32[1024]{0:T(1024)}, u32[]{:S(2)}) copy-start(s32[1024]{0:T(1024)} %near.7) | copy-start | bytes 12292
  2.1 0.7 %copy-start.2 = (bf16[4,256]{1,0:T(4,128)(2,1)S(1)}, bf16[4,256]{1,0:T(4,128)(2,1)}, u32[]{:S(2)}) copy-start(bf16[4,256]{1,0:T(4,128)(2,1)} %coef_own.7) | copy-start | bytes 6148
  2.8 46.0 %copy-start.1 = (s32[1024]{0:T(1024)S(1)}, s32[1024]{0:T(1024)}, u32[]{:S(2)}) copy-start(s32[1024]{0:T(1024)} %near.7) | copy-start | bytes 12292
  2.8 46.0 %copy-start.3 = (bf16[4,256]{1,0:T(4,128)(2,1)S(1)}, bf16[4,256]{1,0:T(4,128)(2,1)}, u32[]{:S(2)}) copy-start(bf16[4,256]{1,0:T(4,128)(2,1)} %coef_own.7) | copy-start | bytes 6148
  31.7 8.2 %collective-permute-start.2 = (bf16[41,16,128]{2,1,0:T(8,128)(2,1)S(1)}, bf16[41,16,128]{2,1,0:T(8,128)(2,1)S(1)}, u32[]{:S(2)}, u32[]{:S(2)}) collective-permute-start(bf16[41,16,128]{2,1,0:T(8,128)(2,1)S(1)} %get-tuple-element.13), channel_id=1, source_target_pairs={{0,3},{1,0},{2,1},{3,2},{4,7},{5,4},{6,5},{7,6},{8,11},{9,8},{10,9... | collective-permute-start | bytes 503816 | tf_op jit(solution)/shard_map/ppermute | solution.py:228
  32.6 7.4 %collective-permute-start.4 = (bf16[41,16,128]{2,1,0:T(8,128)(2,1)S(1)}, bf16[41,16,128]{2,1,0:T(8,128)(2,1)S(1)}, u32[]{:S(2)}, u32[]{:S(2)}) collective-permute-start(bf16[41,16,128]{2,1,0:T(8,128)(2,1)S(1)} %get-tuple-element.15), channel_id=1, source_target_pairs={{0,1},{1,2},{2,3},{3,0},{4,5},{5,6},{6,7},{7,4},{8,9},{9,10},{10,1... | collective-permute-start | bytes 503816 | tf_op jit(solution)/shard_map/ppermute | solution.py:228
  35.0 13.8 %collective-permute-start.7 = (bf16[32,16,128]{2,1,0:T(8,128)(2,1)S(1)}, bf16[32,16,128]{2,1,0:T(8,128)(2,1)S(1)}, u32[]{:S(2)}, u32[]{:S(2)}) collective-permute-start(bf16[32,16,128]{2,1,0:T(8,128)(2,1)S(1)} %get-tuple-element.16), channel_id=1, source_target_pairs={{0,1},{1,2},{2,3},{3,0},{4,5},{5,6},{6,7},{7,4},{8,9},{9,10},{10,1... | collective-permute-start | bytes 393224 | tf_op jit(solution)/shard_map/ppermute | solution.py:228
  35.0 16.4 %collective-permute-start.3 = (bf16[32,16,128]{2,1,0:T(8,128)(2,1)S(1)}, bf16[32,16,128]{2,1,0:T(8,128)(2,1)S(1)}, u32[]{:S(2)}, u32[]{:S(2)}) collective-permute-start(bf16[32,16,128]{2,1,0:T(8,128)(2,1)S(1)} %get-tuple-element.14), channel_id=1, source_target_pairs={{0,3},{1,0},{2,1},{3,2},{4,7},{5,4},{6,5},{7,6},{8,11},{9,8},{10,9... | collective-permute-start | bytes 393224 | tf_op jit(solution)/shard_map/ppermute | solution.py:228
  39.9 11.5 %collective-permute-start.6 = (bf16[32,16,128]{2,1,0:T(8,128)(2,1)S(1)}, bf16[32,16,128]{2,1,0:T(8,128)(2,1)S(1)}, u32[]{:S(2)}, u32[]{:S(2)}) collective-permute-start(bf16[32,16,128]{2,1,0:T(8,128)(2,1)S(1)} %slice.9), channel_id=1, source_target_pairs={{0,3},{1,0},{2,1},{3,2},{4,7},{5,4},{6,5},{7,6},{8,11},{9,8},{10,9... | collective-permute-start | bytes 393224 | tf_op jit(solution)/shard_map/ppermute | solution.py:228
  40.0 11.4 %collective-permute-start.5 = (bf16[32,16,128]{2,1,0:T(8,128)(2,1)S(1)}, bf16[32,16,128]{2,1,0:T(8,128)(2,1)S(1)}, u32[]{:S(2)}, u32[]{:S(2)}) collective-permute-start(bf16[32,16,128]{2,1,0:T(8,128)(2,1)S(1)} %slice.8), channel_id=1, source_target_pairs={{0,1},{1,2},{2,3},{3,0},{4,5},{5,6},{6,7},{7,4},{8,9},{9,10},{10,1... | collective-permute-start | bytes 393224 | tf_op jit(solution)/shard_map/ppermute | solution.py:228
  43.3 5.5 %collective-permute-start.8 = (bf16[9,16,128]{2,1,0:T(8,128)(2,1)S(1)}, bf16[9,16,128]{2,1,0:T(8,128)(2,1)S(1)}, u32[]{:S(2)}, u32[]{:S(2)}) collective-permute-start(bf16[9,16,128]{2,1,0:T(8,128)(2,1)S(1)} %get-tuple-element.17), channel_id=1, source_target_pairs={{0,2},{1,3},{2,0},{3,1},{4,6},{5,7},{6,4},{7,5},{8,10},{9,11},{10,... | collective-permute-start | bytes 110600 | tf_op jit(solution)/shard_map/ppermute | solution.py:228

commit v6 on v5

--- a/solution.py
+++ b/solution.py
@@ -14,6 +14,7 @@
 PAIRS = 16
 POINTS = 4
 PEERS = 32
+FINE = 1024
 BF16 = jnp.bfloat16
 F32 = jnp.float32
 VMEM = pl.BlockSpec(memory_space=pltpu.VMEM)
@@ -31,35 +32,40 @@
 
 def turn_rows(rows, copies):
     for b in range(16):
-        block = rows[:, b * LANES : (b + 1) * LANES].astype(F32)
+        block = rows[:32, b * LANES : (b + 1) * LANES].astype(F32)
         for s in range(8):
             turned = pltpu.roll(block, s * PAIRS, 1) if s else block
             copies[s, b] = turned.astype(BF16)
 
 
-def own_kernel(own, near, coef_own, copies):
-    turn_rows(own, copies)
-
-
-def pack_kernel(near, own_copies, other, coef_own, coef_other, out, other_copies):
+def own_kernel(fetched, copies, near, coef):
+    near[...] = fetched[32:33, :FINE].astype(jnp.int32)
+    coef[...] = halves_stacked(fetched[40:44, : 2 * LANES])
+    turn_rows(fetched, copies)
+
+
+def index_copy(near, scalars, sem):
+    return pltpu.make_async_copy(near, scalars, sem.at[0])
+
+
+def pack_kernel(near, own_copies, other, coef_own, coef_other, out, other_copies, scalars, sem):
+    fetch = index_copy(near, scalars, sem)
+    fetch.start()
     kc = lax.axis_index("kc")
     core = lax.axis_index("kf_2")
     turn_rows(other, other_copies)
     copies = (own_copies, other_copies)
-    a = coef_own[...].astype(F32)
-    o = coef_other[...].astype(F32)
-    first = jnp.where(core == 0, a, o)
-    second = jnp.where(core == 0, o, a)
-    coef = jnp.concatenate(
-        [first[:, :LANES], first[:, LANES:], second[:, :LANES], second[:, LANES:]], axis=0
-    ).astype(BF16)
+    a = coef_own[...]
+    o = halves_stacked(coef_other[...].astype(F32))
+    coef = jnp.concatenate([jnp.where(core == 0, a, o), jnp.where(core == 0, o, a)], axis=0).astype(BF16)
+    fetch.wait()
     group = iota((PAIRS, LANES), 1) // PAIRS
     base = 16 * core + 4 * kc
 
     def body(d, carry):
         tiles = [None, None]
         for j in range(POINTS):
-            c = near[32 * d + base + j]
+            c = scalars[0, 32 * d + base + j]
             for lo in range(2):
                 at = lo * POINTS + j
                 for n in range(2):
@@ -75,7 +81,7 @@
 
 def split_kernel(received, coef_own, up_1, up_2, down_1, down_2, across):
     kc = lax.axis_index("kc")
-    mine = halves_stacked(coef_own[...].astype(F32))
+    mine = coef_own[...]
     mine = jnp.concatenate([mine, jnp.zeros_like(mine)], axis=0).astype(BF16)
     for n in range(64):
         block = received[n // 2, n % 2 * PAIRS : (n % 2 + 1) * PAIRS, :]
@@ -118,21 +124,30 @@
         pairs[2 * n + 1] = jnp.where(low, pltpu.roll(first.astype(F32), 64, 1).astype(BF16), second)
 
 
-def turn_points(near, first, pairs, turn, picked, turned, v):
-    for i in range(32):
-        picked[v % 2, i * PAIRS : (i + 1) * PAIRS, :] = pairs[near[first + 32 * v + i]]
-    turned[:, v * 512 : (v + 1) * 512] = dot_t(turn, picked[v % 2]).astype(BF16)
+def turn_points(scalars, first, pairs, turn, picked, turned, v):
+    for i in range(64):
+        picked[v % 2, i * PAIRS : (i + 1) * PAIRS, :] = pairs[scalars[0, first + 64 * v + i]]
+    turned[:, v * 1024 : (v + 1) * 1024] = dot_t(turn, picked[v % 2]).astype(BF16)
 
 
 def expand_points(turned, cols, result, v):
-    for u in range(4 * v, 4 * v + 4):
+    for u in range(8 * v, 8 * v + 8):
         at = slice(u * LANES, (u + 1) * LANES)
         result[:, at] = jnp.dot(turned[:, at], cols[u], preferred_element_type=F32).astype(BF16)
 
 
+def row_copy(result, out, sem, n, step, v):
+    row = pl.multiple_of((lax.axis_index("kc") + step) % 4 * 64, 64)
+    at = pl.ds(v * 1024, 1024)
+    return pltpu.make_async_copy(result.at[pl.ds(n * 64, 64), at], out.at[pl.ds(row, 64), at], sem.at[1 + 4 * n + v])
+
+
 def middle_kernel(
-    near, received, coef_own, left_1, left_2, right_1, far_coef, result, cols, turn_far, pieces, pairs, diag, picked, turned
+    near, received, coef_own, left_1, left_2, right_1, far_coef, out, cols, turn_far,
+    pieces, pairs, diag, picked, turned, result, scalars, sem
 ):
+    fetch = index_copy(near, scalars, sem)
+    fetch.start()
     kc = lax.axis_index("kc")
     repeat = repeat_matrix()
     same = iota((LANES, LANES), 0) // PAIRS == iota((LANES, LANES), 1) // PAIRS
@@ -147,7 +162,7 @@
 
         return jnp.dot(spread(row_of, 8), repeat, preferred_element_type=F32).astype(BF16) * diag[...]
 
-    turn = turn_of(halves_stacked(coef_own[...].astype(F32)), left_1[40].astype(F32))
+    turn = turn_of(coef_own[...], left_1[40].astype(F32))
     turn_far[...] = turn_of(right_1[40].astype(F32), far_coef[8].astype(F32))
     for p in range(8):
         pieces[kc, p] = received[kc * 8 + p, 2 * PAIRS :, :].astype(F32)
@@ -161,50 +176,50 @@
     )
 
     def build(v):
-        for s in range(4):
-            h, par = s // 2, s % 2
+        for s in range(8):
+            p_index, h, par = 2 * v + s // 4, s // 2 % 2, s % 2
 
             def row_of(p, half):
                 r = h * 8 + half * POINTS + p % POINTS
-                return pieces[par * 2 + p // POINTS, v, r : r + 1, :]
-
-            cols[4 * v + s] = dot_t(repeat, spread(row_of, 8)).astype(BF16) * diag[...]
-
-    for v in range(9):
-        if v < 8:
-            build(v)
-            turn_points(near, 256 * kc, pairs, turn, picked, turned, v)
+                return pieces[par * 2 + p // POINTS, p_index, r : r + 1, :]
+
+            cols[8 * v + s] = dot_t(repeat, spread(row_of, 8)).astype(BF16) * diag[...]
+
+    build(0)
+    fetch.wait()
+    for v in range(5):
+        if v < 4:
+            turn_points(scalars, 256 * kc, pairs, turn, picked, turned, v)
+            if v > 0:
+                build(v)
         if v > 0:
             expand_points(turned, cols, result, v - 1)
-
-
-def last_kernel(near, right_1, right_2, far_1, far_2, cols, turn_far, first, out, pairs, picked, turned, result, sem):
+            for n, step in enumerate((0, 3)):
+                row_copy(result, out, sem, n, step, v - 1).start()
+    for v in range(4):
+        for n, step in enumerate((0, 3)):
+            row_copy(result, out, sem, n, step, v).wait()
+
+
+def last_kernel(near, right_1, right_2, far_1, far_2, cols, turn_far, partial, out, pairs, picked, turned, result, scalars, sem):
+    fetch = index_copy(near, scalars, sem)
+    fetch.start()
     kc = lax.axis_index("kc")
-
-    def copy(n, v):
-        source = first if n < 2 else result
-        row = pl.multiple_of((kc + (0, 3, 1, 2)[n]) % 4 * 64, 64)
-        at = pl.ds(v * 1024, 1024)
-        return pltpu.make_async_copy(source.at[pl.ds(n % 2 * 64, 64), at], out.at[pl.ds(row, 64), at], sem.at[n, v])
-
-    for v in range(4):
-        for n in range(2):
-            copy(n, v).start()
     pair_blocks(
         lambda n: right_2[n] if n < 32 else right_1[n - 32], lambda n: far_1[n] if n < 32 else far_2[n - 32], pairs
     )
     turn = turn_far[...]
-    for v in range(9):
-        if v < 8:
-            turn_points(near, 256 * kc, pairs, turn, picked, turned, v)
+    fetch.wait()
+    for v in range(5):
+        if v < 4:
+            turn_points(scalars, 256 * kc, pairs, turn, picked, turned, v)
         if v > 0:
             expand_points(turned, cols, result, v - 1)
-            if v % 2 == 0:
-                for n in (2, 3):
-                    copy(n, v // 2 - 1).start()
+            for n, step in enumerate((1, 2)):
+                row_copy(result, out, sem, n, step, v - 1).start()
     for v in range(4):
-        for n in range(4):
-            copy(n, v).wait()
+        for n, step in enumerate((1, 2)):
+            row_copy(result, out, sem, n, step, v).wait()
 
 
 def call(kernel, outs, in_specs, out_specs, scratch, flops, aliases=None):
@@ -236,16 +251,27 @@
     other = partner(kernel_coarse)
     coef_other = partner(coefficients)
     rotations = (8, 16, 32, LANES)
-    own_copies = call(own_kernel, shape(*rotations), [VMEM] * 3, VMEM, [], 1000000)(kernel_coarse.astype(F32), nearest, coefficients)
+    table = jnp.pad(nearest.reshape(1, FINE), ((32, 15), (0, FINE))).astype(F32)
+    rows = jnp.pad(coefficients.astype(F32), ((40, 4), (0, 2 * FINE - 2 * LANES)))
+    fetched = jnp.pad(kernel_coarse.astype(F32), ((0, 16), (0, 0))) + table + rows
+    scalars = [pltpu.SMEM((1, FINE), jnp.int32), pltpu.SemaphoreType.DMA((9,))]
+    own_copies, near, coef_own = call(
+        own_kernel,
+        (shape(*rotations), jax.ShapeDtypeStruct((1, FINE), jnp.int32), jax.ShapeDtypeStruct((8, LANES), F32)),
+        [VMEM],
+        (VMEM,) * 3,
+        [],
+        1000000,
+    )(fetched)
     packed = call(
-        pack_kernel, shape(PEERS, 48, LANES), [SMEM] + [VMEM] * 4, VMEM, [pltpu.VMEM(rotations, BF16)], 1000000
-    )(nearest, own_copies, other, coefficients, coef_other)
+        pack_kernel, shape(PEERS, 48, LANES), [VMEM] * 5, VMEM, [pltpu.VMEM(rotations, BF16)] + scalars, 1000000
+    )(near, own_copies, other, coef_own, coef_other)
     received = lax.all_to_all(packed, ZY, split_axis=0, concat_axis=0, tiled=True)
     block = (PAIRS, LANES)
     sizes = (41, 32, 41, 32, 9)
     up_1, up_2, down_1, down_2, across = call(
         split_kernel, tuple(shape(n, *block) for n in sizes), [VMEM, VMEM], (VMEM,) * 5, [], 100000
-    )(received, coefficients)
+    )(received, coef_own)
     left_1 = shift(up_1, 1)
     right_1 = shift(down_1, -1)
     far_coef = shift(across, 2)
@@ -254,24 +280,25 @@
     far_1 = shift(left_1[:PEERS], 1)
     far_2 = shift(right_1[:PEERS], -1)
     pairs = pltpu.VMEM((128, *block), BF16)
-    picked = pltpu.VMEM((2, 512, LANES), BF16)
+    picked = pltpu.VMEM((2, 1024, LANES), BF16)
     turned = pltpu.VMEM((LANES, 4096), BF16)
-    first, cols, turn_far = call(
+    partial, cols, turn_far = call(
         middle_kernel,
-        (shape(LANES, 4096), shape(32, LANES, LANES), shape(LANES, LANES)),
-        [SMEM] + [VMEM] * 6,
-        (VMEM,) * 3,
-        [pltpu.VMEM((4, 8, *block), F32), pairs, pltpu.VMEM((LANES, LANES), BF16), picked, turned],
+        (shape(256, 4096), shape(32, LANES, LANES), shape(LANES, LANES)),
+        [VMEM] * 7,
+        (ANY, VMEM, VMEM),
+        [pltpu.VMEM((4, 8, *block), F32), pairs, pltpu.VMEM((LANES, LANES), BF16), picked, turned, turned] + scalars,
         8000000,
-    )(nearest, received, coefficients, left_1, left_2, right_1, far_coef)
+    )(near, received, coef_own, left_1, left_2, right_1, far_coef)
     return call(
         last_kernel,
         shape(256, 4096),
-        [SMEM] + [VMEM] * 7,
+        [VMEM] * 7 + [ANY],
         ANY,
-        [pairs, picked, turned, turned, pltpu.SemaphoreType.DMA((4, 4))],
+        [pairs, picked, turned, turned] + scalars,
         3000000,
-    )(nearest, right_1, right_2, far_1, far_2, cols, turn_far, first)
+        {7: 0},
+    )(near, right_1, right_2, far_1, far_2, cols, turn_far, partial)
 
 
 def solution(mesh):

time: 54.5 us -> 53.6 us (0.983)
  local copies, waits for them, and re-layouts: 1.39 us -> 0.02 us
    unnamed x8 -> x0, local copies, waits for them, and re-layouts: 1.37 us -> none
    add x0 -> x1, other arithmetic: none -> 0.96 us  [shards(): jnp.pad(kernel_coarse.astype(F32), ((0, 16), (0, 0))) + table + rows]
    convert_element_type x1 -> x0, other arithmetic: 0.92 us -> none  [shards(): kernel_coarse.astype(F32)]
  transfers between devices with their start and end apart: 9 -> 9, of which waited for: 2 -> 2; matrix products, arithmetic and copies ran while one was open for 2% -> 2% of each run, Pallas kernels for 5% -> 6%
where the time goes in v6:
time: 53.6 us; the launch traced here: 53.5 us
  blocking collectives  27.1 us (51%)
  starting transfers between devices  9.22 us (17%)
  waiting for transfers between devices  8.54 us (16%)
  Pallas kernels  7.59 us (14%)
  other arithmetic  0.96 us (2%)
    all_to_all x1, blocking collectives, shards(): lax.all_to_all(packed, ZY, split_axis=0, concat_axis=0, tiled=True)  27.1 us
    ppermute x7, starting transfers between devices, shift(): return lax.ppermute(value, 'kc', [(i, (i + by) % 4) for i in range(4)])  8.71 us
    ppermute x7, waiting for transfers between devices, shift(): return lax.ppermute(value, 'kc', [(i, (i + by) % 4) for i in range(4)])  8.53 us
    pallas_call x1, Pallas kernels, shards(): call(middle_kernel, (shape(256, 4096), shape(32, LANES, LANES), shape(LAN...  3.02 us
    pallas_call x1, Pallas kernels, shards(): call(last_kernel, shape(256, 4096), [VMEM] * 7 + [ANY], ANY, [pairs, pick...  2.52 us
    pallas_call x1, Pallas kernels, shards(): call(pack_kernel, shape(PEERS, 48, LANES), [VMEM] * 5, VMEM, [pltpu.VMEM(...  1.67 us
  transfers between devices with their start and end apart: 9, of which 2 were waited for; matrix products, arithmetic and copies ran while one was open for 2% of the time, Pallas kernels for 6%

profile of v6, /device:TPU:6, one launch (start us, length us, event | category | flops | bytes accessed | tf_op | source)
XLA Modules:
  0.0 53.5 jit_solution(309449831254064585)
XLA Ops:
  0.0 0.0 collective-permute-start.1
  0.0 0.5 collective-permute-start
  0.5 1.0 %convert_add_fusion.fetched = f32[48,2048]{1,0:T(8,128)S(1)} fusion(s32[1,1024]{1,0:T(1,128)} %bitcast.1, bf16[4,256]{1,0:T(4,128)(2,1)} %param.4, bf16[32,2048]{1,0:T(8,128)(2,1)} %param.3), kind=kLoop, calls=%fused_computation | loop fusion | flops 491520 | bytes 530432 | tf_op jit(solution)/shard_map/add | solution.py:256
  1.5 0.3 shard_map.37
  1.8 0.0 collective-permute-done.1.coef_other
  1.8 0.0 collective-permute-done.other
  1.8 1.7 %shard_map.38 = bf16[32,48,128]{2,1,0:T(8,128)(2,1)S(1)} custom-call(s32[1,1024]{1,0:T(1,128)S(1)} %get-tuple-element.16.near, bf16[8,16,32,128]{3,2,1,0:T(8,128)(2,1)S(1)} %get-tuple-element.17.own_copies, bf16[32,2048]{1,0:T(8,128)(2,1)S(1)} %collective-permute-done.other, f32[8,128]{1,0:T(8,128)S(1)} %get-tuple-element.18.coef_own, ...), custom_call_target="tpu_custom_call" | custom-call | flops 1000000 | bytes 100000 | tf_op jit(solution)/shard_map/pallas_call | solution.py:266
  3.5 27.1 %all_to_all.5.received = bf16[32,48,128]{2,1,0:T(8,128)(2,1)S(1)} all-to-all(bf16[32,48,128]{2,1,0:T(8,128)(2,1)S(1)} %shard_map.38), channel_id=1, replica_groups=mesh['kf_0'=8,'kf_1'=4,'kf_2'=2,'kc'=4] {'kf_0','kf_1'}, dimensions={0} | all-to-all | bytes 786432 | tf_op jit(solution)/shard_map/all_to_all | solution.py:269
  30.6 0.1 shard_map.39
  30.6 0.9 %collective-permute-start.2 = (bf16[41,16,128]{2,1,0:T(8,128)(2,1)S(1)}, bf16[41,16,128]{2,1,0:T(8,128)(2,1)S(1)}, u32[]{:S(2)}, u32[]{:S(2)}) collective-permute-start(bf16[41,16,128]{2,1,0:T(8,128)(2,1)S(1)} %get-tuple-element.19), channel_id=1, source_target_pairs={{0,3},{1,0},{2,1},{3,2},{4,7},{5,4},{6,5},{7,6},{8,11},{9,8},{10,9... | collective-permute-start | bytes 503816 | tf_op jit(solution)/shard_map/ppermute | solution.py:243
  31.5 2.4 %collective-permute-start.4 = (bf16[41,16,128]{2,1,0:T(8,128)(2,1)S(1)}, bf16[41,16,128]{2,1,0:T(8,128)(2,1)S(1)}, u32[]{:S(2)}, u32[]{:S(2)}) collective-permute-start(bf16[41,16,128]{2,1,0:T(8,128)(2,1)S(1)} %get-tuple-element.21), channel_id=1, source_target_pairs={{0,1},{1,2},{2,3},{3,0},{4,5},{5,6},{6,7},{7,4},{8,9},{9,10},{10,1... | collective-permute-start | bytes 503816 | tf_op jit(solution)/shard_map/ppermute | solution.py:243
  34.0 0.0 collective-permute-start.7
  34.0 2.0 %collective-permute-start.3 = (bf16[32,16,128]{2,1,0:T(8,128)(2,1)S(1)}, bf16[32,16,128]{2,1,0:T(8,128)(2,1)S(1)}, u32[]{:S(2)}, u32[]{:S(2)}) collective-permute-start(bf16[32,16,128]{2,1,0:T(8,128)(2,1)S(1)} %get-tuple-element.20), channel_id=1, source_target_pairs={{0,3},{1,0},{2,1},{3,2},{4,7},{5,4},{6,5},{7,6},{8,11},{9,8},{10,9... | collective-permute-start | bytes 393224 | tf_op jit(solution)/shard_map/ppermute | solution.py:243
  36.0 3.1 %collective-permute-done.2.right_1 = bf16[41,16,128]{2,1,0:T(8,128)(2,1)S(1)} collective-permute-done((bf16[41,16,128]{2,1,0:T(8,128)(2,1)S(1)}, bf16[41,16,128]{2,1,0:T(8,128)(2,1)S(1)}, u32[]{:S(2)}, u32[]{:S(2)}) %collective-permute-start.2) | collective-permute-done | bytes 167968 | tf_op jit(solution)/shard_map/ppermute | solution.py:243
  39.1 0.1 collective-permute-start.6
  39.1 0.0 collective-permute-done.4.left_1
  39.2 3.3 %collective-permute-start.5 = (bf16[32,16,128]{2,1,0:T(8,128)(2,1)S(1)}, bf16[32,16,128]{2,1,0:T(8,128)(2,1)S(1)}, u32[]{:S(2)}, u32[]{:S(2)}) collective-permute-start(bf16[32,16,128]{2,1,0:T(8,128)(2,1)S(1)} %slice.8), channel_id=1, source_target_pairs={{0,1},{1,2},{2,3},{3,0},{4,5},{5,6},{6,7},{7,4},{8,9},{9,10},{10,1... | collective-permute-start | bytes 393224 | tf_op jit(solution)/shard_map/ppermute | solution.py:243
  42.5 0.0 collective-permute-start.8
  42.5 5.5 %collective-permute-done.8.far_coef = bf16[9,16,128]{2,1,0:T(8,128)(2,1)S(1)} collective-permute-done((bf16[9,16,128]{2,1,0:T(8,128)(2,1)S(1)}, bf16[9,16,128]{2,1,0:T(8,128)(2,1)S(1)}, u32[]{:S(2)}, u32[]{:S(2)}) %collective-permute-start.8) | collective-permute-done | bytes 36896 | tf_op jit(solution)/shard_map/ppermute | solution.py:243
  47.9 0.0 collective-permute-done.7.left_2
  47.9 3.0 %shard_map.40 = (bf16[256,4096]{1,0:T(8,128)(2,1)}, bf16[32,128,128]{2,1,0:T(8,128)(2,1)S(1)}, bf16[128,128]{1,0:T(8,128)(2,1)S(1)}) custom-call(s32[1,1024]{1,0:T(1,128)S(1)} %get-tuple-element.16.near, bf16[32,48,128]{2,1,0:T(8,128)(2,1)S(1)} %all_to_all.5.received, f32[8,128]{1,0:T(8,128)S(1)} %get-tuple-element.18.coef_own, ...), custom_call_target="tpu_custom_call" | custom-call | flops 8000000 | bytes 800000 | tf_op jit(solution)/shard_map/pallas_call | solution.py:285
  51.0 0.0 collective-permute-done.6.far_2
  51.0 0.0 collective-permute-done.5.far_1
  51.0 2.5 %shard_map.41 = bf16[256,4096]{1,0:T(8,128)(2,1)} custom-call(s32[1,1024]{1,0:T(1,128)S(1)} %get-tuple-element.16.near, bf16[41,16,128]{2,1,0:T(8,128)(2,1)S(1)} %collective-permute-done.2.right_1, bf16[32,16,128]{2,1,0:T(8,128)(2,1)S(1)} %collective-permute-done.3.right_2, ...), custom_call_target="tpu_custom_call", output_to_operand_aliasing={{}: (7, {})} | custom-call | flops 3000000 | bytes 300000 | tf_op jit(solution)/shard_map/pallas_call | solution.py:293
  (3 shorter events, 0.0 us)
Async XLA Ops:
  0.0 1.8 %collective-permute-start.1 = (bf16[4,256]{1,0:T(4,128)(2,1)}, bf16[4,256]{1,0:T(4,128)(2,1)S(1)}, u32[]{:S(2)}, u32[]{:S(2)}) collective-permute-start(bf16[4,256]{1,0:T(4,128)(2,1)} %param.4), channel_id=1, source_target_pairs={{0,4},{4,0},{1,5},{5,1},{2,6},{6,2},{3,7},{7,3},{8,12},{12,8},{9,1... | collective-permute-start | bytes 6152 | tf_op jit(solution)/shard_map/ppermute | solution.py:247
  0.0 1.8 %collective-permute-start = (bf16[32,2048]{1,0:T(8,128)(2,1)}, bf16[32,2048]{1,0:T(8,128)(2,1)S(1)}, u32[]{:S(2)}, u32[]{:S(2)}) collective-permute-start(bf16[32,2048]{1,0:T(8,128)(2,1)} %param.3), channel_id=1, source_target_pairs={{0,4},{4,0},{1,5},{5,1},{2,6},{6,2},{3,7},{7,3},{8,12},{12,8},{9,1... | collective-permute-start | bytes 393224 | tf_op jit(solution)/shard_map/ppermute | solution.py:247
  30.6 8.4 %collective-permute-start.2 = (bf16[41,16,128]{2,1,0:T(8,128)(2,1)S(1)}, bf16[41,16,128]{2,1,0:T(8,128)(2,1)S(1)}, u32[]{:S(2)}, u32[]{:S(2)}) collective-permute-start(bf16[41,16,128]{2,1,0:T(8,128)(2,1)S(1)} %get-tuple-element.19), channel_id=1, source_target_pairs={{0,3},{1,0},{2,1},{3,2},{4,7},{5,4},{6,5},{7,6},{8,11},{9,8},{10,9... | collective-permute-start | bytes 503816 | tf_op jit(solution)/shard_map/ppermute | solution.py:243
  31.5 7.6 %collective-permute-start.4 = (bf16[41,16,128]{2,1,0:T(8,128)(2,1)S(1)}, bf16[41,16,128]{2,1,0:T(8,128)(2,1)S(1)}, u32[]{:S(2)}, u32[]{:S(2)}) collective-permute-start(bf16[41,16,128]{2,1,0:T(8,128)(2,1)S(1)} %get-tuple-element.21), channel_id=1, source_target_pairs={{0,1},{1,2},{2,3},{3,0},{4,5},{5,6},{6,7},{7,4},{8,9},{9,10},{10,1... | collective-permute-start | bytes 503816 | tf_op jit(solution)/shard_map/ppermute | solution.py:243
  34.0 14.0 %collective-permute-start.7 = (bf16[32,16,128]{2,1,0:T(8,128)(2,1)S(1)}, bf16[32,16,128]{2,1,0:T(8,128)(2,1)S(1)}, u32[]{:S(2)}, u32[]{:S(2)}) collective-permute-start(bf16[32,16,128]{2,1,0:T(8,128)(2,1)S(1)} %get-tuple-element.22), channel_id=1, source_target_pairs={{0,1},{1,2},{2,3},{3,0},{4,5},{5,6},{6,7},{7,4},{8,9},{9,10},{10,1... | collective-permute-start | bytes 393224 | tf_op jit(solution)/shard_map/ppermute | solution.py:243
  34.0 17.0 %collective-permute-start.3 = (bf16[32,16,128]{2,1,0:T(8,128)(2,1)S(1)}, bf16[32,16,128]{2,1,0:T(8,128)(2,1)S(1)}, u32[]{:S(2)}, u32[]{:S(2)}) collective-permute-start(bf16[32,16,128]{2,1,0:T(8,128)(2,1)S(1)} %get-tuple-element.20), channel_id=1, source_target_pairs={{0,3},{1,0},{2,1},{3,2},{4,7},{5,4},{6,5},{7,6},{8,11},{9,8},{10,9... | collective-permute-start | bytes 393224 | tf_op jit(solution)/shard_map/ppermute | solution.py:243
  39.1 11.9 %collective-permute-start.6 = (bf16[32,16,128]{2,1,0:T(8,128)(2,1)S(1)}, bf16[32,16,128]{2,1,0:T(8,128)(2,1)S(1)}, u32[]{:S(2)}, u32[]{:S(2)}) collective-permute-start(bf16[32,16,128]{2,1,0:T(8,128)(2,1)S(1)} %slice.9), channel_id=1, source_target_pairs={{0,3},{1,0},{2,1},{3,2},{4,7},{5,4},{6,5},{7,6},{8,11},{9,8},{10,9... | collective-permute-start | bytes 393224 | tf_op jit(solution)/shard_map/ppermute | solution.py:243
  39.2 11.8 %collective-permute-start.5 = (bf16[32,16,128]{2,1,0:T(8,128)(2,1)S(1)}, bf16[32,16,128]{2,1,0:T(8,128)(2,1)S(1)}, u32[]{:S(2)}, u32[]{:S(2)}) collective-permute-start(bf16[32,16,128]{2,1,0:T(8,128)(2,1)S(1)} %slice.8), channel_id=1, source_target_pairs={{0,1},{1,2},{2,3},{3,0},{4,5},{5,6},{6,7},{7,4},{8,9},{9,10},{10,1... | collective-permute-start | bytes 393224 | tf_op jit(solution)/shard_map/ppermute | solution.py:243
  42.5 5.5 %collective-permute-start.8 = (bf16[9,16,128]{2,1,0:T(8,128)(2,1)S(1)}, bf16[9,16,128]{2,1,0:T(8,128)(2,1)S(1)}, u32[]{:S(2)}, u32[]{:S(2)}) collective-permute-start(bf16[9,16,128]{2,1,0:T(8,128)(2,1)S(1)} %get-tuple-element.23), channel_id=1, source_target_pairs={{0,2},{1,3},{2,0},{3,1},{4,6},{5,7},{6,4},{7,5},{8,10},{9,11},{10,... | collective-permute-start | bytes 110600 | tf_op jit(solution)/shard_map/ppermute | solution.py:243

commit v7 on v6

--- a/solution.py
+++ b/solution.py
@@ -35,12 +35,18 @@
         block = rows[:32, b * LANES : (b + 1) * LANES].astype(F32)
         for s in range(8):
             turned = pltpu.roll(block, s * PAIRS, 1) if s else block
-            copies[s, b] = turned.astype(BF16)
-
-
-def own_kernel(fetched, copies, near, coef):
-    near[...] = fetched[32:33, :FINE].astype(jnp.int32)
-    coef[...] = halves_stacked(fetched[40:44, : 2 * LANES])
+            copies[s * 16 + b] = turned.astype(BF16)
+
+
+def halves_stacked(coef):
+    return jnp.concatenate([coef[:, :LANES], coef[:, LANES:]], axis=0)
+
+
+def own_kernel(fetched, copies, near, slots, coef):
+    c = fetched[32:33, :FINE].astype(jnp.int32)
+    near[...] = c
+    slots[...] = ((iota((1, FINE), 1) % POINTS - c) & 7) * 16 + (c >> 3)
+    coef[...] = halves_stacked(fetched[40:44, : 2 * LANES]).astype(BF16)
     turn_rows(fetched, copies)
 
 
@@ -48,16 +54,13 @@
     return pltpu.make_async_copy(near, scalars, sem.at[0])
 
 
-def pack_kernel(near, own_copies, other, coef_own, coef_other, out, other_copies, scalars, sem):
-    fetch = index_copy(near, scalars, sem)
+def pack_kernel(slots, own_copies, other, coef, out, other_copies, scalars, sem):
+    fetch = index_copy(slots, scalars, sem)
     fetch.start()
     kc = lax.axis_index("kc")
     core = lax.axis_index("kf_2")
     turn_rows(other, other_copies)
     copies = (own_copies, other_copies)
-    a = coef_own[...]
-    o = halves_stacked(coef_other[...].astype(F32))
-    coef = jnp.concatenate([jnp.where(core == 0, a, o), jnp.where(core == 0, o, a)], axis=0).astype(BF16)
     fetch.wait()
     group = iota((PAIRS, LANES), 1) // PAIRS
     base = 16 * core + 4 * kc
@@ -65,41 +68,52 @@
     def body(d, carry):
         tiles = [None, None]
         for j in range(POINTS):
-            c = scalars[0, 32 * d + base + j]
+            slot = scalars[0, 32 * d + base + j]
             for lo in range(2):
-                at = lo * POINTS + j
                 for n in range(2):
-                    piece = copies[n][(at - c) & 7, c >> 3, lo * PAIRS : (lo + 1) * PAIRS, :]
-                    tiles[n] = piece if tiles[n] is None else jnp.where(group == at, piece, tiles[n])
+                    piece = copies[n][slot ^ (64 * lo), lo * PAIRS : (lo + 1) * PAIRS, :]
+                    tiles[n] = piece if tiles[n] is None else jnp.where(group == lo * POINTS + j, piece, tiles[n])
         out[d, pl.ds(pl.multiple_of(core * PAIRS, PAIRS), PAIRS), :] = tiles[0]
         out[d, pl.ds(pl.multiple_of((1 - core) * PAIRS, PAIRS), PAIRS), :] = tiles[1]
-        out[d, 2 * PAIRS :, :] = coef
+        out[d, 2 * PAIRS :, :] = coef[...]
         return carry
 
     lax.fori_loop(0, PEERS, body, 0, unroll=4)
 
 
-def split_kernel(received, coef_own, up_1, up_2, down_1, down_2, across):
+def row_block(received, n):
+    return received[n // 2, n % 2 * PAIRS : (n % 2 + 1) * PAIRS, :]
+
+
+def first_split_kernel(received, coef_own, up_1, coef_half):
+    for n in range(48):
+        up_1[n] = row_block(received, n)
+    mine = coef_own[...].astype(F32)
+    up_1[48] = jnp.concatenate([mine, mine], axis=0).astype(BF16)
+    for d in range(PEERS):
+        coef_half[d] = received[d, 2 * PAIRS :, :]
+
+
+def second_split_kernel(received, coef_half, coef_other, coef_own, up_2, down_1, down_2, across, home):
     kc = lax.axis_index("kc")
-    mine = coef_own[...]
-    mine = jnp.concatenate([mine, jnp.zeros_like(mine)], axis=0).astype(BF16)
-    for n in range(64):
-        block = received[n // 2, n % 2 * PAIRS : (n % 2 + 1) * PAIRS, :]
-        if n < 32:
-            up_1[n] = block
-            down_2[n] = block
-        else:
-            up_2[n - 32] = block
-            down_1[n - 32] = block
-    for step, target, at in ((1, up_1, 32), (3, down_1, 32), (2, across, 0)):
+    core = lax.axis_index("kf_2")
+    for n in range(16):
+        up_2[n] = row_block(received, 48 + n)
+        down_2[n] = row_block(received, n)
+        down_1[32 + n] = row_block(received, 16 + n)
+    for n in range(32):
+        down_1[n] = row_block(received, 32 + n)
+    for step, target, at in ((0, home, 0), (1, up_2, 16), (3, down_1, 48), (2, across, 0)):
         first = (kc + step) % 4 * 8
         for p in range(8):
-            target[at + p] = received[first + p, 2 * PAIRS :, :]
-        target[at + 8] = mine
-
-
-def halves_stacked(coef):
-    return jnp.concatenate([coef[:, :LANES], coef[:, LANES:]], axis=0)
+            a = coef_half[first + p].astype(F32)
+            o = coef_other[first + p].astype(F32)
+            both = jnp.concatenate([jnp.where(core == 0, a, o), jnp.where(core == 0, o, a)], axis=0)
+            target[at + p] = both.astype(BF16)
+    mine = coef_own[...].astype(F32)
+    mine = jnp.concatenate([mine, mine], axis=0).astype(BF16)
+    down_1[56] = mine
+    across[8] = mine
 
 
 def spread(row_of, count):
@@ -143,7 +157,7 @@
 
 
 def middle_kernel(
-    near, received, coef_own, left_1, left_2, right_1, far_coef, out, cols, turn_far,
+    near, received, coef_own, home, left_1, left_2, right_1, far_coef, out, cols, turn_far,
     pieces, pairs, diag, picked, turned, result, scalars, sem
 ):
     fetch = index_copy(near, scalars, sem)
@@ -162,17 +176,15 @@
 
         return jnp.dot(spread(row_of, 8), repeat, preferred_element_type=F32).astype(BF16) * diag[...]
 
-    turn = turn_of(coef_own[...], left_1[40].astype(F32))
-    turn_far[...] = turn_of(right_1[40].astype(F32), far_coef[8].astype(F32))
+    turn = turn_of(coef_own[...].astype(F32), left_1[48].astype(F32))
+    turn_far[...] = turn_of(right_1[56].astype(F32), far_coef[8].astype(F32))
     for p in range(8):
-        pieces[kc, p] = received[kc * 8 + p, 2 * PAIRS :, :].astype(F32)
-        pieces[(kc + 3) % 4, p] = left_1[32 + p].astype(F32)
-        pieces[(kc + 1) % 4, p] = right_1[32 + p].astype(F32)
+        pieces[kc, p] = home[p].astype(F32)
+        pieces[(kc + 3) % 4, p] = left_2[16 + p].astype(F32)
+        pieces[(kc + 1) % 4, p] = right_1[48 + p].astype(F32)
         pieces[(kc + 2) % 4, p] = far_coef[p].astype(F32)
     pair_blocks(
-        lambda n: received[n // 2, n % 2 * PAIRS : (n % 2 + 1) * PAIRS, :],
-        lambda n: left_1[n] if n < 32 else left_2[n - 32],
-        pairs,
+        lambda n: row_block(received, n), lambda n: left_1[n] if n < 48 else left_2[n - 48], pairs
     )
 
     def build(v):
@@ -206,7 +218,7 @@
     fetch.start()
     kc = lax.axis_index("kc")
     pair_blocks(
-        lambda n: right_2[n] if n < 32 else right_1[n - 32], lambda n: far_1[n] if n < 32 else far_2[n - 32], pairs
+        lambda n: right_2[n] if n < 16 else right_1[n + 16 if n < 32 else n - 32], lambda n: far_1[n] if n < 32 else far_2[n - 32], pairs
     )
     turn = turn_far[...]
     fetch.wait()
@@ -249,30 +261,29 @@
 
 def shards(kernel_coarse, coefficients, nearest):
     other = partner(kernel_coarse)
-    coef_other = partner(coefficients)
-    rotations = (8, 16, 32, LANES)
+    rotations = (128, 32, LANES)
+    block = (PAIRS, LANES)
     table = jnp.pad(nearest.reshape(1, FINE), ((32, 15), (0, FINE))).astype(F32)
     rows = jnp.pad(coefficients.astype(F32), ((40, 4), (0, 2 * FINE - 2 * LANES)))
     fetched = jnp.pad(kernel_coarse.astype(F32), ((0, 16), (0, 0))) + table + rows
     scalars = [pltpu.SMEM((1, FINE), jnp.int32), pltpu.SemaphoreType.DMA((9,))]
-    own_copies, near, coef_own = call(
-        own_kernel,
-        (shape(*rotations), jax.ShapeDtypeStruct((1, FINE), jnp.int32), jax.ShapeDtypeStruct((8, LANES), F32)),
-        [VMEM],
-        (VMEM,) * 3,
-        [],
-        1000000,
+    index = jax.ShapeDtypeStruct((1, FINE), jnp.int32)
+    own_copies, near, slots, coef_own = call(
+        own_kernel, (shape(*rotations), index, index, shape(8, LANES)), [VMEM], (VMEM,) * 4, [], 1000000
     )(fetched)
     packed = call(
-        pack_kernel, shape(PEERS, 48, LANES), [VMEM] * 5, VMEM, [pltpu.VMEM(rotations, BF16)] + scalars, 1000000
-    )(near, own_copies, other, coef_own, coef_other)
+        pack_kernel, shape(PEERS, 40, LANES), [VMEM] * 4, VMEM, [pltpu.VMEM(rotations, BF16)] + scalars, 1000000
+    )(slots, own_copies, other, coef_own)
     received = lax.all_to_all(packed, ZY, split_axis=0, concat_axis=0, tiled=True)
-    block = (PAIRS, LANES)
-    sizes = (41, 32, 41, 32, 9)
-    up_1, up_2, down_1, down_2, across = call(
-        split_kernel, tuple(shape(n, *block) for n in sizes), [VMEM, VMEM], (VMEM,) * 5, [], 100000
+    up_1, coef_half = call(
+        first_split_kernel, (shape(49, *block), shape(PEERS, 8, LANES)), [VMEM] * 2, (VMEM,) * 2, [], 100000
     )(received, coef_own)
+    coef_other = partner(coef_half)
     left_1 = shift(up_1, 1)
+    sizes = (24, 57, 16, 9, 8)
+    up_2, down_1, down_2, across, home = call(
+        second_split_kernel, tuple(shape(n, *block) for n in sizes), [VMEM] * 4, (VMEM,) * 5, [], 100000
+    )(received, coef_half, coef_other, coef_own)
     right_1 = shift(down_1, -1)
     far_coef = shift(across, 2)
     left_2 = shift(up_2, 1)
@@ -285,11 +296,11 @@
     partial, cols, turn_far = call(
         middle_kernel,
         (shape(256, 4096), shape(32, LANES, LANES), shape(LANES, LANES)),
-        [VMEM] * 7,
+        [VMEM] * 8,
         (ANY, VMEM, VMEM),
         [pltpu.VMEM((4, 8, *block), F32), pairs, pltpu.VMEM((LANES, LANES), BF16), picked, turned, turned] + scalars,
         8000000,
-    )(near, received, coef_own, left_1, left_2, right_1, far_coef)
+    )(near, received, coef_own, home, left_1, left_2, right_1, far_coef)
     return call(
         last_kernel,
         shape(256, 4096),

time: 53.6 us -> 57.9 us (1.080)
  the two profiles are of different devices: /device:TPU:6 before, /device:TPU:32 now
where the time goes in v7:
time: 57.9 us; the launch traced here: 57.8 us
  blocking collectives  24.9 us (43%)
  waiting for transfers between devices  15 us (26%)
  starting transfers between devices  9.54 us (16%)
  Pallas kernels  7.27 us (13%)
  other arithmetic  0.96 us (2%)
    all_to_all x1, blocking collectives, shards(): lax.all_to_all(packed, ZY, split_axis=0, concat_axis=0, tiled=True)  24.9 us
    ppermute x7, waiting for transfers between devices, shift(): return lax.ppermute(value, 'kc', [(i, (i + by) % 4) for i in range(4)])  13.5 us
    ppermute x7, starting transfers between devices, shift(): return lax.ppermute(value, 'kc', [(i, (i + by) % 4) for i in range(4)])  9.45 us
    pallas_call x1, Pallas kernels, shards(): call(middle_kernel, (shape(256, 4096), shape(32, LANES, LANES), shape(LAN...  3 us
    pallas_call x1, Pallas kernels, shards(): call(last_kernel, shape(256, 4096), [VMEM] * 7 + [ANY], ANY, [pairs, pick...  2.52 us
    ppermute x2, waiting for transfers between devices, partner(): return lax.ppermute(value, 'kf_2', [(0, 1), (1, 0)])  1.52 us
    pallas_call x1, Pallas kernels, shards(): call(pack_kernel, shape(PEERS, 40, LANES), [VMEM] * 4, VMEM, [pltpu.VMEM(...  1.37 us
  transfers between devices with their start and end apart: 9, of which 4 were waited for; matrix products, arithmetic and copies ran while one was open for 2% of the time, Pallas kernels for 6%

profile of v7, /device:TPU:32, one launch (start us, length us, event | category | flops | bytes accessed | tf_op | source)
XLA Modules:
  0.0 57.8 jit_solution(3656627907656448657)
XLA Ops:
  0.0 0.0 collective-permute-start
  0.0 1.0 %convert_add_fusion.fetched = f32[48,2048]{1,0:T(8,128)S(1)} fusion(s32[1,1024]{1,0:T(1,128)} %bitcast.1, bf16[4,256]{1,0:T(4,128)(2,1)} %param.4, bf16[32,2048]{1,0:T(8,128)(2,1)} %param.3), kind=kLoop, calls=%fused_computation | loop fusion | flops 491520 | bytes 530432 | tf_op jit(solution)/shard_map/add | solution.py:268
  1.0 0.3 shard_map.37
  1.3 0.3 collective-permute-done.other
  1.6 1.4 %shard_map.38 = bf16[32,40,128]{2,1,0:T(8,128)(2,1)S(1)} custom-call(s32[1,1024]{1,0:T(1,128)S(1)} %get-tuple-element.20.slots, bf16[128,32,128]{2,1,0:T(8,128)(2,1)S(1)} %get-tuple-element.21.own_copies, bf16[32,2048]{1,0:T(8,128)(2,1)S(1)} %collective-permute-done.other, bf16[8,128]{1,0:T(8,128)(2,1)S(1)} %get-tuple-element.22.coef.coef_own), custom_call_target="tpu_custom_call" | custom-call | flops 1000000 | bytes 100000 | tf_op jit(solution)/shard_map/pallas_call | solution.py:274
  2.9 24.9 %all_to_all.5.received = bf16[32,40,128]{2,1,0:T(8,128)(2,1)S(1)} all-to-all(bf16[32,40,128]{2,1,0:T(8,128)(2,1)S(1)} %shard_map.38), channel_id=1, replica_groups=mesh['kf_0'=8,'kf_1'=4,'kf_2'=2,'kc'=4] {'kf_0','kf_1'}, dimensions={0} | all-to-all | bytes 655360 | tf_op jit(solution)/shard_map/all_to_all | solution.py:277
  27.9 0.1 collective-permute-start.1
  28.0 1.2 %collective-permute-done.1.coef_other = bf16[32,8,128]{2,1,0:T(8,128)(2,1)S(1)} collective-permute-done((bf16[32,8,128]{2,1,0:T(8,128)(2,1)S(1)}, bf16[32,8,128]{2,1,0:T(8,128)(2,1)S(1)}, u32[]{:S(2)}, u32[]{:S(2)}) %collective-permute-start.1) | collective-permute-done | bytes 65568 | tf_op jit(solution)/shard_map/ppermute | solution.py:259
  29.3 0.1 shard_map.40
  29.3 2.8 %collective-permute-start.2 = (bf16[57,16,128]{2,1,0:T(8,128)(2,1)S(1)}, bf16[57,16,128]{2,1,0:T(8,128)(2,1)S(1)}, u32[]{:S(2)}, u32[]{:S(2)}) collective-permute-start(bf16[57,16,128]{2,1,0:T(8,128)(2,1)S(1)} %get-tuple-element.24), channel_id=1, source_target_pairs={{0,3},{1,0},{2,1},{3,2},{4,7},{5,4},{6,5},{7,6},{8,11},{9,8},{10,9... | collective-permute-start | bytes 700424 | tf_op jit(solution)/shard_map/ppermute | solution.py:255
  32.1 0.0 collective-permute-start.4
  32.1 8.0 %collective-permute-done.4.left_1 = bf16[49,16,128]{2,1,0:T(8,128)(2,1)S(1)} collective-permute-done((bf16[49,16,128]{2,1,0:T(8,128)(2,1)S(1)}, bf16[49,16,128]{2,1,0:T(8,128)(2,1)S(1)}, u32[]{:S(2)}, u32[]{:S(2)}) %collective-permute-start.4) | collective-permute-done | bytes 200736 | tf_op jit(solution)/shard_map/ppermute | solution.py:255
  40.1 0.1 collective-permute-start.5
  40.2 0.0 collective-permute-done.2.right_1
  40.3 3.3 %collective-permute-start.6 = (bf16[32,16,128]{2,1,0:T(8,128)(2,1)S(1)}, bf16[32,16,128]{2,1,0:T(8,128)(2,1)S(1)}, u32[]{:S(2)}, u32[]{:S(2)}) collective-permute-start(bf16[32,16,128]{2,1,0:T(8,128)(2,1)S(1)} %slice.9), channel_id=1, source_target_pairs={{0,3},{1,0},{2,1},{3,2},{4,7},{5,4},{6,5},{7,6},{8,11},{9,8},{10,9... | collective-permute-start | bytes 393224 | tf_op jit(solution)/shard_map/ppermute | solution.py:255
  43.5 0.0 collective-permute-start.7
  43.6 3.2 %collective-permute-start.3 = (bf16[16,16,128]{2,1,0:T(8,128)(2,1)S(1)}, bf16[16,16,128]{2,1,0:T(8,128)(2,1)S(1)}, u32[]{:S(2)}, u32[]{:S(2)}) collective-permute-start(bf16[16,16,128]{2,1,0:T(8,128)(2,1)S(1)} %get-tuple-element.25), channel_id=1, source_target_pairs={{0,3},{1,0},{2,1},{3,2},{4,7},{5,4},{6,5},{7,6},{8,11},{9,8},{10,9... | collective-permute-start | bytes 196616 | tf_op jit(solution)/shard_map/ppermute | solution.py:255
  46.8 0.0 collective-permute-start.8
  46.8 5.5 %collective-permute-done.8.far_coef = bf16[9,16,128]{2,1,0:T(8,128)(2,1)S(1)} collective-permute-done((bf16[9,16,128]{2,1,0:T(8,128)(2,1)S(1)}, bf16[9,16,128]{2,1,0:T(8,128)(2,1)S(1)}, u32[]{:S(2)}, u32[]{:S(2)}) %collective-permute-start.8) | collective-permute-done | bytes 36896 | tf_op jit(solution)/shard_map/ppermute | solution.py:255
  52.2 0.0 collective-permute-done.7.left_2
  52.3 3.0 %shard_map.41 = (bf16[256,4096]{1,0:T(8,128)(2,1)}, bf16[32,128,128]{2,1,0:T(8,128)(2,1)S(1)}, bf16[128,128]{1,0:T(8,128)(2,1)S(1)}) custom-call(s32[1,1024]{1,0:T(1,128)S(1)} %get-tuple-element.19.near, bf16[32,40,128]{2,1,0:T(8,128)(2,1)S(1)} %all_to_all.5.received, bf16[8,128]{1,0:T(8,128)(2,1)S(1)} %get-tuple-element.22.coef.coef_own, ...), custom_call_target="tpu_custom_call" | custom-call | flops 8000000 | bytes 800000 | tf_op jit(solution)/shard_map/pallas_call | solution.py:296
  55.3 0.0 collective-permute-done.3.right_2
  55.3 0.0 collective-permute-done.6.far_2
  55.3 2.5 %shard_map.42 = bf16[256,4096]{1,0:T(8,128)(2,1)} custom-call(s32[1,1024]{1,0:T(1,128)S(1)} %get-tuple-element.19.near, bf16[57,16,128]{2,1,0:T(8,128)(2,1)S(1)} %collective-permute-done.2.right_1, bf16[16,16,128]{2,1,0:T(8,128)(2,1)S(1)} %collective-permute-done.3.right_2, ...), custom_call_target="tpu_custom_call", output_to_operand_aliasing={{}: (7, {})} | custom-call | flops 3000000 | bytes 300000 | tf_op jit(solution)/shard_map/pallas_call | solution.py:304
  (4 shorter events, 0.0 us)
Async XLA Ops:
  0.0 1.6 %collective-permute-start = (bf16[32,2048]{1,0:T(8,128)(2,1)}, bf16[32,2048]{1,0:T(8,128)(2,1)S(1)}, u32[]{:S(2)}, u32[]{:S(2)}) collective-permute-start(bf16[32,2048]{1,0:T(8,128)(2,1)} %param.3), channel_id=1, source_target_pairs={{0,4},{4,0},{1,5},{5,1},{2,6},{6,2},{3,7},{7,3},{8,12},{12,8},{9,1... | collective-permute-start | bytes 393224 | tf_op jit(solution)/shard_map/ppermute | solution.py:259
  27.9 1.3 %collective-permute-start.1 = (bf16[32,8,128]{2,1,0:T(8,128)(2,1)S(1)}, bf16[32,8,128]{2,1,0:T(8,128)(2,1)S(1)}, u32[]{:S(2)}, u32[]{:S(2)}) collective-permute-start(bf16[32,8,128]{2,1,0:T(8,128)(2,1)S(1)} %get-tuple-element.23.coef_half), channel_id=1, source_target_pairs={{0,4},{4,0},{1,5},{5,1},{2,6},{6,2},{3,7},{7,3},{8,12},{12,8},{9,1... | collective-permute-start | bytes 196616 | tf_op jit(solution)/shard_map/ppermute | solution.py:259
  29.3 10.9 %collective-permute-start.2 = (bf16[57,16,128]{2,1,0:T(8,128)(2,1)S(1)}, bf16[57,16,128]{2,1,0:T(8,128)(2,1)S(1)}, u32[]{:S(2)}, u32[]{:S(2)}) collective-permute-start(bf16[57,16,128]{2,1,0:T(8,128)(2,1)S(1)} %get-tuple-element.24), channel_id=1, source_target_pairs={{0,3},{1,0},{2,1},{3,2},{4,7},{5,4},{6,5},{7,6},{8,11},{9,8},{10,9... | collective-permute-start | bytes 700424 | tf_op jit(solution)/shard_map/ppermute | solution.py:255
  32.1 8.0 %collective-permute-start.4 = (bf16[49,16,128]{2,1,0:T(8,128)(2,1)S(1)}, bf16[49,16,128]{2,1,0:T(8,128)(2,1)S(1)}, u32[]{:S(2)}, u32[]{:S(2)}) collective-permute-start(bf16[49,16,128]{2,1,0:T(8,128)(2,1)S(1)} %get-tuple-element.26), channel_id=1, source_target_pairs={{0,1},{1,2},{2,3},{3,0},{4,5},{5,6},{6,7},{7,4},{8,9},{9,10},{10,1... | collective-permute-start | bytes 602120 | tf_op jit(solution)/shard_map/ppermute | solution.py:255
  40.1 15.1 %collective-permute-start.5 = (bf16[32,16,128]{2,1,0:T(8,128)(2,1)S(1)}, bf16[32,16,128]{2,1,0:T(8,128)(2,1)S(1)}, u32[]{:S(2)}, u32[]{:S(2)}) collective-permute-start(bf16[32,16,128]{2,1,0:T(8,128)(2,1)S(1)} %slice.8), channel_id=1, source_target_pairs={{0,1},{1,2},{2,3},{3,0},{4,5},{5,6},{6,7},{7,4},{8,9},{9,10},{10,1... | collective-permute-start | bytes 393224 | tf_op jit(solution)/shard_map/ppermute | solution.py:255
  40.3 15.0 %collective-permute-start.6 = (bf16[32,16,128]{2,1,0:T(8,128)(2,1)S(1)}, bf16[32,16,128]{2,1,0:T(8,128)(2,1)S(1)}, u32[]{:S(2)}, u32[]{:S(2)}) collective-permute-start(bf16[32,16,128]{2,1,0:T(8,128)(2,1)S(1)} %slice.9), channel_id=1, source_target_pairs={{0,3},{1,0},{2,1},{3,2},{4,7},{5,4},{6,5},{7,6},{8,11},{9,8},{10,9... | collective-permute-start | bytes 393224 | tf_op jit(solution)/shard_map/ppermute | solution.py:255
  43.5 8.7 %collective-permute-start.7 = (bf16[24,16,128]{2,1,0:T(8,128)(2,1)S(1)}, bf16[24,16,128]{2,1,0:T(8,128)(2,1)S(1)}, u32[]{:S(2)}, u32[]{:S(2)}) collective-permute-start(bf16[24,16,128]{2,1,0:T(8,128)(2,1)S(1)} %get-tuple-element.28), channel_id=1, source_target_pairs={{0,1},{1,2},{2,3},{3,0},{4,5},{5,6},{6,7},{7,4},{8,9},{9,10},{10,1... | collective-permute-start | bytes 294920 | tf_op jit(solution)/shard_map/ppermute | solution.py:255
  43.6 11.7 %collective-permute-start.3 = (bf16[16,16,128]{2,1,0:T(8,128)(2,1)S(1)}, bf16[16,16,128]{2,1,0:T(8,128)(2,1)S(1)}, u32[]{:S(2)}, u32[]{:S(2)}) collective-permute-start(bf16[16,16,128]{2,1,0:T(8,128)(2,1)S(1)} %get-tuple-element.25), channel_id=1, source_target_pairs={{0,3},{1,0},{2,1},{3,2},{4,7},{5,4},{6,5},{7,6},{8,11},{9,8},{10,9... | collective-permute-start | bytes 196616 | tf_op jit(solution)/shard_map/ppermute | solution.py:255
  46.8 5.5 %collective-permute-start.8 = (bf16[9,16,128]{2,1,0:T(8,128)(2,1)S(1)}, bf16[9,16,128]{2,1,0:T(8,128)(2,1)S(1)}, u32[]{:S(2)}, u32[]{:S(2)}) collective-permute-start(bf16[9,16,128]{2,1,0:T(8,128)(2,1)S(1)} %get-tuple-element.29), channel_id=1, source_target_pairs={{0,2},{1,3},{2,0},{3,1},{4,6},{5,7},{6,4},{7,5},{8,10},{9,11},{10,... | collective-permute-start | bytes 110600 | tf_op jit(solution)/shard_map/ppermute | solution.py:255

commit v8 on v7

--- a/solution.py
+++ b/solution.py
@@ -85,35 +85,35 @@
     return received[n // 2, n % 2 * PAIRS : (n % 2 + 1) * PAIRS, :]
 
 
-def first_split_kernel(received, coef_own, up_1, coef_half):
-    for n in range(48):
+def row_coefficients(coef_own):
+    mine = coef_own[...].astype(F32)
+    return jnp.concatenate([mine, mine], axis=0).astype(BF16)
+
+
+def put_pieces(received, kc, target, at):
+    for p in range(8):
+        target[at + p // 2, p % 2 * 8 : p % 2 * 8 + 8, :] = received[kc * 8 + p, 2 * PAIRS :, :]
+
+
+def split_kernel(received, coef_own, up_1, up_2, down_1, down_2, across):
+    kc = lax.axis_index("kc")
+    mine = row_coefficients(coef_own)
+    for n in range(32):
         up_1[n] = row_block(received, n)
-    mine = coef_own[...].astype(F32)
-    up_1[48] = jnp.concatenate([mine, mine], axis=0).astype(BF16)
-    for d in range(PEERS):
-        coef_half[d] = received[d, 2 * PAIRS :, :]
-
-
-def second_split_kernel(received, coef_half, coef_other, coef_own, up_2, down_1, down_2, across, home):
-    kc = lax.axis_index("kc")
-    core = lax.axis_index("kf_2")
-    for n in range(16):
-        up_2[n] = row_block(received, 48 + n)
         down_2[n] = row_block(received, n)
-        down_1[32 + n] = row_block(received, 16 + n)
-    for n in range(32):
+        up_2[n] = row_block(received, 32 + n)
         down_1[n] = row_block(received, 32 + n)
-    for step, target, at in ((0, home, 0), (1, up_2, 16), (3, down_1, 48), (2, across, 0)):
-        first = (kc + step) % 4 * 8
-        for p in range(8):
-            a = coef_half[first + p].astype(F32)
-            o = coef_other[first + p].astype(F32)
-            both = jnp.concatenate([jnp.where(core == 0, a, o), jnp.where(core == 0, o, a)], axis=0)
-            target[at + p] = both.astype(BF16)
-    mine = coef_own[...].astype(F32)
-    mine = jnp.concatenate([mine, mine], axis=0).astype(BF16)
-    down_1[56] = mine
-    across[8] = mine
+    for step, target, at in ((1, up_1, 32), (3, down_1, 32), (2, across, 0)):
+        put_pieces(received, (kc + step) % 4, target, at)
+        target[at + 4] = mine
+
+
+def collect_kernel(received, left_1, right_1, far_coef, collected):
+    put_pieces(received, lax.axis_index("kc"), collected, 0)
+    for n in range(4):
+        collected[4 + n] = left_1[32 + n]
+        collected[8 + n] = right_1[32 + n]
+        collected[12 + n] = far_coef[n]
 
 
 def spread(row_of, count):
@@ -157,7 +157,7 @@
 
 
 def middle_kernel(
-    near, received, coef_own, home, left_1, left_2, right_1, far_coef, out, cols, turn_far,
+    near, received, coef_own, coef_half, coef_other, left_1, left_2, right_1, far_coef, out, cols, turn_far,
     pieces, pairs, diag, picked, turned, result, scalars, sem
 ):
     fetch = index_copy(near, scalars, sem)
@@ -176,15 +176,16 @@
 
         return jnp.dot(spread(row_of, 8), repeat, preferred_element_type=F32).astype(BF16) * diag[...]
 
-    turn = turn_of(coef_own[...].astype(F32), left_1[48].astype(F32))
-    turn_far[...] = turn_of(right_1[56].astype(F32), far_coef[8].astype(F32))
-    for p in range(8):
-        pieces[kc, p] = home[p].astype(F32)
-        pieces[(kc + 3) % 4, p] = left_2[16 + p].astype(F32)
-        pieces[(kc + 1) % 4, p] = right_1[48 + p].astype(F32)
-        pieces[(kc + 2) % 4, p] = far_coef[p].astype(F32)
+    turn = turn_of(coef_own[...].astype(F32), left_1[36].astype(F32))
+    turn_far[...] = turn_of(right_1[36].astype(F32), far_coef[4].astype(F32))
+    core = lax.axis_index("kf_2")
+    for n, step in enumerate((0, 3, 1, 2)):
+        for p in range(8):
+            for owner, source in ((core, coef_half), (1 - core, coef_other)):
+                piece = source[4 * n + p // 2, p % 2 * 8 : p % 2 * 8 + 8, :].astype(F32)
+                pieces[(kc + step) % 4, p, pl.ds(pl.multiple_of(owner * 8, 8), 8), :] = piece
     pair_blocks(
-        lambda n: row_block(received, n), lambda n: left_1[n] if n < 48 else left_2[n - 48], pairs
+        lambda n: row_block(received, n), lambda n: left_1[n] if n < 32 else left_2[n - 32], pairs
     )
 
     def build(v):
@@ -218,7 +219,7 @@
     fetch.start()
     kc = lax.axis_index("kc")
     pair_blocks(
-        lambda n: right_2[n] if n < 16 else right_1[n + 16 if n < 32 else n - 32], lambda n: far_1[n] if n < 32 else far_2[n - 32], pairs
+        lambda n: right_2[n] if n < 32 else right_1[n - 32], lambda n: far_1[n] if n < 32 else far_2[n - 32], pairs
     )
     turn = turn_far[...]
     fetch.wait()
@@ -275,32 +276,30 @@
         pack_kernel, shape(PEERS, 40, LANES), [VMEM] * 4, VMEM, [pltpu.VMEM(rotations, BF16)] + scalars, 1000000
     )(slots, own_copies, other, coef_own)
     received = lax.all_to_all(packed, ZY, split_axis=0, concat_axis=0, tiled=True)
-    up_1, coef_half = call(
-        first_split_kernel, (shape(49, *block), shape(PEERS, 8, LANES)), [VMEM] * 2, (VMEM,) * 2, [], 100000
+    sizes = (37, 32, 37, 32, 5)
+    up_1, up_2, down_1, down_2, across = call(
+        split_kernel, tuple(shape(n, *block) for n in sizes), [VMEM] * 2, (VMEM,) * 5, [], 100000
     )(received, coef_own)
-    coef_other = partner(coef_half)
     left_1 = shift(up_1, 1)
-    sizes = (24, 57, 16, 9, 8)
-    up_2, down_1, down_2, across, home = call(
-        second_split_kernel, tuple(shape(n, *block) for n in sizes), [VMEM] * 4, (VMEM,) * 5, [], 100000
-    )(received, coef_half, coef_other, coef_own)
     right_1 = shift(down_1, -1)
     far_coef = shift(across, 2)
     left_2 = shift(up_2, 1)
     right_2 = shift(down_2, -1)
     far_1 = shift(left_1[:PEERS], 1)
     far_2 = shift(right_1[:PEERS], -1)
+    coef_half = call(collect_kernel, shape(16, *block), [VMEM] * 4, VMEM, [], 100000)(received, left_1, right_1, far_coef)
+    coef_other = partner(coef_half)
     pairs = pltpu.VMEM((128, *block), BF16)
     picked = pltpu.VMEM((2, 1024, LANES), BF16)
     turned = pltpu.VMEM((LANES, 4096), BF16)
     partial, cols, turn_far = call(
         middle_kernel,
         (shape(256, 4096), shape(32, LANES, LANES), shape(LANES, LANES)),
-        [VMEM] * 8,
+        [VMEM] * 9,
         (ANY, VMEM, VMEM),
         [pltpu.VMEM((4, 8, *block), F32), pairs, pltpu.VMEM((LANES, LANES), BF16), picked, turned, turned] + scalars,
         8000000,
-    )(near, received, coef_own, home, left_1, left_2, right_1, far_coef)
+    )(near, received, coef_own, coef_half, coef_other, left_1, left_2, right_1, far_coef)
     return call(
         last_kernel,
         shape(256, 4096),

time: 57.9 us -> 53.7 us (0.927)
  the two profiles are of different devices: /device:TPU:32 before, /device:TPU:6 now
where the time goes in v8:
time: 53.7 us; the launch traced here: 52.7 us
  blocking collectives  25.9 us (48%)
  waiting for transfers between devices  9.56 us (18%)
  starting transfers between devices  8.81 us (16%)
  Pallas kernels  7.33 us (14%)
  other arithmetic  0.96 us (2%)
    all_to_all x1, blocking collectives, shards(): lax.all_to_all(packed, ZY, split_axis=0, concat_axis=0, tiled=True)  25.9 us
    ppermute x7, starting transfers between devices, shift(): return lax.ppermute(value, 'kc', [(i, (i + by) % 4) for i in range(4)])  8.71 us
    ppermute x7, waiting for transfers between devices, shift(): return lax.ppermute(value, 'kc', [(i, (i + by) % 4) for i in range(4)])  8.05 us
    pallas_call x1, Pallas kernels, shards(): call(middle_kernel, (shape(256, 4096), shape(32, LANES, LANES), shape(LAN...  3.04 us
    pallas_call x1, Pallas kernels, shards(): call(last_kernel, shape(256, 4096), [VMEM] * 7 + [ANY], ANY, [pairs, pick...  2.51 us
    ppermute x2, waiting for transfers between devices, partner(): return lax.ppermute(value, 'kf_2', [(0, 1), (1, 0)])  1.51 us
    pallas_call x1, Pallas kernels, shards(): call(pack_kernel, shape(PEERS, 40, LANES), [VMEM] * 4, VMEM, [pltpu.VMEM(...  1.37 us
  transfers between devices with their start and end apart: 9, of which 4 were waited for; matrix products, arithmetic and copies ran while one was open for 2% of the time, Pallas kernels for 6%

profile of v8, /device:TPU:6, one launch (start us, length us, event | category | flops | bytes accessed | tf_op | source)
XLA Modules:
  0.0 52.7 jit_solution(8724456682676987356)
XLA Ops:
  0.0 0.0 collective-permute-start
  0.0 1.0 %convert_add_fusion.fetched = f32[48,2048]{1,0:T(8,128)S(1)} fusion(s32[1,1024]{1,0:T(1,128)} %bitcast.1, bf16[4,256]{1,0:T(4,128)(2,1)} %param.4, bf16[32,2048]{1,0:T(8,128)(2,1)} %param.3), kind=kLoop, calls=%fused_computation | loop fusion | flops 491520 | bytes 530432 | tf_op jit(solution)/shard_map/add | solution.py:269
  1.0 0.3 shard_map.37
  1.3 0.3 collective-permute-done.other
  1.6 1.4 %shard_map.38 = bf16[32,40,128]{2,1,0:T(8,128)(2,1)S(1)} custom-call(s32[1,1024]{1,0:T(1,128)S(1)} %get-tuple-element.18.slots, bf16[128,32,128]{2,1,0:T(8,128)(2,1)S(1)} %get-tuple-element.19.own_copies, bf16[32,2048]{1,0:T(8,128)(2,1)S(1)} %collective-permute-done.other, bf16[8,128]{1,0:T(8,128)(2,1)S(1)} %get-tuple-element.20.coef.coef_own), custom_call_target="tpu_custom_call" | custom-call | flops 1000000 | bytes 100000 | tf_op jit(solution)/shard_map/pallas_call | solution.py:275
  2.9 25.9 %all_to_all.5.received = bf16[32,40,128]{2,1,0:T(8,128)(2,1)S(1)} all-to-all(bf16[32,40,128]{2,1,0:T(8,128)(2,1)S(1)} %shard_map.38), channel_id=1, replica_groups=mesh['kf_0'=8,'kf_1'=4,'kf_2'=2,'kc'=4] {'kf_0','kf_1'}, dimensions={0} | all-to-all | bytes 655360 | tf_op jit(solution)/shard_map/all_to_all | solution.py:278
  28.8 0.1 shard_map.39
  28.9 0.9 %collective-permute-start.1 = (bf16[37,16,128]{2,1,0:T(8,128)(2,1)S(1)}, bf16[37,16,128]{2,1,0:T(8,128)(2,1)S(1)}, u32[]{:S(2)}, u32[]{:S(2)}) collective-permute-start(bf16[37,16,128]{2,1,0:T(8,128)(2,1)S(1)} %get-tuple-element.21), channel_id=1, source_target_pairs={{0,3},{1,0},{2,1},{3,2},{4,7},{5,4},{6,5},{7,6},{8,11},{9,8},{10,9... | collective-permute-start | bytes 454664 | tf_op jit(solution)/shard_map/ppermute | solution.py:256
  29.8 2.4 %collective-permute-start.3 = (bf16[37,16,128]{2,1,0:T(8,128)(2,1)S(1)}, bf16[37,16,128]{2,1,0:T(8,128)(2,1)S(1)}, u32[]{:S(2)}, u32[]{:S(2)}) collective-permute-start(bf16[37,16,128]{2,1,0:T(8,128)(2,1)S(1)} %get-tuple-element.23), channel_id=1, source_target_pairs={{0,1},{1,2},{2,3},{3,0},{4,5},{5,6},{6,7},{7,4},{8,9},{9,10},{10,1... | collective-permute-start | bytes 454664 | tf_op jit(solution)/shard_map/ppermute | solution.py:256
  32.2 0.0 collective-permute-start.8
  32.3 2.0 %collective-permute-start.2 = (bf16[32,16,128]{2,1,0:T(8,128)(2,1)S(1)}, bf16[32,16,128]{2,1,0:T(8,128)(2,1)S(1)}, u32[]{:S(2)}, u32[]{:S(2)}) collective-permute-start(bf16[32,16,128]{2,1,0:T(8,128)(2,1)S(1)} %get-tuple-element.22), channel_id=1, source_target_pairs={{0,3},{1,0},{2,1},{3,2},{4,7},{5,4},{6,5},{7,6},{8,11},{9,8},{10,9... | collective-permute-start | bytes 393224 | tf_op jit(solution)/shard_map/ppermute | solution.py:256
  34.3 2.8 %collective-permute-done.1.right_1 = bf16[37,16,128]{2,1,0:T(8,128)(2,1)S(1)} collective-permute-done((bf16[37,16,128]{2,1,0:T(8,128)(2,1)S(1)}, bf16[37,16,128]{2,1,0:T(8,128)(2,1)S(1)}, u32[]{:S(2)}, u32[]{:S(2)}) %collective-permute-start.1) | collective-permute-done | bytes 151584 | tf_op jit(solution)/shard_map/ppermute | solution.py:256
  37.0 0.1 collective-permute-start.5
  37.1 0.0 collective-permute-done.3.left_1
  37.2 3.3 %collective-permute-start.4 = (bf16[32,16,128]{2,1,0:T(8,128)(2,1)S(1)}, bf16[32,16,128]{2,1,0:T(8,128)(2,1)S(1)}, u32[]{:S(2)}, u32[]{:S(2)}) collective-permute-start(bf16[32,16,128]{2,1,0:T(8,128)(2,1)S(1)} %slice.8), channel_id=1, source_target_pairs={{0,1},{1,2},{2,3},{3,0},{4,5},{5,6},{6,7},{7,4},{8,9},{9,10},{10,1... | collective-permute-start | bytes 393224 | tf_op jit(solution)/shard_map/ppermute | solution.py:256
  40.4 0.0 collective-permute-start.6
  40.4 5.3 %collective-permute-done.6.far_coef = bf16[5,16,128]{2,1,0:T(8,128)(2,1)S(1)} collective-permute-done((bf16[5,16,128]{2,1,0:T(8,128)(2,1)S(1)}, bf16[5,16,128]{2,1,0:T(8,128)(2,1)S(1)}, u32[]{:S(2)}, u32[]{:S(2)}) %collective-permute-start.6) | collective-permute-done | bytes 20512 | tf_op jit(solution)/shard_map/ppermute | solution.py:256
  45.7 0.1 collective-permute-start.7
  45.8 0.0 collective-permute-done.8.left_2
  45.9 1.2 %collective-permute-done.7.coef_other = bf16[16,16,128]{2,1,0:T(8,128)(2,1)S(1)} collective-permute-done((bf16[16,16,128]{2,1,0:T(8,128)(2,1)S(1)}, bf16[16,16,128]{2,1,0:T(8,128)(2,1)S(1)}, u32[]{:S(2)}, u32[]{:S(2)}) %collective-permute-start.7) | collective-permute-done | bytes 65568 | tf_op jit(solution)/shard_map/ppermute | solution.py:260
  47.1 3.0 %shard_map.41 = (bf16[256,4096]{1,0:T(8,128)(2,1)}, bf16[32,128,128]{2,1,0:T(8,128)(2,1)S(1)}, bf16[128,128]{1,0:T(8,128)(2,1)S(1)}) custom-call(s32[1,1024]{1,0:T(1,128)S(1)} %get-tuple-element.17.near, bf16[32,40,128]{2,1,0:T(8,128)(2,1)S(1)} %all_to_all.5.received, bf16[8,128]{1,0:T(8,128)(2,1)S(1)} %get-tuple-element.20.coef.coef_own, ...), custom_call_target="tpu_custom_call" | custom-call | flops 8000000 | bytes 800000 | tf_op jit(solution)/shard_map/pallas_call | solution.py:295
  50.1 0.0 collective-permute-done.2.right_2
  50.2 0.0 collective-permute-done.4.far_1
  50.2 2.5 %shard_map.42 = bf16[256,4096]{1,0:T(8,128)(2,1)} custom-call(s32[1,1024]{1,0:T(1,128)S(1)} %get-tuple-element.17.near, bf16[37,16,128]{2,1,0:T(8,128)(2,1)S(1)} %collective-permute-done.1.right_1, bf16[32,16,128]{2,1,0:T(8,128)(2,1)S(1)} %collective-permute-done.2.right_2, ...), custom_call_target="tpu_custom_call", output_to_operand_aliasing={{}: (7, {})} | custom-call | flops 3000000 | bytes 300000 | tf_op jit(solution)/shard_map/pallas_call | solution.py:303
  (4 shorter events, 0.0 us)
Async XLA Ops:
  0.0 1.6 %collective-permute-start = (bf16[32,2048]{1,0:T(8,128)(2,1)}, bf16[32,2048]{1,0:T(8,128)(2,1)S(1)}, u32[]{:S(2)}, u32[]{:S(2)}) collective-permute-start(bf16[32,2048]{1,0:T(8,128)(2,1)} %param.3), channel_id=1, source_target_pairs={{0,4},{4,0},{1,5},{5,1},{2,6},{6,2},{3,7},{7,3},{8,12},{12,8},{9,1... | collective-permute-start | bytes 393224 | tf_op jit(solution)/shard_map/ppermute | solution.py:260
  28.9 8.1 %collective-permute-start.1 = (bf16[37,16,128]{2,1,0:T(8,128)(2,1)S(1)}, bf16[37,16,128]{2,1,0:T(8,128)(2,1)S(1)}, u32[]{:S(2)}, u32[]{:S(2)}) collective-permute-start(bf16[37,16,128]{2,1,0:T(8,128)(2,1)S(1)} %get-tuple-element.21), channel_id=1, source_target_pairs={{0,3},{1,0},{2,1},{3,2},{4,7},{5,4},{6,5},{7,6},{8,11},{9,8},{10,9... | collective-permute-start | bytes 454664 | tf_op jit(solution)/shard_map/ppermute | solution.py:256
  29.8 7.3 %collective-permute-start.3 = (bf16[37,16,128]{2,1,0:T(8,128)(2,1)S(1)}, bf16[37,16,128]{2,1,0:T(8,128)(2,1)S(1)}, u32[]{:S(2)}, u32[]{:S(2)}) collective-permute-start(bf16[37,16,128]{2,1,0:T(8,128)(2,1)S(1)} %get-tuple-element.23), channel_id=1, source_target_pairs={{0,1},{1,2},{2,3},{3,0},{4,5},{5,6},{6,7},{7,4},{8,9},{9,10},{10,1... | collective-permute-start | bytes 454664 | tf_op jit(solution)/shard_map/ppermute | solution.py:256
  32.2 13.6 %collective-permute-start.8 = (bf16[32,16,128]{2,1,0:T(8,128)(2,1)S(1)}, bf16[32,16,128]{2,1,0:T(8,128)(2,1)S(1)}, u32[]{:S(2)}, u32[]{:S(2)}) collective-permute-start(bf16[32,16,128]{2,1,0:T(8,128)(2,1)S(1)} %get-tuple-element.25), channel_id=1, source_target_pairs={{0,1},{1,2},{2,3},{3,0},{4,5},{5,6},{6,7},{7,4},{8,9},{9,10},{10,1... | collective-permute-start | bytes 393224 | tf_op jit(solution)/shard_map/ppermute | solution.py:256
  32.3 17.9 %collective-permute-start.2 = (bf16[32,16,128]{2,1,0:T(8,128)(2,1)S(1)}, bf16[32,16,128]{2,1,0:T(8,128)(2,1)S(1)}, u32[]{:S(2)}, u32[]{:S(2)}) collective-permute-start(bf16[32,16,128]{2,1,0:T(8,128)(2,1)S(1)} %get-tuple-element.22), channel_id=1, source_target_pairs={{0,3},{1,0},{2,1},{3,2},{4,7},{5,4},{6,5},{7,6},{8,11},{9,8},{10,9... | collective-permute-start | bytes 393224 | tf_op jit(solution)/shard_map/ppermute | solution.py:256
  37.0 13.1 %collective-permute-start.5 = (bf16[32,16,128]{2,1,0:T(8,128)(2,1)S(1)}, bf16[32,16,128]{2,1,0:T(8,128)(2,1)S(1)}, u32[]{:S(2)}, u32[]{:S(2)}) collective-permute-start(bf16[32,16,128]{2,1,0:T(8,128)(2,1)S(1)} %slice.9), channel_id=1, source_target_pairs={{0,3},{1,0},{2,1},{3,2},{4,7},{5,4},{6,5},{7,6},{8,11},{9,8},{10,9... | collective-permute-start | bytes 393224 | tf_op jit(solution)/shard_map/ppermute | solution.py:256
  37.2 13.0 %collective-permute-start.4 = (bf16[32,16,128]{2,1,0:T(8,128)(2,1)S(1)}, bf16[32,16,128]{2,1,0:T(8,128)(2,1)S(1)}, u32[]{:S(2)}, u32[]{:S(2)}) collective-permute-start(bf16[32,16,128]{2,1,0:T(8,128)(2,1)S(1)} %slice.8), channel_id=1, source_target_pairs={{0,1},{1,2},{2,3},{3,0},{4,5},{5,6},{6,7},{7,4},{8,9},{9,10},{10,1... | collective-permute-start | bytes 393224 | tf_op jit(solution)/shard_map/ppermute | solution.py:256
  40.4 5.3 %collective-permute-start.6 = (bf16[5,16,128]{2,1,0:T(8,128)(2,1)S(1)}, bf16[5,16,128]{2,1,0:T(8,128)(2,1)S(1)}, u32[]{:S(2)}, u32[]{:S(2)}) collective-permute-start(bf16[5,16,128]{2,1,0:T(8,128)(2,1)S(1)} %get-tuple-element.24), channel_id=1, source_target_pairs={{0,2},{1,3},{2,0},{3,1},{4,6},{5,7},{6,4},{7,5},{8,10},{9,11},{10,... | collective-permute-start | bytes 61448 | tf_op jit(solution)/shard_map/ppermute | solution.py:256
  45.7 1.3 %collective-permute-start.7 = (bf16[16,16,128]{2,1,0:T(8,128)(2,1)S(1)}, bf16[16,16,128]{2,1,0:T(8,128)(2,1)S(1)}, u32[]{:S(2)}, u32[]{:S(2)}) collective-permute-start(bf16[16,16,128]{2,1,0:T(8,128)(2,1)S(1)} %shard_map.40.coef_half), channel_id=1, source_target_pairs={{0,4},{4,0},{1,5},{5,1},{2,6},{6,2},{3,7},{7,3},{8,12},{12,8},{9,1... | collective-permute-start | bytes 196616 | tf_op jit(solution)/shard_map/ppermute | solution.py:260
